TPU v7x, 256 devices: a whole 4x4x8 slice. The times are simulated.
256 devices in a mesh: dp: 8 (over y, core), tensor: 4 (over x), ctx: 8 (over z).
Axes of the slice: x: 4, y: 4, z: 8, core: 2. Of those that a mesh axis runs over, the one named last changes fastest.
Arguments:
- grad_down: bfloat16 [8, 18432, 4608], P('dp', 'tensor', 'ctx'), may hold values from -700 to 700
- grad_query: bfloat16 [8, 4608, 2048], P('dp', 'ctx', 'tensor'), may hold values from -700 to 700
- down_param: float32 [18432, 4608], P(('tensor', 'dp'), 'ctx'), may hold values from -0.3 to 0.3
- down_moment: float32 [18432, 4608], P(('tensor', 'dp'), 'ctx'), may hold values from -6 to 6
- down_second: float32 [4608], P('ctx'), may hold values from 0.1 to 2
- query_param: float32 [4608, 2048], P(('ctx', 'dp'), 'tensor'), may hold values from -0.3 to 0.3
- query_moment: float32 [4608, 2048], P(('ctx', 'dp'), 'tensor'), may hold values from -6 to 6
- query_second: float32 [16], P('tensor'), may hold values from 0.1 to 2
- step_count: int32 [1], replicated, may hold values from 1 to 29
Outputs:
- down_param_new: float32 [18432, 4608], P(('tensor', 'dp'), 'ctx')
- down_moment_new: float32 [18432, 4608], P(('tensor', 'dp'), 'ctx')
- down_second_new: float32 [4608], P('ctx')
- down_update: bfloat16 [18432, 4608], P(('tensor', 'dp'), 'ctx')
- query_param_new: float32 [4608, 2048], P(('ctx', 'dp'), 'tensor')
- query_moment_new: float32 [4608, 2048], P(('ctx', 'dp'), 'tensor')
- query_second_new: float32 [16], P('tensor')
- query_update: bfloat16 [4608, 2048], P(('ctx', 'dp'), 'tensor')
All inputs are finite; a program needn't handle non-finite values.
Results may differ from a plain program's by a relative error of at most 0.012.
Values may be sent and summed in bfloat16 or wider, within the bound.
No kernel may reach another device: no remote copies, remote signals or barrier semaphores. Data moves between devices by JAX's collectives and lax.ppermute only.
A program may use at most 64 MiB of HBM per device.

v0:
```python
import jax
import jax.numpy as jnp
from jax import lax
from jax.sharding import PartitionSpec as P

D = 4608
HEAD_DIM = 128
FF = 18432


BETA_ONE = 0.9
BETA_TWO = 0.95
EPSILON = 1e-08
LEARN_RATE = 0.003
DECAY_RATE = 0.1


def sent_to_all(shard, axis):
    copies = jnp.broadcast_to(shard, (lax.axis_size(axis), *shard.shape))
    return lax.all_to_all(copies, axis, split_axis=0, concat_axis=0, tiled=True)


def over_copies(shard, axis):
    everything = sent_to_all(shard, axis)
    return jnp.sum(everything, axis=0)


def finish(parameter, moment, gradient, second_wide, keep_one, keep_two):
    moment_new = BETA_ONE * moment + (1.0 - BETA_ONE) * gradient
    update = moment_new / keep_one / (jnp.sqrt(second_wide / keep_two) + EPSILON)
    parameter_new = parameter - LEARN_RATE * (update + DECAY_RATE * parameter)
    return (parameter_new, moment_new, update.astype(jnp.bfloat16))


def shards(
    grad_down,
    grad_query,
    down_param,
    down_moment,
    down_second,
    query_param,
    query_moment,
    query_second,
    step_count,
):
    replicas = lax.axis_size("dp")
    step_value = step_count[0].astype(jnp.float32)
    keep_one = 1.0 - jnp.power(jnp.float32(BETA_ONE), step_value)
    keep_two = 1.0 - jnp.power(jnp.float32(BETA_TWO), step_value)
    down_summed, query_summed = (
        lax.psum_scatter(grad_down[0], "dp", scatter_dimension=0, tiled=True).astype(jnp.float32),
        lax.psum_scatter(grad_query[0], "dp", scatter_dimension=0, tiled=True).astype(jnp.float32),
    )
    down_grad = down_summed / replicas
    neuron_part = jnp.sum(down_grad * down_grad, axis=0)
    query_grad = query_summed / replicas
    head_count = query_grad.shape[1] // HEAD_DIM
    head_part = jnp.sum(
        (query_grad * query_grad).reshape(query_grad.shape[0], head_count, HEAD_DIM), axis=(0, 2)
    )
    neuron_total = over_copies(neuron_part, ("dp", "tensor"))
    head_total = over_copies(head_part, ("dp", "ctx"))
    down_second_new = BETA_TWO * down_second + (1.0 - BETA_TWO) * (neuron_total / FF)
    query_second_new = BETA_TWO * query_second + (1.0 - BETA_TWO) * (head_total / (D * HEAD_DIM))
    down_param_new, down_moment_new, down_update = finish(
        down_param, down_moment, down_grad, down_second_new[None, :], keep_one, keep_two
    )
    query_wide = jnp.repeat(query_second_new, HEAD_DIM)
    query_param_new, query_moment_new, query_update = finish(
        query_param, query_moment, query_grad, query_wide[None, :], keep_one, keep_two
    )
    return (
        down_param_new,
        down_moment_new,
        down_second_new,
        down_update,
        query_param_new,
        query_moment_new,
        query_second_new,
        query_update,
    )


def solution(mesh):
    in_specs = (
        P("dp", "tensor", "ctx"),
        P("dp", "ctx", "tensor"),
        P(("tensor", "dp"), "ctx"),
        P(("tensor", "dp"), "ctx"),
        P("ctx"),
        P(("ctx", "dp"), "tensor"),
        P(("ctx", "dp"), "tensor"),
        P("tensor"),
        P(),
    )
    out_specs = (
        P(("tensor", "dp"), "ctx"),
        P(("tensor", "dp"), "ctx"),
        P("ctx"),
        P(("tensor", "dp"), "ctx"),
        P(("ctx", "dp"), "tensor"),
        P(("ctx", "dp"), "tensor"),
        P("tensor"),
        P(("ctx", "dp"), "tensor"),
    )
    return jax.shard_map(shards, mesh=mesh, in_specs=in_specs, out_specs=out_specs, check_vma=False)
```

profile of v0, /device:TPU:1, one launch (start us, length us, event | category | flops | bytes accessed | tf_op | source)
XLA Modules:
  0.0 119.7 jit_solution(1090725147647718968)
XLA Ops:
  7.2 0.0 reduce-scatter.5.cloned.1.call-start
  7.2 0.7 reduce-scatter.5.cloned.1.call-update
  7.9 0.0 reduce-scatter.3.cloned.1.call-start
  7.9 8.4 %copy.19 = bf16[1,4608,576]{2,1,0:T(8,128)(2,1)} copy(bf16[1,4608,576]{1,2,0:T(8,128)(2,1)} %param.9) | data formatting | bytes 10616832 | tf_op args[0]
  16.3 0.0 copy-start.8
  16.3 0.0 copy-start.5
  16.3 0.0 copy-start.6
  16.3 0.0 reduce-scatter.3.cloned.1.call-update
  16.4 0.0 copy-start.7
  16.4 0.0 copy-start.2
  16.4 29.7 %reduce-scatter.5.cloned.1.call-done = bf16[72,512]{1,0:T(8,128)(2,1)} async-done(((bf16[576,512]{1,0:T(8,128)(2,1)}), bf16[72,512]{1,0:T(8,128)(2,1)}) %reduce-scatter.5.cloned.1.call-update) | async-done | bytes 73744 | tf_op jit(solution)/shard_map/reduce_scatter | solution.py:52
  46.1 0.9 fusion.6
  47.0 0.1 bitcast_reduce_fusion
  47.1 0.6 broadcast_in_dim.11
  47.8 10.5 %all-to-all-start.1 = ((f32[64,1,4]{2,1,0:T(1,128)}), f32[64,1,4]{2,1,0:T(1,128)S(1)}, u32[]{:S(2)}, u32[]{:S(2)}) async-start(f32[64,1,4]{2,1,0:T(1,128)} %broadcast_in_dim.11), calls=%async_computation.3 | async-start | bytes 65536 | tf_op jit(solution)/shard_map/all_to_all | solution.py:20
  59.0 8.4 %all-to-all-done.1 = f32[64,1,4]{2,1,0:T(1,128)S(1)} async-done(((f32[64,1,4]{2,1,0:T(1,128)}), f32[64,1,4]{2,1,0:T(1,128)S(1)}, u32[]{:S(2)}, u32[]{:S(2)}) %all-to-all-start.1) | async-done | bytes 1056 | tf_op jit(solution)/shard_map/all_to_all | solution.py:20
  67.4 0.1 reduce_sum.48
  67.5 0.0 copy-done.8
  67.5 0.5 add_multiply_fusion.1
  68.0 0.1 broadcast_bitcast_fusion
  68.1 0.0 copy-done.5
  68.1 1.5 %fusion.7 = (bf16[72,512]{1,0:T(8,128)(2,1)}, f32[72,512]{1,0:T(8,128)S(1)}) fusion(f32[512]{0:T(512)S(1)} %broadcast_bitcast_fusion, bf16[72,512]{1,0:T(8,128)(2,1)} %reduce-scatter.5.cloned.1.call-done, f32[72,512]{1,0:T(8,128)S(1)} %copy-done.5), kind=kLoop, calls=%fused_computation.15 | loop fusion | flops 221184 | bytes 444416 | tf_op jit(solution)/shard_map/convert_element_type | solution.py:32
  69.6 0.0 copy-start.4
  69.6 22.9 %reduce-scatter.3.cloned.1.call-done = bf16[576,576]{1,0:T(8,128)(2,1)} async-done(((bf16[4608,576]{1,0:T(8,128)(2,1)}), bf16[576,576]{1,0:T(8,128)(2,1)}) %reduce-scatter.3.cloned.1.call-update) | async-done | bytes 663568 | tf_op jit(solution)/shard_map/reduce_scatter | solution.py:51
  92.5 0.0 copy-start.1
  92.6 1.4 %fusion.2 = f32[576]{0:T(1024)S(1)} fusion(bf16[576,576]{1,0:T(8,128)(2,1)} %reduce-scatter.3.cloned.1.call-done), kind=kLoop, calls=%fused_computation.4 | loop fusion | flops 1326528 | bytes 665856 | tf_op jit(solution)/shard_map/reduce_sum | solution.py:55
  94.0 0.7 broadcast_in_dim.10
  94.6 7.2 %all-to-all-start = ((f32[32,1,576]{2,1,0:T(1,128)}), f32[32,1,576]{2,1,0:T(1,128)S(1)}, u32[]{:S(2)}, u32[]{:S(2)}) async-start(f32[32,1,576]{2,1,0:T(1,128)} %broadcast_in_dim.10), calls=%async_computation.1 | async-start | bytes 163840 | tf_op jit(solution)/shard_map/all_to_all | solution.py:20
  101.8 0.0 copy-done.6
  101.9 0.7 multiply_subtract_fusion.1
  102.6 6.6 %all-to-all-done = f32[32,1,576]{2,1,0:T(1,128)S(1)} async-done(((f32[32,1,576]{2,1,0:T(1,128)}), f32[32,1,576]{2,1,0:T(1,128)S(1)}, u32[]{:S(2)}, u32[]{:S(2)}) %all-to-all-start) | async-done | bytes 73760 | tf_op jit(solution)/shard_map/all_to_all | solution.py:20
  109.1 0.1 reduce_sum.44
  109.2 0.0 copy-done.7
  109.2 0.6 add_multiply_fusion
  109.8 0.0 copy-done.2
  109.8 0.0 copy-done.1
  109.8 0.0 copy-start.3
  109.8 1.1 fusion.3
  111.0 0.0 copy-done.4
  111.0 0.0 copy-start
  111.0 0.5 copy-done.3
  111.5 1.4 %multiply_subtract_fusion = f32[576,576]{1,0:T(8,128)} fusion(f32[576,576]{1,0:T(8,128)S(1)} %copy-done.3, f32[576,576]{1,0:T(8,128)S(1)} %get-tuple-element.13, f32[576]{0:T(1024)S(1)} %get-tuple-element.14), kind=kLoop, calls=%fused_computation.5 | loop fusion | flops 1658880 | bytes 3983616 | tf_op jit(solution)/shard_map/sub | solution.py:31
  112.8 0.0 copy-done
Async XLA Ops:
  7.2 38.9 %reduce-scatter.5.cloned.1.call-start = ((), (), s32[]{:S(2)}) async-start(), calls=%async_computation.5 | async-start | bytes 663552 | tf_op jit(solution)/shard_map/reduce_scatter | solution.py:52
  7.9 84.6 %reduce-scatter.3.cloned.1.call-start = ((), (), s32[]{:S(2)}) async-start(), calls=%async_computation.4 | async-start | bytes 6635520 | tf_op jit(solution)/shard_map/reduce_scatter | solution.py:51
  16.3 51.2 %copy-start.8 = (f32[4]{0:T(128)S(1)}, f32[4]{0:T(128)}, u32[]{:S(2)}) copy-start(f32[4]{0:T(128)} %param.16) | copy-start | bytes 52
  16.3 51.7 %copy-start.5 = (f32[72,512]{1,0:T(8,128)S(1)}, f32[72,512]{1,0:T(8,128)}, u32[]{:S(2)}) copy-start(f32[72,512]{1,0:T(8,128)} %param.15) | copy-start | bytes 442372
  16.3 85.5 %copy-start.6 = (f32[72,512]{1,0:T(8,128)S(1)}, f32[72,512]{1,0:T(8,128)}, u32[]{:S(2)}) copy-start(f32[72,512]{1,0:T(8,128)} %param.14) | copy-start | bytes 442372
  16.4 92.8 %copy-start.7 = (f32[576]{0:T(1024)S(1)}, f32[576]{0:T(1024)}, u32[]{:S(2)}) copy-start(f32[576]{0:T(1024)} %param.13) | copy-start | bytes 6916
  16.4 93.4 %copy-start.2 = (f32[576,576]{1,0:T(8,128)S(1)}, f32[576,576]{1,0:T(8,128)}, u32[]{:S(2)}) copy-start(f32[576,576]{1,0:T(8,128)} %param.12) | copy-start | bytes 3981316
  47.8 19.7 %all-to-all-start.1 = ((f32[64,1,4]{2,1,0:T(1,128)}), f32[64,1,4]{2,1,0:T(1,128)S(1)}, u32[]{:S(2)}, u32[]{:S(2)}) async-start(f32[64,1,4]{2,1,0:T(1,128)} %broadcast_in_dim.11), calls=%async_computation.3 | async-start | bytes 65536 | tf_op jit(solution)/shard_map/all_to_all | solution.py:20
  69.6 41.3 %copy-start.4 = (f32[72,512]{1,0:T(8,128)}, f32[72,512]{1,0:T(8,128)S(1)}, u32[]{:S(2)}) copy-start(f32[72,512]{1,0:T(8,128)S(1)} %get-tuple-element.9) | copy-start | bytes 442372
  92.5 17.3 %copy-start.1 = (bf16[576,576]{1,0:T(8,128)(2,1)S(1)}, bf16[576,576]{1,0:T(8,128)(2,1)}, u32[]{:S(2)}) copy-start(bf16[576,576]{1,0:T(8,128)(2,1)} %reduce-scatter.3.cloned.1.call-done) | copy-start | bytes 1990660
  94.6 14.5 %all-to-all-start = ((f32[32,1,576]{2,1,0:T(1,128)}), f32[32,1,576]{2,1,0:T(1,128)S(1)}, u32[]{:S(2)}, u32[]{:S(2)}) async-start(f32[32,1,576]{2,1,0:T(1,128)} %broadcast_in_dim.10), calls=%async_computation.1 | async-start | bytes 163840 | tf_op jit(solution)/shard_map/all_to_all | solution.py:20
  109.8 1.6 %copy-start.3 = (f32[576,576]{1,0:T(8,128)S(1)}, f32[576,576]{1,0:T(8,128)}, u32[]{:S(2)}) copy-start(f32[576,576]{1,0:T(8,128)} %param.11) | copy-start | bytes 3981316
  111.0 1.9 %copy-start = (f32[576,576]{1,0:T(8,128)}, f32[576,576]{1,0:T(8,128)S(1)}, u32[]{:S(2)}) copy-start(f32[576,576]{1,0:T(8,128)S(1)} %get-tuple-element.13) | copy-start | bytes 3981316
Sparse Core Ops, SparseCore 0:
  10.5 35.5 reduce-scatter.4
  48.6 43.8 reduce-scatter.2
where the time goes:
time: 120 us
  waiting for transfers between devices  68.3 us (57%)
  starting transfers between devices  17.8 us (15%)
  between operations  14.8 us (12%)
  local copies, waits for them, and re-layouts  10.3 us (9%)
  other arithmetic  8.47 us (7%)
    reduce_scatter x1, waiting for transfers between devices, shards(): lax.psum_scatter(grad_query[0], 'dp', scatter_dimension=0, tiled=True)  29.7 us
    reduce_scatter x1, waiting for transfers between devices, shards(): lax.psum_scatter(grad_down[0], 'dp', scatter_dimension=0, tiled=True)  22.9 us
    all_to_all x2, starting transfers between devices, sent_to_all(): return lax.all_to_all(copies, axis, split_axis=0, concat_axis=0, tiled=True)  17.7 us
    all_to_all x2, waiting for transfers between devices, sent_to_all(): return lax.all_to_all(copies, axis, split_axis=0, concat_axis=0, tiled=True)  15 us
    unnamed x19, local copies, waits for them, and re-layouts  8.92 us
    convert_element_type x2, other arithmetic, finish(): return (parameter_new, moment_new, update.astype(jnp.bfloat16))  2.69 us
  transfers between devices with their start and end apart: 4, of which 4 were waited for; matrix products, arithmetic and copies ran while one was open for 11% of the time, Pallas kernels for 0%

commit v1 on v0

v1 whole, which is shorter than its diff:
```python
import jax
import jax.numpy as jnp
from jax import lax
from jax.experimental import pallas as pl
from jax.experimental.pallas import tpu as pltpu
from jax.sharding import PartitionSpec as P

D = 4608
HEAD_DIM = 128
FF = 18432

BETA_ONE = 0.9
BETA_TWO = 0.95
EPSILON = 1e-08
LEARN_RATE = 0.003
DECAY_RATE = 0.1

LANES = 128
PIECES = ((512, 64), (0, 256), (256, 256))
SLOTS = ((0, 1), (0, 2), (1, 3), (1, 2), (0, 0), (0, 3), (1, 0), (1, 1))
ANY = pl.BlockSpec(memory_space=pl.ANY)
HBM = pl.BlockSpec(memory_space=pltpu.HBM)
VMEM = pl.BlockSpec(memory_space=pltpu.VMEM)
SMEM = pl.BlockSpec(memory_space=pltpu.SMEM)


PARAMS = pltpu.CompilerParams(vmem_limit_bytes=8 << 20)


def pairs(size, mask):
    return [(i, i ^ mask) for i in range(size)]


def far(x):
    return pltpu.with_memory_space_constraint(x, pltpu.HBM)


def near(x):
    return pltpu.with_memory_space_constraint(x, pltpu.VMEM)


def pack_piece(piece, columns, query_chunks, after):
    start, width = PIECES[piece]
    quarter = width // 4
    down_block = 2 * width + quarter
    with_query = piece == 0
    q_rows, q_cols = query_chunks.shape[1:]
    q_wide = q_cols // LANES // 2
    block = down_block + (q_rows * q_wide if with_query else 0)
    total = block * len(SLOTS)
    span = columns.shape[1] // 4

    def kernel(down_ref, query_ref, _, send_ref, own_ref, shared_buf, down_sem, shared_sem, query_sem):
        me = lax.axis_index("dp")
        y, core = me // 2, me % 2
        shared, down, query = [], [], []
        for d in range(4):
            lane = pl.multiple_of(span * (y ^ d) + 4 * LANES, LANES)
            source = down_ref.at[pl.ds(start, width), pl.ds(lane, LANES)]
            shared.append(pltpu.make_async_copy(source, shared_buf.at[d], shared_sem.at[d]))
        for side, out in enumerate((send_ref, own_ref)):
            owner = core if side else 1 - core
            for slot, (half, d) in enumerate(SLOTS):
                for j in range(2):
                    lane = pl.multiple_of(span * (y ^ d) + 5 * LANES * owner + (2 * half + j) * LANES, LANES)
                    source = down_ref.at[pl.ds(start, width), pl.ds(lane, LANES)]
                    target = out.at[pl.ds(slot * block + j * width, width), :]
                    down.append(pltpu.make_async_copy(source, target, down_sem.at[side, slot, j]))
                if with_query:
                    for j in range(q_wide):
                        source = query_ref.at[2 * (y ^ d) + owner, :, pl.ds((half * q_wide + j) * LANES, LANES)]
                        target = out.at[pl.ds(slot * block + down_block + j * q_rows, q_rows), :]
                        query.append(pltpu.make_async_copy(source, target, query_sem.at[side, slot, j]))
        for copy in shared + query + down:
            copy.start()
        for copy in shared:
            copy.wait()
        low = lax.broadcasted_iota(jnp.int32, (quarter, LANES), 1) < LANES // 2
        for slot, (half, d) in enumerate(SLOTS):
            first = shared_buf[d, pl.ds(2 * half * quarter, quarter), :].astype(jnp.float32)
            second = shared_buf[d, pl.ds((2 * half + 1) * quarter, quarter), :].astype(jnp.float32)
            of_core = (
                jnp.where(low, first, pltpu.roll(second, LANES // 2, 1)),
                jnp.where(low, pltpu.roll(first, LANES // 2, 1), second),
            )
            at = (pl.ds(slot * block + 2 * width, quarter), slice(None))
            own_ref[at] = jnp.where(core == 0, of_core[0], of_core[1]).astype(jnp.bfloat16)
            send_ref[at] = jnp.where(core == 0, of_core[1], of_core[0]).astype(jnp.bfloat16)
        for copy in query + down:
            copy.wait()

    shape = pltpu.VMEM((total, LANES), jnp.bfloat16)
    return pl.pallas_call(
        kernel,
        out_shape=(shape, shape),
        in_specs=[HBM, HBM, ANY],
        out_specs=(VMEM, VMEM),
        scratch_shapes=[
            pltpu.VMEM((4, width, LANES), jnp.bfloat16),
            pltpu.SemaphoreType.DMA((2, len(SLOTS), 2)),
            pltpu.SemaphoreType.DMA((4,)),
            pltpu.SemaphoreType.DMA((2, len(SLOTS), q_wide)),
        ],
        compiler_params=PARAMS,
    )(far(columns), far(query_chunks), after)


def added(*terms):
    total = terms[0].astype(jnp.float32)
    for term in terms[1:]:
        total = total + term.astype(jnp.float32)
    return total


def sent(x, mask, axis="dp"):
    return lax.ppermute(x, axis, pairs(8, mask))


def reduce_piece(send, own):
    block = own.shape[0] // len(SLOTS)
    other = sent(send, 1)

    def part(first, count):
        return own[first * block : (first + count) * block], other[first * block : (first + count) * block]

    first_a = sent(added(*part(0, 2)).astype(jnp.bfloat16), 2)
    first_b = sent(added(*part(2, 2)).astype(jnp.bfloat16), 6)
    second_a = sent(added(*part(5, 1), first_a[block:]).astype(jnp.bfloat16), 6)
    second_b = sent(added(*part(7, 1), first_b[block:]).astype(jnp.bfloat16), 2)
    return own, other, first_a, first_b, second_a, second_b


def gather_piece(piece, terms, down_moment, moment_so_far, sums_so_far, query_moment):
    start, width = PIECES[piece]
    quarter = width // 4
    down_block = 2 * width + quarter
    block = terms[0].shape[0] // len(SLOTS)
    first = piece == 0
    q_rows, q_cols = query_moment.shape
    q_wide = q_cols // LANES // 2
    half_tile = LANES // 2

    def kernel(*refs):
        own_ref, other_ref, first_a, first_b, second_a, second_b, moment_ref = refs[:7]
        if first:
            query_moment_ref, new_ref, sums_ref, query_new_ref, query_sums_ref = refs[7:]
            sums_ref[...] = jnp.zeros_like(sums_ref)
            query_sums_ref[...] = jnp.zeros_like(query_sums_ref)
        else:
            _, before_ref, new_ref, sums_ref = refs[7:]
            sums_ref[...] = before_ref[...]
        core = lax.axis_index("dp") % 2

        def mean(half, at, count):
            kept = (4 + 2 * half) * block + at
            step_one, step_two = (first_b, second_b) if half else (first_a, second_a)
            return added(
                own_ref[pl.ds(kept, count), :],
                other_ref[pl.ds(kept, count), :],
                step_one[pl.ds(at, count), :],
                step_two[pl.ds(at, count), :],
            ) * (1.0 / 8.0)

        def column_sum(x):
            return jnp.sum(x * x, axis=0, keepdims=True)

        def moment_new(before, grad):
            return BETA_ONE * before + (1.0 - BETA_ONE) * grad

        step = min(width, LANES)
        for c in range(0, width, step):
            span = slice(start + c, start + c + step)
            total = jnp.zeros((1, step), jnp.float32)
            for tile in range(4):
                half, j = tile // 2, tile % 2
                grad = mean(half, j * width + c, step).T
                at = (pl.ds(pl.multiple_of(half_tile * core + tile * LANES, half_tile), LANES), span)
                new_ref[at] = moment_new(moment_ref[at], grad)
                total += column_sum(grad)
            parts = []
            for part in range(c // quarter, (c + step) // quarter):
                packed = mean(part // 2, 2 * width, quarter)
                parts.append(pltpu.roll(packed, half_tile, 1) if part % 2 else packed)
            grad = jnp.concatenate(parts, axis=0).T[:half_tile]
            at = (pl.ds(pl.multiple_of(4 * LANES * (1 - core), half_tile), half_tile), span)
            new_ref[at] = moment_new(moment_ref[at], grad)
            row = (start + c) // LANES
            sums_ref[row : row + 1, :step] = total + column_sum(grad)
        if first:
            for half in range(2):
                for j in range(q_wide):
                    grad = mean(half, down_block + j * q_rows, q_rows)
                    head = half * q_wide + j
                    at = (slice(None), slice(head * LANES, (head + 1) * LANES))
                    query_new_ref[at] = moment_new(query_moment_ref[at], grad)
                    query_sums_ref[head : head + 1, :] = column_sum(grad)

    new = pltpu.VMEM(down_moment.shape, jnp.float32)
    sums = pltpu.VMEM((8, LANES), jnp.float32)
    terms = tuple(near(t) for t in (*terms, down_moment))
    if first:
        return pl.pallas_call(
            kernel,
            out_shape=(new, sums, pltpu.VMEM(query_moment.shape, jnp.float32), sums),
            in_specs=[VMEM] * 8,
            out_specs=(VMEM,) * 4,
            compiler_params=PARAMS,
        )(*terms, near(query_moment))
    return pl.pallas_call(
        kernel,
        out_shape=(new, sums),
        in_specs=[VMEM] * 9,
        out_specs=(VMEM,) * 2,
        input_output_aliases={7: 0},
        compiler_params=PARAMS,
    )(*terms, near(moment_so_far), near(sums_so_far))


def message_kernel(sums_ref, heads_ref, out_ref, *, tensors):
    me = lax.axis_index("tensor")
    sums = sums_ref[...]
    row = lax.broadcasted_iota(jnp.int32, sums.shape, 0)
    lane = lax.broadcasted_iota(jnp.int32, sums.shape, 1)
    neurons = jnp.where(row < 5, sums, 0.0)
    heads = jnp.sum(heads_ref[...], axis=1, keepdims=True)
    spread = jnp.sum(jnp.where(row == lane, heads, 0.0), axis=0, keepdims=True)
    mine = neurons + jnp.where(row == 5, spread, 0.0)
    for target in range(out_ref.shape[0]):
        out_ref[target] = jnp.where(me == target % tensors, mine, neurons)


ROW_BLOCKS = 6


def finish_kernel(
    keep_ref, got_ref, new_ref, param_ref, second_ref, query_new_ref, query_param_ref, query_second_ref,
    param_out, moment_out, update_out, second_out, query_param_out, query_moment_out, query_update_out, query_second_out,
    param_buf, update_buf, query_param_buf, query_update_buf, sems, query_sems,
):
    keep_one, keep_two = keep_ref[0], keep_ref[1]
    moments = (
        pltpu.make_async_copy(new_ref, moment_out, sems.at[0, 0]),
        pltpu.make_async_copy(query_new_ref, query_moment_out, query_sems.at[0]),
    )
    for copy in moments:
        copy.start()
    total = jnp.sum(got_ref[...], axis=0)

    def second_new(before, mean):
        return BETA_TWO * before + (1.0 - BETA_TWO) * mean

    def factor(second):
        return 1.0 / (keep_one * (jnp.sqrt(second / keep_two) + EPSILON))

    def write(at, scale, new, param, update_to, param_to):
        old = param[at]
        update = new[at] * scale
        update_to[at] = update.astype(jnp.bfloat16)
        param_to[at] = old - LEARN_RATE * (update + DECAY_RATE * old)

    rows, cols = new_ref.shape
    spans = [slice(k, min(k + LANES, cols)) for k in range(0, cols, LANES)]
    factors = []
    for k, span in enumerate(spans):
        second = second_new(second_ref[:, span], total[k : k + 1, : span.stop - span.start] * (1.0 / FF))
        second_out[:, span] = second
        factors.append(factor(second))
    copies = []
    block = rows // ROW_BLOCKS
    for b in range(ROW_BLOCKS):
        part = slice(b * block, (b + 1) * block)
        for span, scale in zip(spans, factors):
            write((part, span), scale, new_ref, param_ref, update_buf, param_buf)
        copies.append(pltpu.make_async_copy(param_buf.at[part], param_out.at[part], sems.at[1, b]))
        copies.append(pltpu.make_async_copy(update_buf.at[part], update_out.at[part], sems.at[2, b]))
        copies[-2].start()
        copies[-1].start()
    heads = query_new_ref.shape[1] // HEAD_DIM
    for head in range(heads):
        mean = total[5:6, head : head + 1] * (1.0 / (D * HEAD_DIM))
        second = second_new(query_second_ref[:, head : head + 1], mean)
        query_second_out[:, head : head + 1] = second
        span = slice(head * HEAD_DIM, (head + 1) * HEAD_DIM)
        write((slice(None), span), factor(second), query_new_ref, query_param_ref, query_update_buf, query_param_buf)
    copies.append(pltpu.make_async_copy(query_param_buf, query_param_out, query_sems.at[1]))
    copies.append(pltpu.make_async_copy(query_update_buf, query_update_out, query_sems.at[2]))
    copies[-2].start()
    copies[-1].start()
    for copy in (*moments, *copies):
        copy.wait()


def shards(
    grad_down,
    grad_query,
    down_param,
    down_moment,
    down_second,
    query_param,
    query_moment,
    query_second,
    step_count,
):
    replicas = lax.axis_size("dp")
    step_value = step_count[0].astype(jnp.float32)
    keep = jnp.stack(
        [1.0 - jnp.power(jnp.float32(BETA_ONE), step_value), 1.0 - jnp.power(jnp.float32(BETA_TWO), step_value)]
    )
    columns = grad_down[0].T
    query_chunks = grad_query[0].reshape(replicas, -1, grad_query.shape[2])
    own, new, sums = query_chunks, None, None
    for piece in range(len(PIECES)):
        send, own = pack_piece(piece, columns, query_chunks, own)
        terms = reduce_piece(send, own)
        result = gather_piece(piece, terms, down_moment, new, sums, query_moment)
        new, sums = result[:2]
        if piece == 0:
            query_new, heads = result[2:]
            for mask in (1, 2, 4):
                heads = heads + sent(heads, mask, "ctx")
    group = ("dp", "tensor")
    tensors = lax.axis_size("tensor")
    message = pl.pallas_call(
        lambda *refs: message_kernel(*refs, tensors=tensors),
        out_shape=pltpu.VMEM((lax.axis_size(group), 8, LANES), jnp.float32),
        in_specs=[VMEM, VMEM],
        out_specs=VMEM,
        compiler_params=PARAMS, name="message",
    )(near(sums), near(heads))
    got = lax.all_to_all(message, group, split_axis=0, concat_axis=0, tiled=True)
    f32, bf16 = jnp.float32, jnp.bfloat16
    outs = pl.pallas_call(
        finish_kernel,
        out_shape=(
            jax.ShapeDtypeStruct(down_param.shape, f32),
            jax.ShapeDtypeStruct(down_param.shape, f32),
            jax.ShapeDtypeStruct(down_param.shape, bf16),
            jax.ShapeDtypeStruct((1, down_param.shape[1]), f32),
            jax.ShapeDtypeStruct(query_param.shape, f32),
            jax.ShapeDtypeStruct(query_param.shape, f32),
            jax.ShapeDtypeStruct(query_param.shape, bf16),
            jax.ShapeDtypeStruct((1, query_second.shape[0]), f32),
        ),
        in_specs=[SMEM] + [VMEM] * 7,
        out_specs=(ANY, ANY, ANY, VMEM, ANY, ANY, ANY, VMEM),
        scratch_shapes=[
            pltpu.VMEM(down_param.shape, f32),
            pltpu.VMEM(down_param.shape, bf16),
            pltpu.VMEM(query_param.shape, f32),
            pltpu.VMEM(query_param.shape, bf16),
            pltpu.SemaphoreType.DMA((3, ROW_BLOCKS)),
            pltpu.SemaphoreType.DMA((3,)),
        ],
        compiler_params=PARAMS, name="finish",
    )(
        keep, near(got), near(new), near(down_param), down_second[None, :],
        near(query_new), near(query_param), query_second[None, :],
    )
    (down_param_new, down_moment_new, down_update, down_second_new) = outs[:4]
    (query_param_new, query_moment_new, query_update, query_second_new) = outs[4:]
    return (
        down_param_new,
        down_moment_new,
        down_second_new[0],
        down_update,
        query_param_new,
        query_moment_new,
        query_second_new[0],
        query_update,
    )


def solution(mesh):
    in_specs = (
        P("dp", "tensor", "ctx"),
        P("dp", "ctx", "tensor"),
        P(("tensor", "dp"), "ctx"),
        P(("tensor", "dp"), "ctx"),
        P("ctx"),
        P(("ctx", "dp"), "tensor"),
        P(("ctx", "dp"), "tensor"),
        P("tensor"),
        P(),
    )
    out_specs = (
        P(("tensor", "dp"), "ctx"),
        P(("tensor", "dp"), "ctx"),
        P("ctx"),
        P(("tensor", "dp"), "ctx"),
        P(("ctx", "dp"), "tensor"),
        P(("ctx", "dp"), "tensor"),
        P("tensor"),
        P(("ctx", "dp"), "tensor"),
    )

    return jax.shard_map(shards, mesh=mesh, in_specs=in_specs, out_specs=out_specs, check_vma=False)
```

time: 120 us -> 76.6 us (0.64)
  waiting for transfers between devices: 68.3 us -> 24.2 us
  starting transfers between devices: 17.8 us -> 37.1 us
  between operations: 14.8 us -> 1.55 us
  Pallas kernels: 0 us -> 11.8 us
  local copies, waits for them, and re-layouts: 10.3 us -> 0.04 us
  other arithmetic: 8.47 us -> 1.38 us
    reduce_scatter x2 -> x0, waiting for transfers between devices: 52.6 us -> none  [the longest x1 29.7 us: shards(): lax.psum_scatter(grad_query[0], 'dp', scatter_dimension=0, tiled=True)]
    ppermute x0 -> x18, starting transfers between devices: none -> 25.6 us  [sent(): return lax.ppermute(x, axis, pairs(8, mask))]
    ppermute x0 -> x18, waiting for transfers between devices: none -> 17.5 us  [sent(): return lax.ppermute(x, axis, pairs(8, mask))]
    pallas_call x0 -> x8, Pallas kernels: none -> 11.8 us  [the longest x3 7.04 us: pack_piece(): pl.pallas_call(kernel, out_shape=(shape, shape), in_specs=[HBM, HBM, ANY]...]
    unnamed x19 -> x12, local copies, waits for them, and re-layouts: 8.92 us -> 0.04 us
    all_to_all x2 -> x1, waiting for transfers between devices: 15 us -> 6.77 us  [shards(): lax.all_to_all(message, group, split_axis=0, concat_axis=0, tiled=True)]
    all_to_all x2 -> x1, starting transfers between devices: 17.7 us -> 11.5 us  [shards(): lax.all_to_all(message, group, split_axis=0, concat_axis=0, tiled=True)]
    reduce_sum x5 -> x0, other arithmetic: 2.6 us -> none  [the longest x1 1.42 us: shards(): neuron_part = jnp.sum(down_grad * down_grad, axis=0)]
  transfers between devices with their start and end apart: 4 -> 19, of which waited for: 4 -> 12; matrix products, arithmetic and copies ran while one was open for 11% -> 1% of each run, Pallas kernels for 0% -> 4%
where the time goes in v1:
time: 76.6 us; the launch traced here: 76.1 us
  starting transfers between devices  37.1 us (48%)
  waiting for transfers between devices  24.2 us (32%)
  Pallas kernels  11.8 us (15%)
  between operations  1.55 us (2%)
  other arithmetic  1.38 us (2%)
    ppermute x18, starting transfers between devices, sent(): return lax.ppermute(x, axis, pairs(8, mask))  25.6 us
    ppermute x18, waiting for transfers between devices, sent(): return lax.ppermute(x, axis, pairs(8, mask))  17.5 us
    all_to_all x1, starting transfers between devices, shards(): lax.all_to_all(message, group, split_axis=0, concat_axis=0, tiled=True)  11.5 us
    pallas_call x3, Pallas kernels, pack_piece(): pl.pallas_call(kernel, out_shape=(shape, shape), in_specs=[HBM, HBM, ANY]...  7.04 us
    all_to_all x1, waiting for transfers between devices, shards(): lax.all_to_all(message, group, split_axis=0, concat_axis=0, tiled=True)  6.77 us
    pallas_call x1, Pallas kernels, shards(): pl.pallas_call(finish_kernel, out_shape=(jax.ShapeDtypeStruct(down_param....  3.18 us
  transfers between devices with their start and end apart: 19, of which 12 were waited for; matrix products, arithmetic and copies ran while one was open for 1% of the time, Pallas kernels for 4%

profile of v1, /device:TPU:1, one launch (start us, length us, event | category | flops | bytes accessed | tf_op | source)
XLA Modules:
  0.0 76.1 jit_solution(12707924993929616962)
XLA Ops:
  0.6 2.1 %shard_map.152 = (bf16[2304,128]{1,0:T(8,128)(2,1)S(1)}, bf16[2304,128]{1,0:T(8,128)(2,1)S(1)}) custom-call(bf16[576,4608]{1,0:T(8,128)(2,1)} %bitcast.7, bf16[8,72,512]{2,1,0:T(8,128)(2,1)} %bitcast.10, bf16[8,72,512]{2,1,0:T(8,128)(2,1)} %bitcast.11), custom_call_target="tpu_custom_call" | custom-call | tf_op jit(solution)/shard_map/pallas_call | solution.py:93
  2.7 2.5 %shard_map.153 = (bf16[4608,128]{1,0:T(8,128)(2,1)S(1)}, bf16[4608,128]{1,0:T(8,128)(2,1)S(1)}) custom-call(bf16[576,4608]{1,0:T(8,128)(2,1)} %bitcast.8, bf16[8,72,512]{2,1,0:T(8,128)(2,1)} %bitcast.12, bf16[2304,128]{1,0:T(8,128)(2,1)S(1)} %get-tuple-element.30._.refs_0_), custom_call_target="tpu_custom_call" | custom-call | tf_op jit(solution)/shard_map/pallas_call | solution.py:93
  5.2 3.3 %collective-permute-start.5 = (bf16[4608,128]{1,0:T(8,128)(2,1)S(1)}, bf16[4608,128]{1,0:T(8,128)(2,1)S(1)}, u32[]{:S(2)}, u32[]{:S(2)}) collective-permute-start(bf16[4608,128]{1,0:T(8,128)(2,1)S(1)} %get-tuple-element.34), channel_id=1, source_target_pairs={{0,32},{32,0},{64,96},{96,64},{128,160},{160,128},{192,224},{224,1... | collective-permute-start | bytes 3538952 | tf_op jit(solution)/shard_map/ppermute | solution.py:116
  8.5 0.1 collective-permute-start.10
  8.6 2.5 %shard_map.154 = (bf16[4608,128]{1,0:T(8,128)(2,1)S(1)}, bf16[4608,128]{1,0:T(8,128)(2,1)S(1)}) custom-call(bf16[576,4608]{1,0:T(8,128)(2,1)} %bitcast.9, bf16[8,72,512]{2,1,0:T(8,128)(2,1)} %bitcast.13, bf16[4608,128]{1,0:T(8,128)(2,1)S(1)} %get-tuple-element.31._.refs_0_), custom_call_target="tpu_custom_call" | custom-call | tf_op jit(solution)/shard_map/pallas_call | solution.py:93
  11.1 0.5 collective-permute-start
  11.6 0.2 collective-permute-done.10.refs_1_
  11.8 0.1 add_convert_fusion.4
  11.9 0.1 collective-permute-start.11
  12.0 1.5 %collective-permute-start.12 = (bf16[576,128]{1,0:T(8,128)(2,1)S(1)}, bf16[576,128]{1,0:T(8,128)(2,1)S(1)}, u32[]{:S(2)}, u32[]{:S(2)}) collective-permute-start(bf16[576,128]{1,0:T(8,128)(2,1)S(1)} %get-tuple-element.62), channel_id=1, source_target_pairs={{0,192},{32,224},{64,128},{96,160},{128,64},{160,96},{192,0},{224,... | collective-permute-start | bytes 442376 | tf_op jit(solution)/shard_map/ppermute | solution.py:116
  13.5 0.0 collective-permute-done.5.refs_1_
  13.5 0.2 add_convert_fusion
  13.6 0.5 collective-permute-start.6
  14.1 1.6 %collective-permute-start.7 = (bf16[1152,128]{1,0:T(8,128)(2,1)S(1)}, bf16[1152,128]{1,0:T(8,128)(2,1)S(1)}, u32[]{:S(2)}, u32[]{:S(2)}) collective-permute-start(bf16[1152,128]{1,0:T(8,128)(2,1)S(1)} %get-tuple-element.54), channel_id=1, source_target_pairs={{0,192},{32,224},{64,128},{96,160},{128,64},{160,96},{192,0},{224,... | collective-permute-start | bytes 884744 | tf_op jit(solution)/shard_map/ppermute | solution.py:116
  15.8 0.0 collective-permute-done.refs_1_
  15.8 0.2 add_convert_fusion.2
  15.9 0.2 collective-permute-start.1
  16.1 0.9 %collective-permute-done.11.refs_2_ = bf16[576,128]{1,0:T(8,128)(2,1)S(1)} collective-permute-done((bf16[576,128]{1,0:T(8,128)(2,1)S(1)}, bf16[576,128]{1,0:T(8,128)(2,1)S(1)}, u32[]{:S(2)}, u32[]{:S(2)}) %collective-permute-start.11) | collective-permute-done | bytes 147488 | tf_op jit(solution)/shard_map/ppermute | solution.py:116
  17.0 1.0 %collective-permute-start.2 = (bf16[1152,128]{1,0:T(8,128)(2,1)S(1)}, bf16[1152,128]{1,0:T(8,128)(2,1)S(1)}, u32[]{:S(2)}, u32[]{:S(2)}) collective-permute-start(bf16[1152,128]{1,0:T(8,128)(2,1)S(1)} %get-tuple-element.58), channel_id=1, source_target_pairs={{0,192},{32,224},{64,128},{96,160},{128,64},{160,96},{192,0},{224,... | collective-permute-start | bytes 884744 | tf_op jit(solution)/shard_map/ppermute | solution.py:116
  18.0 0.3 collective-permute-done.12.refs_3_
  18.3 0.1 add_convert_fusion.10
  18.4 0.0 copy-start
  18.4 0.0 copy-start.2
  18.4 1.5 %collective-permute-start.13 = (bf16[288,128]{1,0:T(8,128)(2,1)S(1)}, bf16[288,128]{1,0:T(8,128)(2,1)S(1)}, u32[]{:S(2)}, u32[]{:S(2)}) collective-permute-start(bf16[288,128]{1,0:T(8,128)(2,1)S(1)} %get-tuple-element.61), channel_id=1, source_target_pairs={{0,192},{32,224},{64,128},{96,160},{128,64},{160,96},{192,0},{224,... | collective-permute-start | bytes 221192 | tf_op jit(solution)/shard_map/ppermute | solution.py:116
  19.9 3.5 %collective-permute-done.6.refs_2_ = bf16[1152,128]{1,0:T(8,128)(2,1)S(1)} collective-permute-done((bf16[1152,128]{1,0:T(8,128)(2,1)S(1)}, bf16[1152,128]{1,0:T(8,128)(2,1)S(1)}, u32[]{:S(2)}, u32[]{:S(2)}) %collective-permute-start.6) | collective-permute-done | bytes 294944 | tf_op jit(solution)/shard_map/ppermute | solution.py:116
  23.3 1.3 %collective-permute-done.7.refs_3_ = bf16[1152,128]{1,0:T(8,128)(2,1)S(1)} collective-permute-done((bf16[1152,128]{1,0:T(8,128)(2,1)S(1)}, bf16[1152,128]{1,0:T(8,128)(2,1)S(1)}, u32[]{:S(2)}, u32[]{:S(2)}) %collective-permute-start.7) | collective-permute-done | bytes 294944 | tf_op jit(solution)/shard_map/ppermute | solution.py:116
  24.6 0.1 add_convert_fusion.6
  24.8 1.4 %collective-permute-start.8 = (bf16[576,128]{1,0:T(8,128)(2,1)S(1)}, bf16[576,128]{1,0:T(8,128)(2,1)S(1)}, u32[]{:S(2)}, u32[]{:S(2)}) collective-permute-start(bf16[576,128]{1,0:T(8,128)(2,1)S(1)} %get-tuple-element.53), channel_id=1, source_target_pairs={{0,192},{32,224},{64,128},{96,160},{128,64},{160,96},{192,0},{224,... | collective-permute-start | bytes 442376 | tf_op jit(solution)/shard_map/ppermute | solution.py:116
  26.2 0.0 collective-permute-start.9
  26.2 3.4 %collective-permute-done.1.refs_2_ = bf16[1152,128]{1,0:T(8,128)(2,1)S(1)} collective-permute-done((bf16[1152,128]{1,0:T(8,128)(2,1)S(1)}, bf16[1152,128]{1,0:T(8,128)(2,1)S(1)}, u32[]{:S(2)}, u32[]{:S(2)}) %collective-permute-start.1) | collective-permute-done | bytes 294944 | tf_op jit(solution)/shard_map/ppermute | solution.py:116
  29.7 1.3 %collective-permute-done.2.refs_3_ = bf16[1152,128]{1,0:T(8,128)(2,1)S(1)} collective-permute-done((bf16[1152,128]{1,0:T(8,128)(2,1)S(1)}, bf16[1152,128]{1,0:T(8,128)(2,1)S(1)}, u32[]{:S(2)}, u32[]{:S(2)}) %collective-permute-start.2) | collective-permute-done | bytes 294944 | tf_op jit(solution)/shard_map/ppermute | solution.py:116
  31.0 0.1 add_convert_fusion.8
  31.1 1.4 %collective-permute-start.3 = (bf16[576,128]{1,0:T(8,128)(2,1)S(1)}, bf16[576,128]{1,0:T(8,128)(2,1)S(1)}, u32[]{:S(2)}, u32[]{:S(2)}) collective-permute-start(bf16[576,128]{1,0:T(8,128)(2,1)S(1)} %get-tuple-element.57), channel_id=1, source_target_pairs={{0,192},{32,224},{64,128},{96,160},{128,64},{160,96},{192,0},{224,... | collective-permute-start | bytes 442376 | tf_op jit(solution)/shard_map/ppermute | solution.py:116
  32.5 0.0 collective-permute-start.4
  32.5 0.0 collective-permute-done.13.refs_4_
  32.5 1.5 %collective-permute-start.14 = (bf16[288,128]{1,0:T(8,128)(2,1)S(1)}, bf16[288,128]{1,0:T(8,128)(2,1)S(1)}, u32[]{:S(2)}, u32[]{:S(2)}) collective-permute-start(bf16[288,128]{1,0:T(8,128)(2,1)S(1)} %get-tuple-element.60), channel_id=1, source_target_pairs={{0,64},{32,96},{64,0},{96,32},{128,192},{160,224},{192,128},{224,1... | collective-permute-start | bytes 221192 | tf_op jit(solution)/shard_map/ppermute | solution.py:116
  34.0 3.4 %collective-permute-done.14.refs_5_ = bf16[288,128]{1,0:T(8,128)(2,1)S(1)} collective-permute-done((bf16[288,128]{1,0:T(8,128)(2,1)S(1)}, bf16[288,128]{1,0:T(8,128)(2,1)S(1)}, u32[]{:S(2)}, u32[]{:S(2)}) %collective-permute-start.14) | collective-permute-done | bytes 73760 | tf_op jit(solution)/shard_map/ppermute | solution.py:116
  37.4 0.0 copy-done
  37.4 0.0 copy-done.2
  37.4 0.2 shard_map.155
  37.6 1.7 %collective-permute-start.15 = (f32[8,128]{1,0:T(8,128)S(1)}, f32[8,128]{1,0:T(8,128)S(1)}, u32[]{:S(2)}, u32[]{:S(2)}) collective-permute-start(f32[8,128]{1,0:T(8,128)S(1)} %get-tuple-element.41), channel_id=1, source_target_pairs={{0,1},{1,0},{2,3},{3,2},{4,5},{5,4},{6,7},{7,6},{8,9},{9,8},{10,11... | collective-permute-start | bytes 12296 | tf_op jit(solution)/shard_map/ppermute | solution.py:116
  39.3 1.1 %collective-permute-done.15 = f32[8,128]{1,0:T(8,128)S(1)} collective-permute-done((f32[8,128]{1,0:T(8,128)S(1)}, f32[8,128]{1,0:T(8,128)S(1)}, u32[]{:S(2)}, u32[]{:S(2)}) %collective-permute-start.15) | collective-permute-done | bytes 4128 | tf_op jit(solution)/shard_map/ppermute | solution.py:116
  40.5 3.1 %collective-permute-start.16 = (f32[8,128]{1,0:T(8,128)S(1)}, f32[8,128]{1,0:T(8,128)S(1)}, u32[]{:S(2)}, u32[]{:S(2)}) collective-permute-start(f32[8,128]{1,0:T(8,128)S(1)} %add.81), channel_id=1, source_target_pairs={{0,2},{1,3},{2,0},{3,1},{4,6},{5,7},{6,4},{7,5},{8,10},{9,11},{10,... | collective-permute-start | bytes 12296 | tf_op jit(solution)/shard_map/ppermute | solution.py:116
  43.6 1.0 %collective-permute-done.16 = f32[8,128]{1,0:T(8,128)S(1)} collective-permute-done((f32[8,128]{1,0:T(8,128)S(1)}, f32[8,128]{1,0:T(8,128)S(1)}, u32[]{:S(2)}, u32[]{:S(2)}) %collective-permute-start.16) | collective-permute-done | bytes 4128 | tf_op jit(solution)/shard_map/ppermute | solution.py:116
  44.6 6.1 %collective-permute-start.17 = (f32[8,128]{1,0:T(8,128)S(1)}, f32[8,128]{1,0:T(8,128)S(1)}, u32[]{:S(2)}, u32[]{:S(2)}) collective-permute-start(f32[8,128]{1,0:T(8,128)S(1)} %add.82), channel_id=1, source_target_pairs={{0,4},{1,5},{2,6},{3,7},{4,0},{5,1},{6,2},{7,3},{8,12},{9,13},{10,... | collective-permute-start | bytes 12296 | tf_op jit(solution)/shard_map/ppermute | solution.py:116
  50.7 1.0 %collective-permute-done.17 = f32[8,128]{1,0:T(8,128)S(1)} collective-permute-done((f32[8,128]{1,0:T(8,128)S(1)}, f32[8,128]{1,0:T(8,128)S(1)}, u32[]{:S(2)}, u32[]{:S(2)}) %collective-permute-start.17) | collective-permute-done | bytes 4128 | tf_op jit(solution)/shard_map/ppermute | solution.py:116
  51.7 0.0 collective-permute-done.8.refs_4_
  51.7 0.0 collective-permute-done.9.refs_5_
  51.7 0.3 shard_map.156
  52.1 0.0 collective-permute-done.3.refs_4_
  52.1 0.0 collective-permute-done.4.refs_5_
  52.1 0.0 copy-start.5
  52.1 0.0 copy-start.1
  52.1 0.0 copy-start.3
  52.1 0.0 copy-start.4
  52.1 0.3 shard_map.157
  52.4 0.8 message.1
  53.2 11.5 %all-to-all-start = ((f32[32,8,128]{2,1,0:T(8,128)}), f32[32,8,128]{2,1,0:T(8,128)S(1)}, u32[]{:S(2)}, u32[]{:S(2)}) async-start(f32[32,8,128]{2,1,0:T(8,128)} %message.1), calls=%async_computation | async-start | bytes 262144 | tf_op jit(solution)/shard_map/all_to_all | solution.py:330
  65.5 0.0 copy-done.5
  65.5 0.1 pad_maximum_fusion.keep_ref
  65.6 6.8 %all-to-all-done.got_ref = f32[32,8,128]{2,1,0:T(8,128)S(1)} async-done(((f32[32,8,128]{2,1,0:T(8,128)}), f32[32,8,128]{2,1,0:T(8,128)S(1)}, u32[]{:S(2)}, u32[]{:S(2)}) %all-to-all-start) | async-done | bytes 131104 | tf_op jit(solution)/shard_map/all_to_all | solution.py:330
  72.3 0.0 copy-done.1
  72.3 3.2 %finish.1 = (f32[576,576]{1,0:T(8,128)}, f32[576,576]{1,0:T(8,128)}, bf16[576,576]{1,0:T(8,128)(2,1)}, f32[1,576]{1,0:T(1,128)S(1)}, f32[72,512]{1,0:T(8,128)}, ...) custom-call(f32[2]{0:T(128)S(1)} %pad_maximum_fusion.keep_ref, ...), custom_call_target="tpu_custom_call" | custom-call | tf_op jit(solution)/shard_map/finish/pallas_call | solution.py:332
  75.5 0.6 reduce
  (6 shorter events, 0.0 us)
Async XLA Ops:
  5.2 8.3 %collective-permute-start.5 = (bf16[4608,128]{1,0:T(8,128)(2,1)S(1)}, bf16[4608,128]{1,0:T(8,128)(2,1)S(1)}, u32[]{:S(2)}, u32[]{:S(2)}) collective-permute-start(bf16[4608,128]{1,0:T(8,128)(2,1)S(1)} %get-tuple-element.34), channel_id=1, source_target_pairs={{0,32},{32,0},{64,96},{96,64},{128,160},{160,128},{192,224},{224,1... | collective-permute-start | bytes 3538952 | tf_op jit(solution)/shard_map/ppermute | solution.py:116
  8.5 3.3 %collective-permute-start.10 = (bf16[2304,128]{1,0:T(8,128)(2,1)S(1)}, bf16[2304,128]{1,0:T(8,128)(2,1)S(1)}, u32[]{:S(2)}, u32[]{:S(2)}) collective-permute-start(bf16[2304,128]{1,0:T(8,128)(2,1)S(1)} %get-tuple-element.35), channel_id=1, source_target_pairs={{0,32},{32,0},{64,96},{96,64},{128,160},{160,128},{192,224},{224,1... | collective-permute-start | bytes 1769480 | tf_op jit(solution)/shard_map/ppermute | solution.py:116
  11.1 4.7 %collective-permute-start = (bf16[4608,128]{1,0:T(8,128)(2,1)S(1)}, bf16[4608,128]{1,0:T(8,128)(2,1)S(1)}, u32[]{:S(2)}, u32[]{:S(2)}) collective-permute-start(bf16[4608,128]{1,0:T(8,128)(2,1)S(1)} %get-tuple-element.33), channel_id=1, source_target_pairs={{0,32},{32,0},{64,96},{96,64},{128,160},{160,128},{192,224},{224,1... | collective-permute-start | bytes 3538952 | tf_op jit(solution)/shard_map/ppermute | solution.py:116
  11.9 5.1 %collective-permute-start.11 = (bf16[576,128]{1,0:T(8,128)(2,1)S(1)}, bf16[576,128]{1,0:T(8,128)(2,1)S(1)}, u32[]{:S(2)}, u32[]{:S(2)}) collective-permute-start(bf16[576,128]{1,0:T(8,128)(2,1)S(1)} %get-tuple-element.63), channel_id=1, source_target_pairs={{0,64},{32,96},{64,0},{96,32},{128,192},{160,224},{192,128},{224,1... | collective-permute-start | bytes 442376 | tf_op jit(solution)/shard_map/ppermute | solution.py:116
  12.0 6.3 %collective-permute-start.12 = (bf16[576,128]{1,0:T(8,128)(2,1)S(1)}, bf16[576,128]{1,0:T(8,128)(2,1)S(1)}, u32[]{:S(2)}, u32[]{:S(2)}) collective-permute-start(bf16[576,128]{1,0:T(8,128)(2,1)S(1)} %get-tuple-element.62), channel_id=1, source_target_pairs={{0,192},{32,224},{64,128},{96,160},{128,64},{160,96},{192,0},{224,... | collective-permute-start | bytes 442376 | tf_op jit(solution)/shard_map/ppermute | solution.py:116
  13.6 9.7 %collective-permute-start.6 = (bf16[1152,128]{1,0:T(8,128)(2,1)S(1)}, bf16[1152,128]{1,0:T(8,128)(2,1)S(1)}, u32[]{:S(2)}, u32[]{:S(2)}) collective-permute-start(bf16[1152,128]{1,0:T(8,128)(2,1)S(1)} %get-tuple-element.55), channel_id=1, source_target_pairs={{0,64},{32,96},{64,0},{96,32},{128,192},{160,224},{192,128},{224,1... | collective-permute-start | bytes 884744 | tf_op jit(solution)/shard_map/ppermute | solution.py:116
  14.1 10.5 %collective-permute-start.7 = (bf16[1152,128]{1,0:T(8,128)(2,1)S(1)}, bf16[1152,128]{1,0:T(8,128)(2,1)S(1)}, u32[]{:S(2)}, u32[]{:S(2)}) collective-permute-start(bf16[1152,128]{1,0:T(8,128)(2,1)S(1)} %get-tuple-element.54), channel_id=1, source_target_pairs={{0,192},{32,224},{64,128},{96,160},{128,64},{160,96},{192,0},{224,... | collective-permute-start | bytes 884744 | tf_op jit(solution)/shard_map/ppermute | solution.py:116
  15.9 13.7 %collective-permute-start.1 = (bf16[1152,128]{1,0:T(8,128)(2,1)S(1)}, bf16[1152,128]{1,0:T(8,128)(2,1)S(1)}, u32[]{:S(2)}, u32[]{:S(2)}) collective-permute-start(bf16[1152,128]{1,0:T(8,128)(2,1)S(1)} %get-tuple-element.59), channel_id=1, source_target_pairs={{0,64},{32,96},{64,0},{96,32},{128,192},{160,224},{192,128},{224,1... | collective-permute-start | bytes 884744 | tf_op jit(solution)/shard_map/ppermute | solution.py:116
  17.0 14.0 %collective-permute-start.2 = (bf16[1152,128]{1,0:T(8,128)(2,1)S(1)}, bf16[1152,128]{1,0:T(8,128)(2,1)S(1)}, u32[]{:S(2)}, u32[]{:S(2)}) collective-permute-start(bf16[1152,128]{1,0:T(8,128)(2,1)S(1)} %get-tuple-element.58), channel_id=1, source_target_pairs={{0,192},{32,224},{64,128},{96,160},{128,64},{160,96},{192,0},{224,... | collective-permute-start | bytes 884744 | tf_op jit(solution)/shard_map/ppermute | solution.py:116
  18.4 19.0 %copy-start = (f32[576,576]{1,0:T(8,128)S(1)}, f32[576,576]{1,0:T(8,128)}, u32[]{:S(2)}) copy-start(f32[576,576]{1,0:T(8,128)} %refs_6_.5) | copy-start | bytes 3981316
  18.4 19.0 %copy-start.2 = (f32[72,512]{1,0:T(8,128)S(1)}, f32[72,512]{1,0:T(8,128)}, u32[]{:S(2)}) copy-start(f32[72,512]{1,0:T(8,128)} %refs_7_.1) | copy-start | bytes 442372
  18.4 14.1 %collective-permute-start.13 = (bf16[288,128]{1,0:T(8,128)(2,1)S(1)}, bf16[288,128]{1,0:T(8,128)(2,1)S(1)}, u32[]{:S(2)}, u32[]{:S(2)}) collective-permute-start(bf16[288,128]{1,0:T(8,128)(2,1)S(1)} %get-tuple-element.61), channel_id=1, source_target_pairs={{0,192},{32,224},{64,128},{96,160},{128,64},{160,96},{192,0},{224,... | collective-permute-start | bytes 221192 | tf_op jit(solution)/shard_map/ppermute | solution.py:116
  24.8 27.0 %collective-permute-start.8 = (bf16[576,128]{1,0:T(8,128)(2,1)S(1)}, bf16[576,128]{1,0:T(8,128)(2,1)S(1)}, u32[]{:S(2)}, u32[]{:S(2)}) collective-permute-start(bf16[576,128]{1,0:T(8,128)(2,1)S(1)} %get-tuple-element.53), channel_id=1, source_target_pairs={{0,192},{32,224},{64,128},{96,160},{128,64},{160,96},{192,0},{224,... | collective-permute-start | bytes 442376 | tf_op jit(solution)/shard_map/ppermute | solution.py:116
  26.2 25.5 %collective-permute-start.9 = (bf16[576,128]{1,0:T(8,128)(2,1)S(1)}, bf16[576,128]{1,0:T(8,128)(2,1)S(1)}, u32[]{:S(2)}, u32[]{:S(2)}) collective-permute-start(bf16[576,128]{1,0:T(8,128)(2,1)S(1)} %get-tuple-element.52), channel_id=1, source_target_pairs={{0,64},{32,96},{64,0},{96,32},{128,192},{160,224},{192,128},{224,1... | collective-permute-start | bytes 442376 | tf_op jit(solution)/shard_map/ppermute | solution.py:116
  31.1 21.0 %collective-permute-start.3 = (bf16[576,128]{1,0:T(8,128)(2,1)S(1)}, bf16[576,128]{1,0:T(8,128)(2,1)S(1)}, u32[]{:S(2)}, u32[]{:S(2)}) collective-permute-start(bf16[576,128]{1,0:T(8,128)(2,1)S(1)} %get-tuple-element.57), channel_id=1, source_target_pairs={{0,192},{32,224},{64,128},{96,160},{128,64},{160,96},{192,0},{224,... | collective-permute-start | bytes 442376 | tf_op jit(solution)/shard_map/ppermute | solution.py:116
  32.5 19.5 %collective-permute-start.4 = (bf16[576,128]{1,0:T(8,128)(2,1)S(1)}, bf16[576,128]{1,0:T(8,128)(2,1)S(1)}, u32[]{:S(2)}, u32[]{:S(2)}) collective-permute-start(bf16[576,128]{1,0:T(8,128)(2,1)S(1)} %get-tuple-element.56), channel_id=1, source_target_pairs={{0,64},{32,96},{64,0},{96,32},{128,192},{160,224},{192,128},{224,1... | collective-permute-start | bytes 442376 | tf_op jit(solution)/shard_map/ppermute | solution.py:116
  32.5 4.8 %collective-permute-start.14 = (bf16[288,128]{1,0:T(8,128)(2,1)S(1)}, bf16[288,128]{1,0:T(8,128)(2,1)S(1)}, u32[]{:S(2)}, u32[]{:S(2)}) collective-permute-start(bf16[288,128]{1,0:T(8,128)(2,1)S(1)} %get-tuple-element.60), channel_id=1, source_target_pairs={{0,64},{32,96},{64,0},{96,32},{128,192},{160,224},{192,128},{224,1... | collective-permute-start | bytes 221192 | tf_op jit(solution)/shard_map/ppermute | solution.py:116
  37.6 2.9 %collective-permute-start.15 = (f32[8,128]{1,0:T(8,128)S(1)}, f32[8,128]{1,0:T(8,128)S(1)}, u32[]{:S(2)}, u32[]{:S(2)}) collective-permute-start(f32[8,128]{1,0:T(8,128)S(1)} %get-tuple-element.41), channel_id=1, source_target_pairs={{0,1},{1,0},{2,3},{3,2},{4,5},{5,4},{6,7},{7,6},{8,9},{9,8},{10,11... | collective-permute-start | bytes 12296 | tf_op jit(solution)/shard_map/ppermute | solution.py:116
  40.5 4.1 %collective-permute-start.16 = (f32[8,128]{1,0:T(8,128)S(1)}, f32[8,128]{1,0:T(8,128)S(1)}, u32[]{:S(2)}, u32[]{:S(2)}) collective-permute-start(f32[8,128]{1,0:T(8,128)S(1)} %add.81), channel_id=1, source_target_pairs={{0,2},{1,3},{2,0},{3,1},{4,6},{5,7},{6,4},{7,5},{8,10},{9,11},{10,... | collective-permute-start | bytes 12296 | tf_op jit(solution)/shard_map/ppermute | solution.py:116
  44.6 7.1 %collective-permute-start.17 = (f32[8,128]{1,0:T(8,128)S(1)}, f32[8,128]{1,0:T(8,128)S(1)}, u32[]{:S(2)}, u32[]{:S(2)}) collective-permute-start(f32[8,128]{1,0:T(8,128)S(1)} %add.82), channel_id=1, source_target_pairs={{0,4},{1,5},{2,6},{3,7},{4,0},{5,1},{6,2},{7,3},{8,12},{9,13},{10,... | collective-permute-start | bytes 12296 | tf_op jit(solution)/shard_map/ppermute | solution.py:116
  52.1 13.4 %copy-start.5 = (f32[576]{0:T(1024)S(1)}, f32[576]{0:T(1024)}, u32[]{:S(2)}) copy-start(f32[576]{0:T(1024)} %param.13) | copy-start | bytes 6916
  52.1 20.2 %copy-start.1 = (f32[576,576]{1,0:T(8,128)S(1)}, f32[576,576]{1,0:T(8,128)}, u32[]{:S(2)}) copy-start(f32[576,576]{1,0:T(8,128)} %param_ref.1) | copy-start | bytes 3981316
  52.1 20.2 %copy-start.3 = (f32[72,512]{1,0:T(8,128)S(1)}, f32[72,512]{1,0:T(8,128)}, u32[]{:S(2)}) copy-start(f32[72,512]{1,0:T(8,128)} %query_param_ref.1) | copy-start | bytes 442372
  52.1 20.2 %copy-start.4 = (f32[4]{0:T(128)S(1)}, f32[4]{0:T(128)}, u32[]{:S(2)}) copy-start(f32[4]{0:T(128)} %param.16) | copy-start | bytes 52
  53.2 19.1 %all-to-all-start = ((f32[32,8,128]{2,1,0:T(8,128)}), f32[32,8,128]{2,1,0:T(8,128)S(1)}, u32[]{:S(2)}, u32[]{:S(2)}) async-start(f32[32,8,128]{2,1,0:T(8,128)} %message.1), calls=%async_computation | async-start | bytes 262144 | tf_op jit(solution)/shard_map/all_to_all | solution.py:330

commit v2 on v1

v2 whole, which is shorter than its diff:
```python
import jax
import jax.numpy as jnp
from jax import lax
from jax.experimental import pallas as pl
from jax.experimental.pallas import tpu as pltpu
from jax.sharding import PartitionSpec as P

D = 4608
HEAD_DIM = 128
FF = 18432

BETA_ONE = 0.9
BETA_TWO = 0.95
EPSILON = 1e-08
LEARN_RATE = 0.003
DECAY_RATE = 0.1

LANES = 128
ROW_BLOCKS = 6
PIECES = ((0, 256), (256, 320))
SLOTS = ((0, 1), (0, 2), (1, 3), (1, 2), (0, 0), (0, 3), (1, 0), (1, 1))
ANY = pl.BlockSpec(memory_space=pl.ANY)
HBM = pl.BlockSpec(memory_space=pltpu.HBM)
VMEM = pl.BlockSpec(memory_space=pltpu.VMEM)
SMEM = pl.BlockSpec(memory_space=pltpu.SMEM)


PARAMS = pltpu.CompilerParams(vmem_limit_bytes=8 << 20)


def pairs(size, mask):
    return [(i, i ^ mask) for i in range(size)]


def far(x):
    return pltpu.with_memory_space_constraint(x, pltpu.HBM)


def near(x):
    return pltpu.with_memory_space_constraint(x, pltpu.VMEM)


def down_rows(piece):
    return 2 * PIECES[piece][1] + PIECES[piece][1] // 4


def query_rows(piece, query_chunks):
    return query_chunks.shape[1] * query_chunks.shape[2] // LANES if piece == 0 else 0


def down_at(piece, query, slot):
    return slot * down_rows(piece) + query * (0 if slot < 2 else 1 if slot < 4 else 2)


def query_at(query, d):
    block = down_rows(0)
    return {1: 2 * block, 3: 4 * block + query, 2: 8 * block + 2 * query, 0: 8 * block + 3 * query}[d]


def piece_rows(piece, query):
    return len(SLOTS) * down_rows(piece) + 4 * query


def pack(parts, columns, query_chunks, after):
    q_rows, q_cols = query_chunks.shape[1:]
    heads = q_cols // LANES
    span = columns.shape[1] // 4
    slots = len(SLOTS)

    def kernel(down_ref, query_ref, _, *refs):
        outs, bufs, sems = refs[: len(parts)], refs[len(parts) : 2 * len(parts)], refs[2 * len(parts) :]
        me = lax.axis_index("dp")
        y, core = me // 2, me % 2
        shared, whole = [], []
        for (piece, mine), out, buf, sem in zip(parts, outs, bufs, sems):
            start, width = PIECES[piece]
            query = query_rows(piece, query_chunks)
            owner = core if mine else 1 - core
            for d in range(4):
                lane = pl.multiple_of(span * (y ^ d) + 4 * LANES, LANES)
                source = down_ref.at[pl.ds(start, width), pl.ds(lane, LANES)]
                shared.append(pltpu.make_async_copy(source, buf.at[d], sem.at[slots, d]))
            for slot, (half, d) in enumerate(SLOTS):
                for j in range(2):
                    lane = pl.multiple_of(span * (y ^ d) + 5 * LANES * owner + (2 * half + j) * LANES, LANES)
                    source = down_ref.at[pl.ds(start, width), pl.ds(lane, LANES)]
                    target = out.at[pl.ds(down_at(piece, query, slot) + j * width, width), :]
                    whole.append(pltpu.make_async_copy(source, target, sem.at[slot, j]))
            if piece == 0:
                for d in range(4):
                    for head in range(heads):
                        source = query_ref.at[2 * (y ^ d) + owner, :, pl.ds(head * LANES, LANES)]
                        target = out.at[pl.ds(query_at(query, d) + head * q_rows, q_rows), :]
                        whole.append(pltpu.make_async_copy(source, target, sem.at[2 * d + head // 2, 2 + head % 2]))
        for copy in shared + whole:
            copy.start()
        for copy in shared:
            copy.wait()
        for (piece, mine), out, buf in zip(parts, outs, bufs):
            width = PIECES[piece][1]
            quarter = width // 4
            lower = (core == 0) if mine else (core == 1)
            low = lax.broadcasted_iota(jnp.int32, (quarter, LANES), 1) < LANES // 2
            for slot, (half, d) in enumerate(SLOTS):
                first = buf[d, pl.ds(2 * half * quarter, quarter), :].astype(jnp.float32)
                second = buf[d, pl.ds((2 * half + 1) * quarter, quarter), :].astype(jnp.float32)
                packed = jnp.where(
                    lower,
                    jnp.where(low, first, pltpu.roll(second, LANES // 2, 1)),
                    jnp.where(low, pltpu.roll(first, LANES // 2, 1), second),
                )
                row = down_at(piece, query_rows(piece, query_chunks), slot) + 2 * width
                at = (pl.ds(row, quarter), slice(None))
                out[at] = packed.astype(jnp.bfloat16)
        for copy in whole:
            copy.wait()

    return pl.pallas_call(
        kernel,
        out_shape=tuple(
            pltpu.VMEM((piece_rows(p, query_rows(p, query_chunks)), LANES), jnp.bfloat16) for p, _ in parts
        ),
        in_specs=[HBM, HBM, ANY],
        out_specs=(VMEM,) * len(parts),
        scratch_shapes=[pltpu.VMEM((4, PIECES[p][1], LANES), jnp.bfloat16) for p, _ in parts]
        + [pltpu.SemaphoreType.DMA((slots + 1, 4)) for _ in parts],
        compiler_params=PARAMS,
    )(far(columns), far(query_chunks), after)


def added(*terms):
    total = terms[0].astype(jnp.float32)
    for term in terms[1:]:
        total = total + term.astype(jnp.float32)
    return total


def sent(x, mask, axis="dp"):
    return lax.ppermute(x, axis, pairs(8, mask))


def reduce_piece(piece, query, other, own):
    block = down_rows(piece)

    def part(first, last):
        return own[first:last], other[first:last]

    b_at, kept_at = down_at(piece, query, 2), down_at(piece, query, 4)
    first_a = added(*part(0, b_at)).astype(jnp.bfloat16)
    first_b = added(*part(b_at, kept_at)).astype(jnp.bfloat16)
    if query:
        across = added(*part(query_at(query, 2), query_at(query, 2) + query)).astype(jnp.bfloat16)
    first_a = sent(first_a, 2)
    first_b = sent(first_b, 6)
    if query:
        across = sent(across, 4)
    a_at, b_at = down_at(piece, query, 5), down_at(piece, query, 7)
    second_a = added(*part(a_at, a_at + block), first_a[block : 2 * block]).astype(jnp.bfloat16)
    second_b = added(*part(b_at, b_at + block), first_b[block : 2 * block]).astype(jnp.bfloat16)
    second_a = sent(second_a, 6)
    second_b = sent(second_b, 2)
    return (own, other, first_a, first_b, second_a, second_b), (across if query else None)


def moment_new(before, grad):
    return BETA_ONE * before + (1.0 - BETA_ONE) * grad


def column_sum(x):
    return jnp.sum(x * x, axis=0, keepdims=True)


def gather_query(query, terms, across, query_moment):
    q_rows, q_cols = query_moment.shape
    block = down_rows(0)

    def kernel(own_ref, other_ref, first_a, first_b, across_ref, moment_ref, new_ref, sums_ref):
        sums_ref[...] = jnp.zeros_like(sums_ref)
        for head in range(q_cols // LANES):
            at = head * q_rows
            grad = added(
                own_ref[pl.ds(query_at(query, 0) + at, q_rows), :],
                other_ref[pl.ds(query_at(query, 0) + at, q_rows), :],
                first_a[pl.ds(2 * block + at, q_rows), :],
                first_b[pl.ds(2 * block + at, q_rows), :],
                across_ref[pl.ds(at, q_rows), :],
            ) * (1.0 / 8.0)
            span = (slice(None), slice(head * LANES, (head + 1) * LANES))
            new_ref[span] = moment_new(moment_ref[span], grad)
            sums_ref[head : head + 1, :] = column_sum(grad)

    return pl.pallas_call(
        kernel,
        out_shape=(pltpu.VMEM(query_moment.shape, jnp.float32), pltpu.VMEM((8, LANES), jnp.float32)),
        in_specs=[VMEM] * 6,
        out_specs=(VMEM,) * 2,
        compiler_params=PARAMS,
        name="query",
    )(*(near(t) for t in (*terms[:4], across, query_moment)))


def gather_piece(piece, query, terms, down_moment, so_far):
    start, width = PIECES[piece]
    quarter = width // 4
    first, last = piece == 0, piece == len(PIECES) - 1
    half_tile = LANES // 2
    tensors = lax.axis_size("tensor")

    def kernel(*refs):
        own_ref, other_ref, first_a, first_b, second_a, second_b, moment_ref = refs[:7]
        if first:
            new_ref, sums_ref = refs[7:]
            sums_ref[...] = jnp.zeros_like(sums_ref)
        elif last:
            _, before_ref, heads_ref, new_ref, message_ref, sums_ref = refs[7:]
            sums_ref[...] = before_ref[...]
        else:
            _, before_ref, new_ref, sums_ref = refs[7:]
            sums_ref[...] = before_ref[...]
        core = lax.axis_index("dp") % 2

        def mean(half, at, count):
            kept = down_at(piece, query, 4 + 2 * half) + at
            step_one, step_two = (first_b, second_b) if half else (first_a, second_a)
            return added(
                own_ref[pl.ds(kept, count), :],
                other_ref[pl.ds(kept, count), :],
                step_one[pl.ds(at, count), :],
                step_two[pl.ds(at, count), :],
            ) * (1.0 / 8.0)

        parts = []
        for part in range(4):
            packed = mean(part // 2, 2 * width, quarter)
            parts.append(pltpu.roll(packed, half_tile, 1) if part % 2 else packed)
        rest = jnp.concatenate(parts, axis=0)
        for c in range(0, width, LANES):
            step = min(LANES, width - c)
            span = slice(start + c, start + c + step)
            total = jnp.zeros((1, step), jnp.float32)
            for tile in range(4):
                half, j = tile // 2, tile % 2
                grad = mean(half, j * width + c, step).T
                at = (pl.ds(pl.multiple_of(half_tile * core + tile * LANES, half_tile), LANES), span)
                new_ref[at] = moment_new(moment_ref[at], grad)
                total += column_sum(grad)
            grad = rest[c : c + step].T[:half_tile]
            at = (pl.ds(pl.multiple_of(4 * LANES * (1 - core), half_tile), half_tile), span)
            new_ref[at] = moment_new(moment_ref[at], grad)
            row = (start + c) // LANES
            sums_ref[row : row + 1, :step] = total + column_sum(grad)
        if last:
            me = lax.axis_index("tensor")
            sums = sums_ref[...]
            row = lax.broadcasted_iota(jnp.int32, sums.shape, 0)
            lane = lax.broadcasted_iota(jnp.int32, sums.shape, 1)
            neurons = jnp.where(row < 5, sums, 0.0)
            heads = jnp.sum(heads_ref[...], axis=1, keepdims=True)
            spread = jnp.sum(jnp.where(row == lane, heads, 0.0), axis=0, keepdims=True)
            mine = neurons + jnp.where(row == 5, spread, 0.0)
            for target in range(message_ref.shape[0]):
                message_ref[target] = jnp.where(me == target % tensors, mine, neurons)

    new = pltpu.VMEM(down_moment.shape, jnp.float32)
    sums = pltpu.VMEM((8, LANES), jnp.float32)
    out_shape, extra = (new, sums), so_far
    scratch = []
    if last:
        message = pltpu.VMEM((lax.axis_size("dp") * tensors, 8, LANES), jnp.float32)
        out_shape, scratch = (new, message), [sums]
    operands = tuple(near(t) for t in (*terms, down_moment, *extra))
    return pl.pallas_call(
        kernel,
        out_shape=out_shape,
        in_specs=[VMEM] * len(operands),
        out_specs=(VMEM,) * len(out_shape),
        scratch_shapes=scratch,
        input_output_aliases={} if first else {7: 0},
        compiler_params=PARAMS,
    )(*operands)


def store_kernel(new_ref, query_new_ref, moment_out, query_moment_out, sems):
    copies = (
        pltpu.make_async_copy(new_ref, moment_out, sems.at[0]),
        pltpu.make_async_copy(query_new_ref, query_moment_out, sems.at[1]),
    )
    for copy in copies:
        copy.start()
    for copy in copies:
        copy.wait()


def finish_kernel(
    keep_ref, got_ref, new_ref, param_ref, second_ref, query_new_ref, query_param_ref, query_second_ref,
    param_out, update_out, second_out, query_param_out, query_update_out, query_second_out,
    param_buf, update_buf, query_param_buf, query_update_buf, sems, query_sems,
):
    keep_one, keep_two = keep_ref[0], keep_ref[1]
    total = jnp.sum(got_ref[...], axis=0)

    def second_new(before, mean):
        return BETA_TWO * before + (1.0 - BETA_TWO) * mean

    def factor(second):
        return 1.0 / (keep_one * (jnp.sqrt(second / keep_two) + EPSILON))

    def write(at, scale, new, param, update_to, param_to):
        old = param[at]
        update = new[at] * scale
        update_to[at] = update.astype(jnp.bfloat16)
        param_to[at] = old - LEARN_RATE * (update + DECAY_RATE * old)

    rows, cols = new_ref.shape
    spans = [slice(k, min(k + LANES, cols)) for k in range(0, cols, LANES)]
    factors = []
    for k, span in enumerate(spans):
        second = second_new(second_ref[:, span], total[k : k + 1, : span.stop - span.start] * (1.0 / FF))
        second_out[span] = second[0]
        factors.append(factor(second))
    copies = []
    block = rows // ROW_BLOCKS
    for b in range(ROW_BLOCKS):
        part = slice(b * block, (b + 1) * block)
        for span, scale in zip(spans, factors):
            write((part, span), scale, new_ref, param_ref, update_buf, param_buf)
        copies.append(pltpu.make_async_copy(param_buf.at[part], param_out.at[part], sems.at[0, b]))
        copies.append(pltpu.make_async_copy(update_buf.at[part], update_out.at[part], sems.at[1, b]))
        copies[-2].start()
        copies[-1].start()
    heads = query_new_ref.shape[1] // HEAD_DIM
    for head in range(heads):
        mean = total[5:6, head : head + 1] * (1.0 / (D * HEAD_DIM))
        second = second_new(query_second_ref[:, head : head + 1], mean)
        query_second_out[:, head : head + 1] = second
        span = slice(head * HEAD_DIM, (head + 1) * HEAD_DIM)
        write((slice(None), span), factor(second), query_new_ref, query_param_ref, query_update_buf, query_param_buf)
    copies.append(pltpu.make_async_copy(query_param_buf, query_param_out, query_sems.at[0]))
    copies.append(pltpu.make_async_copy(query_update_buf, query_update_out, query_sems.at[1]))
    copies[-2].start()
    copies[-1].start()
    for copy in copies:
        copy.wait()


def shards(
    grad_down,
    grad_query,
    down_param,
    down_moment,
    down_second,
    query_param,
    query_moment,
    query_second,
    step_count,
):
    replicas = lax.axis_size("dp")
    step_value = step_count[0].astype(jnp.float32)
    keep = jnp.stack(
        [1.0 - jnp.power(jnp.float32(BETA_ONE), step_value), 1.0 - jnp.power(jnp.float32(BETA_TWO), step_value)]
    )
    columns = grad_down[0].T
    query_chunks = grad_query[0].reshape(replicas, -1, grad_query.shape[2])
    last = len(PIECES) - 1
    (send,) = pack(((0, False),), columns, query_chunks, query_chunks)
    others, owns = [sent(send, 1)], []
    for piece in range(last):
        own, send = pack(((piece, True), (piece + 1, False)), columns, query_chunks, send)
        owns.append(own)
        others.append(sent(send, 1))
    owns += pack(((last, True),), columns, query_chunks, send)
    so_far = ()
    gathered = []
    for piece in range(len(PIECES)):
        query = query_rows(piece, query_chunks)
        terms, across = reduce_piece(piece, query, others[piece], owns[piece])
        gathered.append((piece, query, terms))
        if query:
            query_new, heads = gather_query(query, terms, across, query_moment)
    for mask in (1, 2, 7):
        heads = heads + sent(heads, mask, "ctx")
    for piece, query, terms in gathered:
        if piece == last:
            so_far += (heads,)
        so_far = gather_piece(piece, query, terms, down_moment, so_far)
    new, message = so_far
    got = lax.all_to_all(message, ("dp", "tensor"), split_axis=0, concat_axis=0, tiled=True)
    down_moment_new, query_moment_new = pl.pallas_call(
        store_kernel,
        out_shape=tuple(pltpu.HBM(x.shape, jnp.float32) for x in (new, query_new)),
        in_specs=[VMEM, VMEM],
        out_specs=(HBM, HBM),
        scratch_shapes=[pltpu.SemaphoreType.DMA((2,))],
        compiler_params=PARAMS,
        name="store",
    )(near(new), near(query_new))
    f32, bf16 = jnp.float32, jnp.bfloat16
    outs = pl.pallas_call(
        finish_kernel,
        out_shape=(
            pltpu.HBM(down_param.shape, f32),
            pltpu.HBM(down_param.shape, bf16),
            jax.ShapeDtypeStruct(down_second.shape, f32),
            pltpu.HBM(query_param.shape, f32),
            pltpu.HBM(query_param.shape, bf16),
            jax.ShapeDtypeStruct((1, query_second.shape[0]), f32),
        ),
        in_specs=[SMEM] + [VMEM] * 7,
        out_specs=(HBM, HBM, VMEM, HBM, HBM, VMEM),
        scratch_shapes=[
            pltpu.VMEM(down_param.shape, f32),
            pltpu.VMEM(down_param.shape, bf16),
            pltpu.VMEM(query_param.shape, f32),
            pltpu.VMEM(query_param.shape, bf16),
            pltpu.SemaphoreType.DMA((2, ROW_BLOCKS)),
            pltpu.SemaphoreType.DMA((2,)),
        ],
        compiler_params=PARAMS, name="finish",
    )(
        keep, near(got), near(new), near(down_param), down_second[None, :],
        near(query_new), near(query_param), query_second[None, :],
    )
    down_param_new, down_update, down_second_new = outs[:3]
    query_param_new, query_update, query_second_new = outs[3:]
    return (
        down_param_new,
        down_moment_new,
        down_second_new,
        down_update,
        query_param_new,
        query_moment_new,
        query_second_new[0],
        query_update,
    )


def solution(mesh):
    in_specs = (
        P("dp", "tensor", "ctx"),
        P("dp", "ctx", "tensor"),
        P(("tensor", "dp"), "ctx"),
        P(("tensor", "dp"), "ctx"),
        P("ctx"),
        P(("ctx", "dp"), "tensor"),
        P(("ctx", "dp"), "tensor"),
        P("tensor"),
        P(),
    )
    out_specs = (
        P(("tensor", "dp"), "ctx"),
        P(("tensor", "dp"), "ctx"),
        P("ctx"),
        P(("tensor", "dp"), "ctx"),
        P(("ctx", "dp"), "tensor"),
        P(("ctx", "dp"), "tensor"),
        P("tensor"),
        P(("ctx", "dp"), "tensor"),
    )

    return jax.shard_map(shards, mesh=mesh, in_specs=in_specs, out_specs=out_specs, check_vma=False)
```

time: 76.6 us -> 74.9 us (0.978)
  starting transfers between devices: 37.1 us -> 33.6 us
  waiting for transfers between devices: 24.2 us -> 27 us
    ppermute x18 -> x14, starting transfers between devices: 25.6 us -> 20.4 us  [sent(): return lax.ppermute(x, axis, pairs(8, mask))]
    ppermute x18 -> x14, waiting for transfers between devices: 17.5 us -> 21.4 us  [sent(): return lax.ppermute(x, axis, pairs(8, mask))]
    all_to_all x1, starting transfers between devices: 11.5 us -> 13.2 us  [shards(): lax.all_to_all(message, ('dp', 'tensor'), split_axis=0, concat_axis=0, ti...]
    all_to_all x1, waiting for transfers between devices: 6.77 us -> 5.6 us  [shards(): lax.all_to_all(message, ('dp', 'tensor'), split_axis=0, concat_axis=0, ti...]
  transfers between devices with their start and end apart: 19 -> 15, of which waited for: 12 -> 9; matrix products, arithmetic and copies ran while one was open for 1% -> 1% of each run, Pallas kernels for 4% -> 8%
where the time goes in v2:
time: 74.9 us; the launch traced here: 74.5 us
  starting transfers between devices  33.6 us (45%)
  waiting for transfers between devices  27 us (36%)
  Pallas kernels  11.7 us (16%)
  between operations  1.53 us (2%)
  other arithmetic  0.76 us (1%)
    ppermute x14, waiting for transfers between devices, sent(): return lax.ppermute(x, axis, pairs(8, mask))  21.4 us
    ppermute x14, starting transfers between devices, sent(): return lax.ppermute(x, axis, pairs(8, mask))  20.4 us
    all_to_all x1, starting transfers between devices, shards(): lax.all_to_all(message, ('dp', 'tensor'), split_axis=0, concat_axis=0, ti...  13.2 us
    pallas_call x3, Pallas kernels, pack(): pl.pallas_call(kernel, out_shape=tuple((pltpu.VMEM((piece_rows(p, query_r...  6.24 us
    all_to_all x1, waiting for transfers between devices, shards(): lax.all_to_all(message, ('dp', 'tensor'), split_axis=0, concat_axis=0, ti...  5.6 us
    pallas_call x1, Pallas kernels, shards(): pl.pallas_call(finish_kernel, out_shape=(pltpu.HBM(down_param.shape, f32)...  2.76 us
  transfers between devices with their start and end apart: 15, of which 9 were waited for; matrix products, arithmetic and copies ran while one was open for 1% of the time, Pallas kernels for 8%

profile of v2, /device:TPU:1, one launch (start us, length us, event | category | flops | bytes accessed | tf_op | source)
XLA Modules:
  0.0 74.5 jit_solution(12709588435440867772)
XLA Ops:
  0.6 1.7 %shard_map.152._ = bf16[5760,128]{1,0:T(8,128)(2,1)S(1)} custom-call(bf16[576,4608]{1,0:T(8,128)(2,1)} %bitcast.7, bf16[8,72,512]{2,1,0:T(8,128)(2,1)} %bitcast.10, bf16[8,72,512]{2,1,0:T(8,128)(2,1)} %bitcast.11), custom_call_target="tpu_custom_call" | custom-call | tf_op jit(solution)/shard_map/pallas_call | solution.py:118
  2.4 3.3 %collective-permute-start.5 = (bf16[5760,128]{1,0:T(8,128)(2,1)S(1)}, bf16[5760,128]{1,0:T(8,128)(2,1)S(1)}, u32[]{:S(2)}, u32[]{:S(2)}) collective-permute-start(bf16[5760,128]{1,0:T(8,128)(2,1)S(1)} %shard_map.152._), channel_id=1, source_target_pairs={{0,32},{32,0},{64,96},{96,64},{128,160},{160,128},{192,224},{224,1... | collective-permute-start | bytes 4423688 | tf_op jit(solution)/shard_map/ppermute | solution.py:139
  5.6 2.7 %shard_map.153 = (bf16[5760,128]{1,0:T(8,128)(2,1)S(1)}, bf16[5760,128]{1,0:T(8,128)(2,1)S(1)}) custom-call(bf16[576,4608]{1,0:T(8,128)(2,1)} %bitcast.8, bf16[8,72,512]{2,1,0:T(8,128)(2,1)} %bitcast.12, bf16[5760,128]{1,0:T(8,128)(2,1)S(1)} %shard_map.152._), custom_call_target="tpu_custom_call" | custom-call | tf_op jit(solution)/shard_map/pallas_call | solution.py:118
  8.3 0.1 collective-permute-start
  8.5 1.8 %shard_map.154.refs_0_ = bf16[5760,128]{1,0:T(8,128)(2,1)S(1)} custom-call(bf16[576,4608]{1,0:T(8,128)(2,1)} %bitcast.9, bf16[8,72,512]{2,1,0:T(8,128)(2,1)} %bitcast.13, bf16[5760,128]{1,0:T(8,128)(2,1)S(1)} %get-tuple-element.24._), custom_call_target="tpu_custom_call" | custom-call | tf_op jit(solution)/shard_map/pallas_call | solution.py:118
  10.3 0.0 collective-permute-done.5.refs_1_.other_ref
  10.3 0.2 add_convert_fusion
  10.5 0.1 collective-permute-start.6
  10.6 1.5 %collective-permute-start.7 = (bf16[1440,128]{1,0:T(8,128)(2,1)S(1)}, bf16[1440,128]{1,0:T(8,128)(2,1)S(1)}, u32[]{:S(2)}, u32[]{:S(2)}) collective-permute-start(bf16[1440,128]{1,0:T(8,128)(2,1)S(1)} %get-tuple-element.42), channel_id=1, source_target_pairs={{0,192},{32,224},{64,128},{96,160},{128,64},{160,96},{192,0},{224,... | collective-permute-start | bytes 1105928 | tf_op jit(solution)/shard_map/ppermute | solution.py:139
  12.1 0.0 collective-permute-done.refs_1_
  12.1 0.2 add_convert_fusion.2
  12.3 0.0 copy-start.3
  12.3 0.5 collective-permute-start.1
  12.8 1.6 %collective-permute-start.2 = (bf16[1440,128]{1,0:T(8,128)(2,1)S(1)}, bf16[1440,128]{1,0:T(8,128)(2,1)S(1)}, u32[]{:S(2)}, u32[]{:S(2)}) collective-permute-start(bf16[1440,128]{1,0:T(8,128)(2,1)S(1)} %get-tuple-element.46), channel_id=1, source_target_pairs={{0,192},{32,224},{64,128},{96,160},{128,64},{160,96},{192,0},{224,... | collective-permute-start | bytes 1105928 | tf_op jit(solution)/shard_map/ppermute | solution.py:139
  14.5 5.8 %collective-permute-done.6.refs_2_.first_a = bf16[1440,128]{1,0:T(8,128)(2,1)S(1)} collective-permute-done((bf16[1440,128]{1,0:T(8,128)(2,1)S(1)}, bf16[1440,128]{1,0:T(8,128)(2,1)S(1)}, u32[]{:S(2)}, u32[]{:S(2)}) %collective-permute-start.6) | collective-permute-done | bytes 368672 | tf_op jit(solution)/shard_map/ppermute | solution.py:139
  20.3 1.3 %collective-permute-done.7.refs_3_.first_b = bf16[1440,128]{1,0:T(8,128)(2,1)S(1)} collective-permute-done((bf16[1440,128]{1,0:T(8,128)(2,1)S(1)}, bf16[1440,128]{1,0:T(8,128)(2,1)S(1)}, u32[]{:S(2)}, u32[]{:S(2)}) %collective-permute-start.7) | collective-permute-done | bytes 368672 | tf_op jit(solution)/shard_map/ppermute | solution.py:139
  21.6 0.1 add_convert_fusion.6
  21.7 1.2 %collective-permute-start.8 = (bf16[576,128]{1,0:T(8,128)(2,1)S(1)}, bf16[576,128]{1,0:T(8,128)(2,1)S(1)}, u32[]{:S(2)}, u32[]{:S(2)}) collective-permute-start(bf16[576,128]{1,0:T(8,128)(2,1)S(1)} %get-tuple-element.41), channel_id=1, source_target_pairs={{0,192},{32,224},{64,128},{96,160},{128,64},{160,96},{192,0},{224,... | collective-permute-start | bytes 442376 | tf_op jit(solution)/shard_map/ppermute | solution.py:139
  22.9 0.0 collective-permute-start.9
  22.9 5.3 %collective-permute-done.1.refs_2_ = bf16[1440,128]{1,0:T(8,128)(2,1)S(1)} collective-permute-done((bf16[1440,128]{1,0:T(8,128)(2,1)S(1)}, bf16[1440,128]{1,0:T(8,128)(2,1)S(1)}, u32[]{:S(2)}, u32[]{:S(2)}) %collective-permute-start.1) | collective-permute-done | bytes 368672 | tf_op jit(solution)/shard_map/ppermute | solution.py:139
  28.2 1.3 %collective-permute-done.2.refs_3_ = bf16[1440,128]{1,0:T(8,128)(2,1)S(1)} collective-permute-done((bf16[1440,128]{1,0:T(8,128)(2,1)S(1)}, bf16[1440,128]{1,0:T(8,128)(2,1)S(1)}, u32[]{:S(2)}, u32[]{:S(2)}) %collective-permute-start.2) | collective-permute-done | bytes 368672 | tf_op jit(solution)/shard_map/ppermute | solution.py:139
  29.5 0.1 add_convert_fusion.4
  29.7 1.2 %collective-permute-start.3 = (bf16[720,128]{1,0:T(8,128)(2,1)S(1)}, bf16[720,128]{1,0:T(8,128)(2,1)S(1)}, u32[]{:S(2)}, u32[]{:S(2)}) collective-permute-start(bf16[720,128]{1,0:T(8,128)(2,1)S(1)} %get-tuple-element.45), channel_id=1, source_target_pairs={{0,192},{32,224},{64,128},{96,160},{128,64},{160,96},{192,0},{224,... | collective-permute-start | bytes 552968 | tf_op jit(solution)/shard_map/ppermute | solution.py:139
  30.9 0.0 collective-permute-start.4
  30.9 0.0 copy-start
  30.9 2.8 %collective-permute-start.10 = (bf16[288,128]{1,0:T(8,128)(2,1)S(1)}, bf16[288,128]{1,0:T(8,128)(2,1)S(1)}, u32[]{:S(2)}, u32[]{:S(2)}) collective-permute-start(bf16[288,128]{1,0:T(8,128)(2,1)S(1)} %add_convert_fusion.8), channel_id=1, source_target_pairs={{0,128},{32,160},{64,192},{96,224},{128,0},{160,32},{192,64},{224,... | collective-permute-start | bytes 221192 | tf_op jit(solution)/shard_map/ppermute | solution.py:139
  33.7 3.7 %collective-permute-done.10.across_ref = bf16[288,128]{1,0:T(8,128)(2,1)S(1)} collective-permute-done((bf16[288,128]{1,0:T(8,128)(2,1)S(1)}, bf16[288,128]{1,0:T(8,128)(2,1)S(1)}, u32[]{:S(2)}, u32[]{:S(2)}) %collective-permute-start.10) | collective-permute-done | bytes 73760 | tf_op jit(solution)/shard_map/ppermute | solution.py:139
  37.4 0.0 copy-done.3
  37.4 0.1 query.1
  37.5 0.9 %collective-permute-start.11 = (f32[8,128]{1,0:T(8,128)S(1)}, f32[8,128]{1,0:T(8,128)S(1)}, u32[]{:S(2)}, u32[]{:S(2)}) collective-permute-start(f32[8,128]{1,0:T(8,128)S(1)} %get-tuple-element.28), channel_id=1, source_target_pairs={{0,1},{1,0},{2,3},{3,2},{4,5},{5,4},{6,7},{7,6},{8,9},{9,8},{10,11... | collective-permute-start | bytes 12296 | tf_op jit(solution)/shard_map/ppermute | solution.py:139
  38.4 1.9 %collective-permute-done.11 = f32[8,128]{1,0:T(8,128)S(1)} collective-permute-done((f32[8,128]{1,0:T(8,128)S(1)}, f32[8,128]{1,0:T(8,128)S(1)}, u32[]{:S(2)}, u32[]{:S(2)}) %collective-permute-start.11) | collective-permute-done | bytes 4128 | tf_op jit(solution)/shard_map/ppermute | solution.py:139
  40.4 2.3 %collective-permute-start.12 = (f32[8,128]{1,0:T(8,128)S(1)}, f32[8,128]{1,0:T(8,128)S(1)}, u32[]{:S(2)}, u32[]{:S(2)}) collective-permute-start(f32[8,128]{1,0:T(8,128)S(1)} %add.61), channel_id=1, source_target_pairs={{0,2},{1,3},{2,0},{3,1},{4,6},{5,7},{6,4},{7,5},{8,10},{9,11},{10,... | collective-permute-start | bytes 12296 | tf_op jit(solution)/shard_map/ppermute | solution.py:139
  42.7 1.0 %collective-permute-done.12 = f32[8,128]{1,0:T(8,128)S(1)} collective-permute-done((f32[8,128]{1,0:T(8,128)S(1)}, f32[8,128]{1,0:T(8,128)S(1)}, u32[]{:S(2)}, u32[]{:S(2)}) %collective-permute-start.12) | collective-permute-done | bytes 4128 | tf_op jit(solution)/shard_map/ppermute | solution.py:139
  43.7 4.8 %collective-permute-start.13 = (f32[8,128]{1,0:T(8,128)S(1)}, f32[8,128]{1,0:T(8,128)S(1)}, u32[]{:S(2)}, u32[]{:S(2)}) collective-permute-start(f32[8,128]{1,0:T(8,128)S(1)} %add.62), channel_id=1, source_target_pairs={{0,7},{1,6},{2,5},{3,4},{4,3},{5,2},{6,1},{7,0},{8,15},{9,14},{10,... | collective-permute-start | bytes 12296 | tf_op jit(solution)/shard_map/ppermute | solution.py:139
  48.5 1.0 %collective-permute-done.13 = f32[8,128]{1,0:T(8,128)S(1)} collective-permute-done((f32[8,128]{1,0:T(8,128)S(1)}, f32[8,128]{1,0:T(8,128)S(1)}, u32[]{:S(2)}, u32[]{:S(2)}) %collective-permute-start.13) | collective-permute-done | bytes 4128 | tf_op jit(solution)/shard_map/ppermute | solution.py:139
  49.5 0.0 collective-permute-done.8.refs_4_
  49.5 0.0 collective-permute-done.9.refs_5_
  49.5 0.0 copy-done
  49.5 0.3 shard_map.155
  49.8 0.0 collective-permute-done.3.refs_4_
  49.8 0.0 collective-permute-done.4.refs_5_
  49.8 0.0 copy-start.5
  49.8 1.1 %shard_map.156 = (f32[576,576]{1,0:T(8,128)S(1)}, f32[32,8,128]{2,1,0:T(8,128)}) custom-call(bf16[5760,128]{1,0:T(8,128)(2,1)S(1)} %shard_map.154.refs_0_, bf16[5760,128]{1,0:T(8,128)(2,1)S(1)} %collective-permute-done.refs_1_, bf16[1440,128]{1,0:T(8,128)(2,1)S(1)} %collective-permute-done.1.refs_2_, ...), custom_call_target="tpu_custom_call", output_to_operand_aliasing={{0}: (7, {})} | custom-call | tf_op jit(solution)/shard_map/pallas_call | solution.py:272
  50.9 0.0 copy-start.1
  50.9 0.0 copy-start.2
  50.9 0.0 copy-start.4
  50.9 13.2 %all-to-all-start = ((f32[32,8,128]{2,1,0:T(8,128)}), f32[32,8,128]{2,1,0:T(8,128)S(1)}, u32[]{:S(2)}, u32[]{:S(2)}) async-start(f32[32,8,128]{2,1,0:T(8,128)} %get-tuple-element.29), calls=%async_computation | async-start | bytes 262144 | tf_op jit(solution)/shard_map/all_to_all | solution.py:387
  64.9 0.0 copy-done.5
  64.9 0.1 pad_maximum_fusion.keep_ref
  65.0 1.2 %store.1 = (f32[576,576]{1,0:T(8,128)}, f32[72,512]{1,0:T(8,128)}) custom-call(f32[576,576]{1,0:T(8,128)S(1)} %get-tuple-element.30.new_ref, f32[72,512]{1,0:T(8,128)S(1)} %get-tuple-element.31.query_new_ref), custom_call_target="tpu_custom_call" | custom-call | tf_op jit(solution)/shard_map/store/pallas_call | solution.py:388
  66.2 5.6 %all-to-all-done.got_ref = f32[32,8,128]{2,1,0:T(8,128)S(1)} async-done(((f32[32,8,128]{2,1,0:T(8,128)}), f32[32,8,128]{2,1,0:T(8,128)S(1)}, u32[]{:S(2)}, u32[]{:S(2)}) %all-to-all-start) | async-done | bytes 131104 | tf_op jit(solution)/shard_map/all_to_all | solution.py:387
  71.8 0.0 copy-done.1
  71.8 0.0 copy-done.2
  71.8 0.0 copy-done.4
  71.8 2.8 %finish.1 = (f32[576,576]{1,0:T(8,128)}, bf16[576,576]{1,0:T(8,128)(2,1)}, f32[576]{0:T(1024)}, f32[72,512]{1,0:T(8,128)}, bf16[72,512]{1,0:T(8,128)(2,1)}, /*index=5*/f32[1,4]{1,0:T(1,128)}) custom-call(f32[2]{0:T(128)S(1)} %pad_maximum_fusion.keep_ref, f32[32,8,128]{2,1,0:T(8,128)S(1)} %all-to-all-done.got_ref, f32[576,576]{1,0:T(8,128)S(1)} %get-tuple-element.30.new_ref, ...), custom_call_target="tpu_custom_call" | custom-call | tf_op jit(solution)/shard_map/finish/pallas_call | solution.py:398
  (5 shorter events, 0.0 us)
Async XLA Ops:
  2.4 8.0 %collective-permute-start.5 = (bf16[5760,128]{1,0:T(8,128)(2,1)S(1)}, bf16[5760,128]{1,0:T(8,128)(2,1)S(1)}, u32[]{:S(2)}, u32[]{:S(2)}) collective-permute-start(bf16[5760,128]{1,0:T(8,128)(2,1)S(1)} %shard_map.152._), channel_id=1, source_target_pairs={{0,32},{32,0},{64,96},{96,64},{128,160},{160,128},{192,224},{224,1... | collective-permute-start | bytes 4423688 | tf_op jit(solution)/shard_map/ppermute | solution.py:139
  8.3 3.8 %collective-permute-start = (bf16[5760,128]{1,0:T(8,128)(2,1)S(1)}, bf16[5760,128]{1,0:T(8,128)(2,1)S(1)}, u32[]{:S(2)}, u32[]{:S(2)}) collective-permute-start(bf16[5760,128]{1,0:T(8,128)(2,1)S(1)} %get-tuple-element.24._), channel_id=1, source_target_pairs={{0,32},{32,0},{64,96},{96,64},{128,160},{160,128},{192,224},{224,1... | collective-permute-start | bytes 4423688 | tf_op jit(solution)/shard_map/ppermute | solution.py:139
  10.5 9.8 %collective-permute-start.6 = (bf16[1440,128]{1,0:T(8,128)(2,1)S(1)}, bf16[1440,128]{1,0:T(8,128)(2,1)S(1)}, u32[]{:S(2)}, u32[]{:S(2)}) collective-permute-start(bf16[1440,128]{1,0:T(8,128)(2,1)S(1)} %get-tuple-element.43), channel_id=1, source_target_pairs={{0,64},{32,96},{64,0},{96,32},{128,192},{160,224},{192,128},{224,1... | collective-permute-start | bytes 1105928 | tf_op jit(solution)/shard_map/ppermute | solution.py:139
  10.6 11.0 %collective-permute-start.7 = (bf16[1440,128]{1,0:T(8,128)(2,1)S(1)}, bf16[1440,128]{1,0:T(8,128)(2,1)S(1)}, u32[]{:S(2)}, u32[]{:S(2)}) collective-permute-start(bf16[1440,128]{1,0:T(8,128)(2,1)S(1)} %get-tuple-element.42), channel_id=1, source_target_pairs={{0,192},{32,224},{64,128},{96,160},{128,64},{160,96},{192,0},{224,... | collective-permute-start | bytes 1105928 | tf_op jit(solution)/shard_map/ppermute | solution.py:139
  12.3 25.1 %copy-start.3 = (f32[72,512]{1,0:T(8,128)S(1)}, f32[72,512]{1,0:T(8,128)}, u32[]{:S(2)}) copy-start(f32[72,512]{1,0:T(8,128)} %moment_ref.1) | copy-start | bytes 442372
  12.3 15.9 %collective-permute-start.1 = (bf16[1440,128]{1,0:T(8,128)(2,1)S(1)}, bf16[1440,128]{1,0:T(8,128)(2,1)S(1)}, u32[]{:S(2)}, u32[]{:S(2)}) collective-permute-start(bf16[1440,128]{1,0:T(8,128)(2,1)S(1)} %get-tuple-element.47), channel_id=1, source_target_pairs={{0,64},{32,96},{64,0},{96,32},{128,192},{160,224},{192,128},{224,1... | collective-permute-start | bytes 1105928 | tf_op jit(solution)/shard_map/ppermute | solution.py:139
  12.8 16.7 %collective-permute-start.2 = (bf16[1440,128]{1,0:T(8,128)(2,1)S(1)}, bf16[1440,128]{1,0:T(8,128)(2,1)S(1)}, u32[]{:S(2)}, u32[]{:S(2)}) collective-permute-start(bf16[1440,128]{1,0:T(8,128)(2,1)S(1)} %get-tuple-element.46), channel_id=1, source_target_pairs={{0,192},{32,224},{64,128},{96,160},{128,64},{160,96},{192,0},{224,... | collective-permute-start | bytes 1105928 | tf_op jit(solution)/shard_map/ppermute | solution.py:139
  21.7 27.7 %collective-permute-start.8 = (bf16[576,128]{1,0:T(8,128)(2,1)S(1)}, bf16[576,128]{1,0:T(8,128)(2,1)S(1)}, u32[]{:S(2)}, u32[]{:S(2)}) collective-permute-start(bf16[576,128]{1,0:T(8,128)(2,1)S(1)} %get-tuple-element.41), channel_id=1, source_target_pairs={{0,192},{32,224},{64,128},{96,160},{128,64},{160,96},{192,0},{224,... | collective-permute-start | bytes 442376 | tf_op jit(solution)/shard_map/ppermute | solution.py:139
  22.9 26.5 %collective-permute-start.9 = (bf16[576,128]{1,0:T(8,128)(2,1)S(1)}, bf16[576,128]{1,0:T(8,128)(2,1)S(1)}, u32[]{:S(2)}, u32[]{:S(2)}) collective-permute-start(bf16[576,128]{1,0:T(8,128)(2,1)S(1)} %get-tuple-element.40), channel_id=1, source_target_pairs={{0,64},{32,96},{64,0},{96,32},{128,192},{160,224},{192,128},{224,1... | collective-permute-start | bytes 442376 | tf_op jit(solution)/shard_map/ppermute | solution.py:139
  29.7 20.1 %collective-permute-start.3 = (bf16[720,128]{1,0:T(8,128)(2,1)S(1)}, bf16[720,128]{1,0:T(8,128)(2,1)S(1)}, u32[]{:S(2)}, u32[]{:S(2)}) collective-permute-start(bf16[720,128]{1,0:T(8,128)(2,1)S(1)} %get-tuple-element.45), channel_id=1, source_target_pairs={{0,192},{32,224},{64,128},{96,160},{128,64},{160,96},{192,0},{224,... | collective-permute-start | bytes 552968 | tf_op jit(solution)/shard_map/ppermute | solution.py:139
  30.9 19.0 %collective-permute-start.4 = (bf16[720,128]{1,0:T(8,128)(2,1)S(1)}, bf16[720,128]{1,0:T(8,128)(2,1)S(1)}, u32[]{:S(2)}, u32[]{:S(2)}) collective-permute-start(bf16[720,128]{1,0:T(8,128)(2,1)S(1)} %get-tuple-element.44), channel_id=1, source_target_pairs={{0,64},{32,96},{64,0},{96,32},{128,192},{160,224},{192,128},{224,1... | collective-permute-start | bytes 552968 | tf_op jit(solution)/shard_map/ppermute | solution.py:139
  30.9 18.6 %copy-start = (f32[576,576]{1,0:T(8,128)S(1)}, f32[576,576]{1,0:T(8,128)}, u32[]{:S(2)}) copy-start(f32[576,576]{1,0:T(8,128)} %refs_6_.3) | copy-start | bytes 3981316
  30.9 6.5 %collective-permute-start.10 = (bf16[288,128]{1,0:T(8,128)(2,1)S(1)}, bf16[288,128]{1,0:T(8,128)(2,1)S(1)}, u32[]{:S(2)}, u32[]{:S(2)}) collective-permute-start(bf16[288,128]{1,0:T(8,128)(2,1)S(1)} %add_convert_fusion.8), channel_id=1, source_target_pairs={{0,128},{32,160},{64,192},{96,224},{128,0},{160,32},{192,64},{224,... | collective-permute-start | bytes 221192 | tf_op jit(solution)/shard_map/ppermute | solution.py:139
  37.5 2.8 %collective-permute-start.11 = (f32[8,128]{1,0:T(8,128)S(1)}, f32[8,128]{1,0:T(8,128)S(1)}, u32[]{:S(2)}, u32[]{:S(2)}) collective-permute-start(f32[8,128]{1,0:T(8,128)S(1)} %get-tuple-element.28), channel_id=1, source_target_pairs={{0,1},{1,0},{2,3},{3,2},{4,5},{5,4},{6,7},{7,6},{8,9},{9,8},{10,11... | collective-permute-start | bytes 12296 | tf_op jit(solution)/shard_map/ppermute | solution.py:139
  40.4 3.4 %collective-permute-start.12 = (f32[8,128]{1,0:T(8,128)S(1)}, f32[8,128]{1,0:T(8,128)S(1)}, u32[]{:S(2)}, u32[]{:S(2)}) collective-permute-start(f32[8,128]{1,0:T(8,128)S(1)} %add.61), channel_id=1, source_target_pairs={{0,2},{1,3},{2,0},{3,1},{4,6},{5,7},{6,4},{7,5},{8,10},{9,11},{10,... | collective-permute-start | bytes 12296 | tf_op jit(solution)/shard_map/ppermute | solution.py:139
  43.7 5.7 %collective-permute-start.13 = (f32[8,128]{1,0:T(8,128)S(1)}, f32[8,128]{1,0:T(8,128)S(1)}, u32[]{:S(2)}, u32[]{:S(2)}) collective-permute-start(f32[8,128]{1,0:T(8,128)S(1)} %add.62), channel_id=1, source_target_pairs={{0,7},{1,6},{2,5},{3,4},{4,3},{5,2},{6,1},{7,0},{8,15},{9,14},{10,... | collective-permute-start | bytes 12296 | tf_op jit(solution)/shard_map/ppermute | solution.py:139
  49.8 15.1 %copy-start.5 = (f32[576]{0:T(1024)S(1)}, f32[576]{0:T(1024)}, u32[]{:S(2)}) copy-start(f32[576]{0:T(1024)} %param.13) | copy-start | bytes 6916
  50.9 20.9 %copy-start.1 = (f32[576,576]{1,0:T(8,128)S(1)}, f32[576,576]{1,0:T(8,128)}, u32[]{:S(2)}) copy-start(f32[576,576]{1,0:T(8,128)} %param_ref.1) | copy-start | bytes 3981316
  50.9 20.9 %copy-start.2 = (f32[72,512]{1,0:T(8,128)S(1)}, f32[72,512]{1,0:T(8,128)}, u32[]{:S(2)}) copy-start(f32[72,512]{1,0:T(8,128)} %query_param_ref.1) | copy-start | bytes 442372
  50.9 20.9 %copy-start.4 = (f32[4]{0:T(128)S(1)}, f32[4]{0:T(128)}, u32[]{:S(2)}) copy-start(f32[4]{0:T(128)} %param.16) | copy-start | bytes 52
  50.9 20.9 %all-to-all-start = ((f32[32,8,128]{2,1,0:T(8,128)}), f32[32,8,128]{2,1,0:T(8,128)S(1)}, u32[]{:S(2)}, u32[]{:S(2)}) async-start(f32[32,8,128]{2,1,0:T(8,128)} %get-tuple-element.29), calls=%async_computation | async-start | bytes 262144 | tf_op jit(solution)/shard_map/all_to_all | solution.py:387

commit v3 on v2

--- a/solution.py
+++ b/solution.py
@@ -22,7 +22,6 @@
 ANY = pl.BlockSpec(memory_space=pl.ANY)
 HBM = pl.BlockSpec(memory_space=pltpu.HBM)
 VMEM = pl.BlockSpec(memory_space=pltpu.VMEM)
-SMEM = pl.BlockSpec(memory_space=pltpu.SMEM)
 
 
 PARAMS = pltpu.CompilerParams(vmem_limit_bytes=8 << 20)
@@ -49,19 +48,30 @@
 
 
 def down_at(piece, query, slot):
-    return slot * down_rows(piece) + query * (0 if slot < 2 else 1 if slot < 4 else 2)
+    return slot * down_rows(piece) + query * (0 if slot < 2 else 1 if slot < 4 else 3)
 
 
 def query_at(query, d):
     block = down_rows(0)
-    return {1: 2 * block, 3: 4 * block + query, 2: 8 * block + 2 * query, 0: 8 * block + 3 * query}[d]
+    return {1: 2 * block, 3: 4 * block + query, 2: 4 * block + 2 * query, 0: 8 * block + 3 * query}[d]
 
 
 def piece_rows(piece, query):
     return len(SLOTS) * down_rows(piece) + 4 * query
 
 
-def pack(parts, columns, query_chunks, after):
+def group(piece, query, part):
+    a, b, kept = (down_at(piece, query, slot) for slot in (0, 2, 4))
+    end = piece_rows(piece, query)
+    return {
+        "a": (a, b - a, (0, 1), (1,)),
+        "b": (b, kept - b, (2, 3), (3, 2)),
+        "kept": (kept, end - kept, (4, 5, 6, 7), (0,)),
+        "all": (0, end, tuple(range(len(SLOTS))), (1, 3, 2, 0)),
+    }[part]
+
+
+def pack(parts, columns, query_chunks, after, place):
     q_rows, q_cols = query_chunks.shape[1:]
     heads = q_cols // LANES
     span = columns.shape[1] // 4
@@ -72,36 +82,48 @@
         me = lax.axis_index("dp")
         y, core = me // 2, me % 2
         shared, whole = [], []
-        for (piece, mine), out, buf, sem in zip(parts, outs, bufs, sems):
+
+        def put(copies, source, target, semaphore):
+            if place is far:
+                copies.append(pltpu.make_async_copy(source, target, semaphore))
+            else:
+                target[...] = source[...]
+
+        for (piece, part, mine), out, buf, sem in zip(parts, outs, bufs, sems):
             start, width = PIECES[piece]
             query = query_rows(piece, query_chunks)
+            base, _, its_slots, its_chunks = group(piece, query, part)
             owner = core if mine else 1 - core
-            for d in range(4):
+            for d in sorted({SLOTS[slot][1] for slot in its_slots}):
                 lane = pl.multiple_of(span * (y ^ d) + 4 * LANES, LANES)
                 source = down_ref.at[pl.ds(start, width), pl.ds(lane, LANES)]
-                shared.append(pltpu.make_async_copy(source, buf.at[d], sem.at[slots, d]))
-            for slot, (half, d) in enumerate(SLOTS):
+                put(shared, source, buf.at[d], sem.at[slots, d])
+            for slot in its_slots:
+                half, d = SLOTS[slot]
                 for j in range(2):
                     lane = pl.multiple_of(span * (y ^ d) + 5 * LANES * owner + (2 * half + j) * LANES, LANES)
                     source = down_ref.at[pl.ds(start, width), pl.ds(lane, LANES)]
-                    target = out.at[pl.ds(down_at(piece, query, slot) + j * width, width), :]
-                    whole.append(pltpu.make_async_copy(source, target, sem.at[slot, j]))
+                    target = out.at[pl.ds(down_at(piece, query, slot) - base + j * width, width), :]
+                    put(whole, source, target, sem.at[slot, j])
             if piece == 0:
-                for d in range(4):
+                for d in its_chunks:
                     for head in range(heads):
                         source = query_ref.at[2 * (y ^ d) + owner, :, pl.ds(head * LANES, LANES)]
-                        target = out.at[pl.ds(query_at(query, d) + head * q_rows, q_rows), :]
-                        whole.append(pltpu.make_async_copy(source, target, sem.at[2 * d + head // 2, 2 + head % 2]))
+                        target = out.at[pl.ds(query_at(query, d) - base + head * q_rows, q_rows), :]
+                        put(whole, source, target, sem.at[2 * d + head // 2, 2 + head % 2])
         for copy in shared + whole:
             copy.start()
         for copy in shared:
             copy.wait()
-        for (piece, mine), out, buf in zip(parts, outs, bufs):
+        for (piece, part, mine), out, buf in zip(parts, outs, bufs):
             width = PIECES[piece][1]
+            query = query_rows(piece, query_chunks)
+            base, _, its_slots, _ = group(piece, query, part)
             quarter = width // 4
             lower = (core == 0) if mine else (core == 1)
             low = lax.broadcasted_iota(jnp.int32, (quarter, LANES), 1) < LANES // 2
-            for slot, (half, d) in enumerate(SLOTS):
+            for slot in its_slots:
+                half, d = SLOTS[slot]
                 first = buf[d, pl.ds(2 * half * quarter, quarter), :].astype(jnp.float32)
                 second = buf[d, pl.ds((2 * half + 1) * quarter, quarter), :].astype(jnp.float32)
                 packed = jnp.where(
@@ -109,7 +131,7 @@
                     jnp.where(low, first, pltpu.roll(second, LANES // 2, 1)),
                     jnp.where(low, pltpu.roll(first, LANES // 2, 1), second),
                 )
-                row = down_at(piece, query_rows(piece, query_chunks), slot) + 2 * width
+                row = down_at(piece, query, slot) - base + 2 * width
                 at = (pl.ds(row, quarter), slice(None))
                 out[at] = packed.astype(jnp.bfloat16)
         for copy in whole:
@@ -118,14 +140,14 @@
     return pl.pallas_call(
         kernel,
         out_shape=tuple(
-            pltpu.VMEM((piece_rows(p, query_rows(p, query_chunks)), LANES), jnp.bfloat16) for p, _ in parts
+            pltpu.VMEM((group(p, query_rows(p, query_chunks), part)[1], LANES), jnp.bfloat16) for p, part, _ in parts
         ),
-        in_specs=[HBM, HBM, ANY],
+        in_specs=[HBM, HBM, ANY] if place is far else [VMEM, VMEM, ANY],
         out_specs=(VMEM,) * len(parts),
-        scratch_shapes=[pltpu.VMEM((4, PIECES[p][1], LANES), jnp.bfloat16) for p, _ in parts]
+        scratch_shapes=[pltpu.VMEM((4, PIECES[p][1], LANES), jnp.bfloat16) for p, _, _ in parts]
         + [pltpu.SemaphoreType.DMA((slots + 1, 4)) for _ in parts],
         compiler_params=PARAMS,
-    )(far(columns), far(query_chunks), after)
+    )(place(columns), place(query_chunks), after)
 
 
 def added(*terms):
@@ -142,24 +164,31 @@
 def reduce_piece(piece, query, other, own):
     block = down_rows(piece)
 
-    def part(first, last):
-        return own[first:last], other[first:last]
-
-    b_at, kept_at = down_at(piece, query, 2), down_at(piece, query, 4)
-    first_a = added(*part(0, b_at)).astype(jnp.bfloat16)
-    first_b = added(*part(b_at, kept_at)).astype(jnp.bfloat16)
-    if query:
-        across = added(*part(query_at(query, 2), query_at(query, 2) + query)).astype(jnp.bfloat16)
+    def rows(first, count):
+        found = []
+        for side in (own, other):
+            for part, array in side.items():
+                base, size = group(piece, query, part)[:2]
+                if base <= first and first + count <= base + size:
+                    found.append(array[first - base : first - base + count])
+        return found
+
+    b_at = down_at(piece, query, 2)
+    first_a = added(*rows(0, b_at)).astype(jnp.bfloat16)
+    first_b = added(*rows(b_at, 2 * block + query)).astype(jnp.bfloat16)
     first_a = sent(first_a, 2)
     first_b = sent(first_b, 6)
+    across = None
     if query:
+        across = added(*rows(query_at(query, 2), query)).astype(jnp.bfloat16)
         across = sent(across, 4)
     a_at, b_at = down_at(piece, query, 5), down_at(piece, query, 7)
-    second_a = added(*part(a_at, a_at + block), first_a[block : 2 * block]).astype(jnp.bfloat16)
-    second_b = added(*part(b_at, b_at + block), first_b[block : 2 * block]).astype(jnp.bfloat16)
+    second_a = added(*rows(a_at, block), first_a[block : 2 * block]).astype(jnp.bfloat16)
+    second_b = added(*rows(b_at, block), first_b[block : 2 * block]).astype(jnp.bfloat16)
     second_a = sent(second_a, 6)
     second_b = sent(second_b, 2)
-    return (own, other, first_a, first_b, second_a, second_b), (across if query else None)
+    part = "kept" if "kept" in own else "all"
+    return (own[part], other[part], first_a, first_b, second_a, second_b), across
 
 
 def moment_new(before, grad):
@@ -173,14 +202,15 @@
 def gather_query(query, terms, across, query_moment):
     q_rows, q_cols = query_moment.shape
     block = down_rows(0)
+    kept = query_at(query, 0) - group(0, query, "kept")[0]
 
     def kernel(own_ref, other_ref, first_a, first_b, across_ref, moment_ref, new_ref, sums_ref):
         sums_ref[...] = jnp.zeros_like(sums_ref)
         for head in range(q_cols // LANES):
             at = head * q_rows
             grad = added(
-                own_ref[pl.ds(query_at(query, 0) + at, q_rows), :],
-                other_ref[pl.ds(query_at(query, 0) + at, q_rows), :],
+                own_ref[pl.ds(kept + at, q_rows), :],
+                other_ref[pl.ds(kept + at, q_rows), :],
                 first_a[pl.ds(2 * block + at, q_rows), :],
                 first_b[pl.ds(2 * block + at, q_rows), :],
                 across_ref[pl.ds(at, q_rows), :],
@@ -203,6 +233,7 @@
     start, width = PIECES[piece]
     quarter = width // 4
     first, last = piece == 0, piece == len(PIECES) - 1
+    base = down_at(piece, query, 4) if first else 0
     half_tile = LANES // 2
     tensors = lax.axis_size("tensor")
 
@@ -220,7 +251,7 @@
         core = lax.axis_index("dp") % 2
 
         def mean(half, at, count):
-            kept = down_at(piece, query, 4 + 2 * half) + at
+            kept = down_at(piece, query, 4 + 2 * half) - base + at
             step_one, step_two = (first_b, second_b) if half else (first_a, second_a)
             return added(
                 own_ref[pl.ds(kept, count), :],
@@ -294,9 +325,9 @@
 def finish_kernel(
     keep_ref, got_ref, new_ref, param_ref, second_ref, query_new_ref, query_param_ref, query_second_ref,
     param_out, update_out, second_out, query_param_out, query_update_out, query_second_out,
-    param_buf, update_buf, query_param_buf, query_update_buf, sems, query_sems,
+    param_buf, update_buf, second_buf, query_param_buf, query_update_buf, query_second_buf, sems, query_sems, second_sems,
 ):
-    keep_one, keep_two = keep_ref[0], keep_ref[1]
+    keep_one, keep_two = keep_ref[:, 0:1], keep_ref[:, 1:2]
     total = jnp.sum(got_ref[...], axis=0)
 
     def second_new(before, mean):
@@ -316,9 +347,10 @@
     factors = []
     for k, span in enumerate(spans):
         second = second_new(second_ref[:, span], total[k : k + 1, : span.stop - span.start] * (1.0 / FF))
-        second_out[span] = second[0]
+        second_buf[span] = second[0]
         factors.append(factor(second))
-    copies = []
+    copies = [pltpu.make_async_copy(second_buf, second_out, second_sems.at[0])]
+    copies[-1].start()
     block = rows // ROW_BLOCKS
     for b in range(ROW_BLOCKS):
         part = slice(b * block, (b + 1) * block)
@@ -332,13 +364,14 @@
     for head in range(heads):
         mean = total[5:6, head : head + 1] * (1.0 / (D * HEAD_DIM))
         second = second_new(query_second_ref[:, head : head + 1], mean)
-        query_second_out[:, head : head + 1] = second
+        query_second_buf[:, head : head + 1] = second
         span = slice(head * HEAD_DIM, (head + 1) * HEAD_DIM)
         write((slice(None), span), factor(second), query_new_ref, query_param_ref, query_update_buf, query_param_buf)
     copies.append(pltpu.make_async_copy(query_param_buf, query_param_out, query_sems.at[0]))
     copies.append(pltpu.make_async_copy(query_update_buf, query_update_out, query_sems.at[1]))
-    copies[-2].start()
-    copies[-1].start()
+    copies.append(pltpu.make_async_copy(query_second_buf, query_second_out, second_sems.at[1]))
+    for copy in copies[-3:]:
+        copy.start()
     for copy in copies:
         copy.wait()
 
@@ -362,13 +395,23 @@
     columns = grad_down[0].T
     query_chunks = grad_query[0].reshape(replicas, -1, grad_query.shape[2])
     last = len(PIECES) - 1
-    (send,) = pack(((0, False),), columns, query_chunks, query_chunks)
-    others, owns = [sent(send, 1)], []
-    for piece in range(last):
-        own, send = pack(((piece, True), (piece + 1, False)), columns, query_chunks, send)
-        owns.append(own)
-        others.append(sent(send, 1))
-    owns += pack(((last, True),), columns, query_chunks, send)
+    last = len(PIECES) - 1
+
+    def packed(step, *parts):
+        return pack(parts, columns, query_chunks, send, near if step else far)
+
+    send = query_chunks
+    send_a, send_b = packed(0, (0, "a", False), (0, "b", False))
+    others = [{"a": sent(send_a, 1), "b": sent(send_b, 1)}, {}]
+    send = send_a
+    own_a, own_b = packed(1, (0, "a", True), (0, "b", True))
+    owns = [{"a": own_a, "b": own_b}, {}]
+    send = own_a
+    (send,) = packed(2, (1, "all", False))
+    others[1]["all"] = sent(send, 1)
+    owns[0]["kept"], send = packed(3, (0, "kept", True), (0, "kept", False))
+    others[0]["kept"] = sent(send, 1)
+    (owns[1]["all"],) = packed(4, (1, "all", True))
     so_far = ()
     gathered = []
     for piece in range(len(PIECES)):
@@ -400,25 +443,28 @@
         out_shape=(
             pltpu.HBM(down_param.shape, f32),
             pltpu.HBM(down_param.shape, bf16),
-            jax.ShapeDtypeStruct(down_second.shape, f32),
+            pltpu.HBM(down_second.shape, f32),
             pltpu.HBM(query_param.shape, f32),
             pltpu.HBM(query_param.shape, bf16),
-            jax.ShapeDtypeStruct((1, query_second.shape[0]), f32),
+            pltpu.HBM((1, query_second.shape[0]), f32),
         ),
-        in_specs=[SMEM] + [VMEM] * 7,
-        out_specs=(HBM, HBM, VMEM, HBM, HBM, VMEM),
+        in_specs=[VMEM] * 8,
+        out_specs=(HBM,) * 6,
         scratch_shapes=[
             pltpu.VMEM(down_param.shape, f32),
             pltpu.VMEM(down_param.shape, bf16),
+            pltpu.VMEM(down_second.shape, f32),
             pltpu.VMEM(query_param.shape, f32),
             pltpu.VMEM(query_param.shape, bf16),
+            pltpu.VMEM((1, query_second.shape[0]), f32),
             pltpu.SemaphoreType.DMA((2, ROW_BLOCKS)),
+            pltpu.SemaphoreType.DMA((2,)),
             pltpu.SemaphoreType.DMA((2,)),
         ],
         compiler_params=PARAMS, name="finish",
     )(
-        keep, near(got), near(new), near(down_param), down_second[None, :],
-        near(query_new), near(query_param), query_second[None, :],
+        near(keep[None, :]), near(got), near(new), near(down_param), near(down_second[None, :]),
+        near(query_new), near(query_param), near(query_second[None, :]),
     )
     down_param_new, down_update, down_second_new = outs[:3]
     query_param_new, query_update, query_second_new = outs[3:]

time: 74.9 us -> 76.1 us (1.016)
  waiting for transfers between devices: 27 us -> 31.8 us
  starting transfers between devices: 33.6 us -> 31 us
  Pallas kernels: 11.7 us -> 9.73 us
  local copies, waits for them, and re-layouts: 0.03 us -> 1.04 us
    ppermute x14 -> x16, waiting for transfers between devices: 21.4 us -> 26.2 us  [sent(): return lax.ppermute(x, axis, pairs(8, mask))]
    ppermute x14 -> x16, starting transfers between devices: 20.4 us -> 17.9 us  [sent(): return lax.ppermute(x, axis, pairs(8, mask))]
    unnamed x12 -> x16, local copies, waits for them, and re-layouts: 0.03 us -> 1.04 us
    pallas_call x3 -> x5, Pallas kernels: 6.24 us -> 5.28 us  [pack(): pl.pallas_call(kernel, out_shape=tuple((pltpu.VMEM((group(p, query_rows(p...]
    pallas_call x1, Pallas kernels: 2.76 us -> 1.8 us  [shards(): pl.pallas_call(finish_kernel, out_shape=(pltpu.HBM(down_param.shape, f32)...]
  transfers between devices with their start and end apart: 15 -> 17, of which waited for: 9 -> 11; matrix products, arithmetic and copies ran while one was open for 1% -> 1% of each run, Pallas kernels for 8% -> 4%
where the time goes in v3:
time: 76.1 us; the launch traced here: 75.9 us
  waiting for transfers between devices  31.8 us (42%)
  starting transfers between devices  31 us (41%)
  Pallas kernels  9.73 us (13%)
  between operations  1.56 us (2%)
  local copies, waits for them, and re-layouts  1.04 us (1%)
  other arithmetic  0.77 us (1%)
    ppermute x16, waiting for transfers between devices, sent(): return lax.ppermute(x, axis, pairs(8, mask))  26.2 us
    ppermute x16, starting transfers between devices, sent(): return lax.ppermute(x, axis, pairs(8, mask))  17.9 us
    all_to_all x1, starting transfers between devices, shards(): lax.all_to_all(message, ('dp', 'tensor'), split_axis=0, concat_axis=0, ti...  13.1 us
    all_to_all x1, waiting for transfers between devices, shards(): lax.all_to_all(message, ('dp', 'tensor'), split_axis=0, concat_axis=0, ti...  5.6 us
    pallas_call x5, Pallas kernels, pack(): pl.pallas_call(kernel, out_shape=tuple((pltpu.VMEM((group(p, query_rows(p...  5.28 us
    pallas_call x1, Pallas kernels, shards(): pl.pallas_call(finish_kernel, out_shape=(pltpu.HBM(down_param.shape, f32)...  1.8 us
  transfers between devices with their start and end apart: 17, of which 11 were waited for; matrix products, arithmetic and copies ran while one was open for 1% of the time, Pallas kernels for 4%

profile of v3, /device:TPU:1, one launch (start us, length us, event | category | flops | bytes accessed | tf_op | source)
XLA Modules:
  0.0 75.9 jit_solution(18092224200946390386)
XLA Ops:
  0.6 0.0 copy-start
  0.6 0.0 copy-start.1
  0.7 2.0 %shard_map.152 = (bf16[1440,128]{1,0:T(8,128)(2,1)S(1)}, bf16[1728,128]{1,0:T(8,128)(2,1)S(1)}) custom-call(bf16[576,4608]{1,0:T(8,128)(2,1)} %bitcast.8, bf16[8,72,512]{2,1,0:T(8,128)(2,1)} %bitcast.13, bf16[8,72,512]{2,1,0:T(8,128)(2,1)} %bitcast.14), custom_call_target="tpu_custom_call" | custom-call | tf_op jit(solution)/shard_map/pallas_call | solution.py:140
  2.7 0.9 %copy-done = bf16[1,4608,576]{1,2,0:T(8,128)(2,1)S(1)} copy-done((bf16[1,4608,576]{1,2,0:T(8,128)(2,1)S(1)}, bf16[1,4608,576]{1,2,0:T(8,128)(2,1)}, u32[]{:S(2)}) %copy-start) | copy-done | bytes 5308440
  3.6 0.1 copy-done.1
  3.7 0.8 %shard_map.153 = (bf16[1440,128]{1,0:T(8,128)(2,1)S(1)}, bf16[1728,128]{1,0:T(8,128)(2,1)S(1)}) custom-call(bf16[576,4608]{1,0:T(8,128)(2,1)S(1)} %bitcast.9, bf16[8,72,512]{2,1,0:T(8,128)(2,1)S(1)} %bitcast.15, bf16[1440,128]{1,0:T(8,128)(2,1)S(1)} %get-tuple-element.28._), custom_call_target="tpu_custom_call" | custom-call | tf_op jit(solution)/shard_map/pallas_call | solution.py:140
  4.5 0.7 shard_map.154._
  5.3 3.3 %collective-permute-start = (bf16[5760,128]{1,0:T(8,128)(2,1)S(1)}, bf16[5760,128]{1,0:T(8,128)(2,1)S(1)}, u32[]{:S(2)}, u32[]{:S(2)}) collective-permute-start(bf16[5760,128]{1,0:T(8,128)(2,1)S(1)} %shard_map.154._), channel_id=1, source_target_pairs={{0,32},{32,0},{64,96},{96,64},{128,160},{160,128},{192,224},{224,1... | collective-permute-start | bytes 4423688 | tf_op jit(solution)/shard_map/ppermute | solution.py:161
  8.6 0.1 collective-permute-start.6
  8.7 0.9 %shard_map.155 = (bf16[2592,128]{1,0:T(8,128)(2,1)S(1)}, bf16[2592,128]{1,0:T(8,128)(2,1)S(1)}) custom-call(bf16[576,4608]{1,0:T(8,128)(2,1)S(1)} %bitcast.11, bf16[8,72,512]{2,1,0:T(8,128)(2,1)S(1)} %bitcast.17, bf16[5760,128]{1,0:T(8,128)(2,1)S(1)} %shard_map.154._), custom_call_target="tpu_custom_call" | custom-call | tf_op jit(solution)/shard_map/pallas_call | solution.py:140
  9.6 0.5 collective-permute-start.5
  10.1 0.1 collective-permute-start.8
  10.2 0.7 shard_map.156.refs_0_
  11.0 1.0 %collective-permute-done.6 = bf16[1440,128]{1,0:T(8,128)(2,1)S(1)} collective-permute-done((bf16[1440,128]{1,0:T(8,128)(2,1)S(1)}, bf16[1440,128]{1,0:T(8,128)(2,1)S(1)}, u32[]{:S(2)}, u32[]{:S(2)}) %collective-permute-start.6) | collective-permute-done | bytes 368672 | tf_op jit(solution)/shard_map/ppermute | solution.py:161
  12.0 0.1 add_convert_fusion.1
  12.1 0.1 collective-permute-start.7
  12.2 1.4 %collective-permute-done.8 = bf16[1728,128]{1,0:T(8,128)(2,1)S(1)} collective-permute-done((bf16[1728,128]{1,0:T(8,128)(2,1)S(1)}, bf16[1728,128]{1,0:T(8,128)(2,1)S(1)}, u32[]{:S(2)}, u32[]{:S(2)}) %collective-permute-start.8) | collective-permute-done | bytes 442400 | tf_op jit(solution)/shard_map/ppermute | solution.py:161
  13.6 0.1 add_convert_fusion
  13.7 1.1 %collective-permute-start.9 = (bf16[1440,128]{1,0:T(8,128)(2,1)S(1)}, bf16[1440,128]{1,0:T(8,128)(2,1)S(1)}, u32[]{:S(2)}, u32[]{:S(2)}) collective-permute-start(bf16[1440,128]{1,0:T(8,128)(2,1)S(1)} %add_convert_fusion), channel_id=1, source_target_pairs={{0,192},{32,224},{64,128},{96,160},{128,64},{160,96},{192,0},{224,... | collective-permute-start | bytes 1105928 | tf_op jit(solution)/shard_map/ppermute | solution.py:161
  14.8 0.0 collective-permute-done.refs_1_
  14.8 0.2 add_convert_fusion.2
  15.0 0.0 copy-start.4
  15.0 0.1 collective-permute-start.1
  15.1 1.7 %collective-permute-start.2 = (bf16[1440,128]{1,0:T(8,128)(2,1)S(1)}, bf16[1440,128]{1,0:T(8,128)(2,1)S(1)}, u32[]{:S(2)}, u32[]{:S(2)}) collective-permute-start(bf16[1440,128]{1,0:T(8,128)(2,1)S(1)} %get-tuple-element.50), channel_id=1, source_target_pairs={{0,192},{32,224},{64,128},{96,160},{128,64},{160,96},{192,0},{224,... | collective-permute-start | bytes 1105928 | tf_op jit(solution)/shard_map/ppermute | solution.py:161
  16.8 0.0 collective-permute-done.5.refs_1_.other_ref
  16.8 5.1 %collective-permute-done.7.refs_2_.first_a = bf16[1440,128]{1,0:T(8,128)(2,1)S(1)} collective-permute-done((bf16[1440,128]{1,0:T(8,128)(2,1)S(1)}, bf16[1440,128]{1,0:T(8,128)(2,1)S(1)}, u32[]{:S(2)}, u32[]{:S(2)}) %collective-permute-start.7) | collective-permute-done | bytes 368672 | tf_op jit(solution)/shard_map/ppermute | solution.py:161
  22.0 2.8 %collective-permute-done.9.refs_3_.first_b = bf16[1440,128]{1,0:T(8,128)(2,1)S(1)} collective-permute-done((bf16[1440,128]{1,0:T(8,128)(2,1)S(1)}, bf16[1440,128]{1,0:T(8,128)(2,1)S(1)}, u32[]{:S(2)}, u32[]{:S(2)}) %collective-permute-start.9) | collective-permute-done | bytes 368672 | tf_op jit(solution)/shard_map/ppermute | solution.py:161
  24.8 0.1 add_convert_fusion.6
  24.9 1.1 %collective-permute-start.10 = (bf16[576,128]{1,0:T(8,128)(2,1)S(1)}, bf16[576,128]{1,0:T(8,128)(2,1)S(1)}, u32[]{:S(2)}, u32[]{:S(2)}) collective-permute-start(bf16[576,128]{1,0:T(8,128)(2,1)S(1)} %get-tuple-element.53), channel_id=1, source_target_pairs={{0,192},{32,224},{64,128},{96,160},{128,64},{160,96},{192,0},{224,... | collective-permute-start | bytes 442376 | tf_op jit(solution)/shard_map/ppermute | solution.py:161
  26.0 0.0 collective-permute-start.11
  26.0 3.9 %collective-permute-done.1.refs_2_ = bf16[1440,128]{1,0:T(8,128)(2,1)S(1)} collective-permute-done((bf16[1440,128]{1,0:T(8,128)(2,1)S(1)}, bf16[1440,128]{1,0:T(8,128)(2,1)S(1)}, u32[]{:S(2)}, u32[]{:S(2)}) %collective-permute-start.1) | collective-permute-done | bytes 368672 | tf_op jit(solution)/shard_map/ppermute | solution.py:161
  29.9 2.8 %collective-permute-done.2.refs_3_ = bf16[1440,128]{1,0:T(8,128)(2,1)S(1)} collective-permute-done((bf16[1440,128]{1,0:T(8,128)(2,1)S(1)}, bf16[1440,128]{1,0:T(8,128)(2,1)S(1)}, u32[]{:S(2)}, u32[]{:S(2)}) %collective-permute-start.2) | collective-permute-done | bytes 368672 | tf_op jit(solution)/shard_map/ppermute | solution.py:161
  32.6 0.1 add_convert_fusion.4
  32.8 0.0 copy-start.2
  32.8 1.1 %collective-permute-start.3 = (bf16[720,128]{1,0:T(8,128)(2,1)S(1)}, bf16[720,128]{1,0:T(8,128)(2,1)S(1)}, u32[]{:S(2)}, u32[]{:S(2)}) collective-permute-start(bf16[720,128]{1,0:T(8,128)(2,1)S(1)} %get-tuple-element.49), channel_id=1, source_target_pairs={{0,192},{32,224},{64,128},{96,160},{128,64},{160,96},{192,0},{224,... | collective-permute-start | bytes 552968 | tf_op jit(solution)/shard_map/ppermute | solution.py:161
  33.9 0.0 collective-permute-start.4
  34.0 2.9 %collective-permute-start.12 = (bf16[288,128]{1,0:T(8,128)(2,1)S(1)}, bf16[288,128]{1,0:T(8,128)(2,1)S(1)}, u32[]{:S(2)}, u32[]{:S(2)}) collective-permute-start(bf16[288,128]{1,0:T(8,128)(2,1)S(1)} %add_convert_fusion.8), channel_id=1, source_target_pairs={{0,128},{32,160},{64,192},{96,224},{128,0},{160,32},{192,64},{224,... | collective-permute-start | bytes 221192 | tf_op jit(solution)/shard_map/ppermute | solution.py:161
  36.9 3.7 %collective-permute-done.12.across_ref = bf16[288,128]{1,0:T(8,128)(2,1)S(1)} collective-permute-done((bf16[288,128]{1,0:T(8,128)(2,1)S(1)}, bf16[288,128]{1,0:T(8,128)(2,1)S(1)}, u32[]{:S(2)}, u32[]{:S(2)}) %collective-permute-start.12) | collective-permute-done | bytes 73760 | tf_op jit(solution)/shard_map/ppermute | solution.py:161
  40.6 0.0 copy-done.4
  40.6 0.1 query.1
  40.7 0.2 collective-permute-start.13
  40.8 2.7 %collective-permute-done.13 = f32[8,128]{1,0:T(8,128)S(1)} collective-permute-done((f32[8,128]{1,0:T(8,128)S(1)}, f32[8,128]{1,0:T(8,128)S(1)}, u32[]{:S(2)}, u32[]{:S(2)}) %collective-permute-start.13) | collective-permute-done | bytes 4128 | tf_op jit(solution)/shard_map/ppermute | solution.py:161
  43.5 1.5 %collective-permute-start.14 = (f32[8,128]{1,0:T(8,128)S(1)}, f32[8,128]{1,0:T(8,128)S(1)}, u32[]{:S(2)}, u32[]{:S(2)}) collective-permute-start(f32[8,128]{1,0:T(8,128)S(1)} %add.61), channel_id=1, source_target_pairs={{0,2},{1,3},{2,0},{3,1},{4,6},{5,7},{6,4},{7,5},{8,10},{9,11},{10,... | collective-permute-start | bytes 12296 | tf_op jit(solution)/shard_map/ppermute | solution.py:161
  45.0 1.8 %collective-permute-done.14 = f32[8,128]{1,0:T(8,128)S(1)} collective-permute-done((f32[8,128]{1,0:T(8,128)S(1)}, f32[8,128]{1,0:T(8,128)S(1)}, u32[]{:S(2)}, u32[]{:S(2)}) %collective-permute-start.14) | collective-permute-done | bytes 4128 | tf_op jit(solution)/shard_map/ppermute | solution.py:161
  46.9 4.0 %collective-permute-start.15 = (f32[8,128]{1,0:T(8,128)S(1)}, f32[8,128]{1,0:T(8,128)S(1)}, u32[]{:S(2)}, u32[]{:S(2)}) collective-permute-start(f32[8,128]{1,0:T(8,128)S(1)} %add.62), channel_id=1, source_target_pairs={{0,7},{1,6},{2,5},{3,4},{4,3},{5,2},{6,1},{7,0},{8,15},{9,14},{10,... | collective-permute-start | bytes 12296 | tf_op jit(solution)/shard_map/ppermute | solution.py:161
  50.9 1.0 %collective-permute-done.15 = f32[8,128]{1,0:T(8,128)S(1)} collective-permute-done((f32[8,128]{1,0:T(8,128)S(1)}, f32[8,128]{1,0:T(8,128)S(1)}, u32[]{:S(2)}, u32[]{:S(2)}) %collective-permute-start.15) | collective-permute-done | bytes 4128 | tf_op jit(solution)/shard_map/ppermute | solution.py:161
  51.9 0.0 collective-permute-done.10.refs_4_
  51.9 0.0 collective-permute-done.11.refs_5_
  51.9 0.0 copy-done.2
  51.9 0.3 shard_map.157
  52.2 0.0 collective-permute-done.3.refs_4_
  52.2 0.0 collective-permute-done.4.refs_5_
  52.2 0.0 copy-start.7
  52.3 1.1 %shard_map.158 = (f32[576,576]{1,0:T(8,128)S(1)}, f32[32,8,128]{2,1,0:T(8,128)}) custom-call(bf16[5760,128]{1,0:T(8,128)(2,1)S(1)} %shard_map.156.refs_0_, bf16[5760,128]{1,0:T(8,128)(2,1)S(1)} %collective-permute-done.refs_1_, bf16[1440,128]{1,0:T(8,128)(2,1)S(1)} %collective-permute-done.1.refs_2_, ...), custom_call_target="tpu_custom_call", output_to_operand_aliasing={{0}: (7, {})} | custom-call | tf_op jit(solution)/shard_map/pallas_call | solution.py:303
  53.4 0.0 copy-start.3
  53.4 13.1 %all-to-all-start = ((f32[32,8,128]{2,1,0:T(8,128)}), f32[32,8,128]{2,1,0:T(8,128)S(1)}, u32[]{:S(2)}, u32[]{:S(2)}) async-start(f32[32,8,128]{2,1,0:T(8,128)} %get-tuple-element.37), calls=%async_computation | async-start | bytes 262144 | tf_op jit(solution)/shard_map/all_to_all | solution.py:430
  67.2 0.0 copy-done.7
  67.3 0.1 maximum_bitcast_fusion.keep_ref
  67.3 1.2 %store.1 = (f32[576,576]{1,0:T(8,128)}, f32[72,512]{1,0:T(8,128)}) custom-call(f32[576,576]{1,0:T(8,128)S(1)} %get-tuple-element.38.new_ref, f32[72,512]{1,0:T(8,128)S(1)} %get-tuple-element.39.query_new_ref), custom_call_target="tpu_custom_call" | custom-call | tf_op jit(solution)/shard_map/store/pallas_call | solution.py:431
  68.5 5.6 %all-to-all-done.got_ref = f32[32,8,128]{2,1,0:T(8,128)S(1)} async-done(((f32[32,8,128]{2,1,0:T(8,128)}), f32[32,8,128]{2,1,0:T(8,128)S(1)}, u32[]{:S(2)}, u32[]{:S(2)}) %all-to-all-start) | async-done | bytes 131104 | tf_op jit(solution)/shard_map/all_to_all | solution.py:430
  74.1 0.0 copy-done.3
  74.1 0.0 copy-done.5
  74.1 0.0 copy-done.6
  74.1 1.8 %finish.1 = (f32[576,576]{1,0:T(8,128)}, bf16[576,576]{1,0:T(8,128)(2,1)}, f32[576]{0:T(1024)}, f32[72,512]{1,0:T(8,128)}, bf16[72,512]{1,0:T(8,128)(2,1)}, /*index=5*/f32[1,4]{1,0:T(1,128)}) custom-call(f32[1,2]{1,0:T(1,128)S(1)} %maximum_bitcast_fusion.keep_ref, f32[32,8,128]{2,1,0:T(8,128)S(1)} %all-to-all-done.got_ref, ...), custom_call_target="tpu_custom_call" | custom-call | tf_op jit(solution)/shard_map/finish/pallas_call | solution.py:441
  (7 shorter events, 0.0 us)
Async XLA Ops:
  0.6 2.9 %copy-start = (bf16[1,4608,576]{1,2,0:T(8,128)(2,1)S(1)}, bf16[1,4608,576]{1,2,0:T(8,128)(2,1)}, u32[]{:S(2)}) copy-start(bf16[1,4608,576]{1,2,0:T(8,128)(2,1)} %param.9) | copy-start | bytes 15925252
  0.6 3.0 %copy-start.1 = (bf16[1,576,512]{2,1,0:T(8,128)(2,1)S(1)}, bf16[1,576,512]{2,1,0:T(8,128)(2,1)}, u32[]{:S(2)}) copy-start(bf16[1,576,512]{2,1,0:T(8,128)(2,1)} %param.10) | copy-start | bytes 1769476
  5.3 9.5 %collective-permute-start = (bf16[5760,128]{1,0:T(8,128)(2,1)S(1)}, bf16[5760,128]{1,0:T(8,128)(2,1)S(1)}, u32[]{:S(2)}, u32[]{:S(2)}) collective-permute-start(bf16[5760,128]{1,0:T(8,128)(2,1)S(1)} %shard_map.154._), channel_id=1, source_target_pairs={{0,32},{32,0},{64,96},{96,64},{128,160},{160,128},{192,224},{224,1... | collective-permute-start | bytes 4423688 | tf_op jit(solution)/shard_map/ppermute | solution.py:161
  8.6 3.4 %collective-permute-start.6 = (bf16[1440,128]{1,0:T(8,128)(2,1)S(1)}, bf16[1440,128]{1,0:T(8,128)(2,1)S(1)}, u32[]{:S(2)}, u32[]{:S(2)}) collective-permute-start(bf16[1440,128]{1,0:T(8,128)(2,1)S(1)} %get-tuple-element.28._), channel_id=1, source_target_pairs={{0,32},{32,0},{64,96},{96,64},{128,160},{160,128},{192,224},{224,1... | collective-permute-start | bytes 1105928 | tf_op jit(solution)/shard_map/ppermute | solution.py:161
  9.6 7.2 %collective-permute-start.5 = (bf16[2592,128]{1,0:T(8,128)(2,1)S(1)}, bf16[2592,128]{1,0:T(8,128)(2,1)S(1)}, u32[]{:S(2)}, u32[]{:S(2)}) collective-permute-start(bf16[2592,128]{1,0:T(8,128)(2,1)S(1)} %get-tuple-element.30._), channel_id=1, source_target_pairs={{0,32},{32,0},{64,96},{96,64},{128,160},{160,128},{192,224},{224,1... | collective-permute-start | bytes 1990664 | tf_op jit(solution)/shard_map/ppermute | solution.py:161
  10.1 3.5 %collective-permute-start.8 = (bf16[1728,128]{1,0:T(8,128)(2,1)S(1)}, bf16[1728,128]{1,0:T(8,128)(2,1)S(1)}, u32[]{:S(2)}, u32[]{:S(2)}) collective-permute-start(bf16[1728,128]{1,0:T(8,128)(2,1)S(1)} %get-tuple-element.33), channel_id=1, source_target_pairs={{0,32},{32,0},{64,96},{96,64},{128,160},{160,128},{192,224},{224,1... | collective-permute-start | bytes 1327112 | tf_op jit(solution)/shard_map/ppermute | solution.py:161
  12.1 9.9 %collective-permute-start.7 = (bf16[1440,128]{1,0:T(8,128)(2,1)S(1)}, bf16[1440,128]{1,0:T(8,128)(2,1)S(1)}, u32[]{:S(2)}, u32[]{:S(2)}) collective-permute-start(bf16[1440,128]{1,0:T(8,128)(2,1)S(1)} %add_convert_fusion.1), channel_id=1, source_target_pairs={{0,64},{32,96},{64,0},{96,32},{128,192},{160,224},{192,128},{224,1... | collective-permute-start | bytes 1105928 | tf_op jit(solution)/shard_map/ppermute | solution.py:161
  13.7 11.1 %collective-permute-start.9 = (bf16[1440,128]{1,0:T(8,128)(2,1)S(1)}, bf16[1440,128]{1,0:T(8,128)(2,1)S(1)}, u32[]{:S(2)}, u32[]{:S(2)}) collective-permute-start(bf16[1440,128]{1,0:T(8,128)(2,1)S(1)} %add_convert_fusion), channel_id=1, source_target_pairs={{0,192},{32,224},{64,128},{96,160},{128,64},{160,96},{192,0},{224,... | collective-permute-start | bytes 1105928 | tf_op jit(solution)/shard_map/ppermute | solution.py:161
  15.0 25.6 %copy-start.4 = (f32[72,512]{1,0:T(8,128)S(1)}, f32[72,512]{1,0:T(8,128)}, u32[]{:S(2)}) copy-start(f32[72,512]{1,0:T(8,128)} %moment_ref.1) | copy-start | bytes 442372
  15.0 14.9 %collective-permute-start.1 = (bf16[1440,128]{1,0:T(8,128)(2,1)S(1)}, bf16[1440,128]{1,0:T(8,128)(2,1)S(1)}, u32[]{:S(2)}, u32[]{:S(2)}) collective-permute-start(bf16[1440,128]{1,0:T(8,128)(2,1)S(1)} %get-tuple-element.51), channel_id=1, source_target_pairs={{0,64},{32,96},{64,0},{96,32},{128,192},{160,224},{192,128},{224,1... | collective-permute-start | bytes 1105928 | tf_op jit(solution)/shard_map/ppermute | solution.py:161
  15.1 17.5 %collective-permute-start.2 = (bf16[1440,128]{1,0:T(8,128)(2,1)S(1)}, bf16[1440,128]{1,0:T(8,128)(2,1)S(1)}, u32[]{:S(2)}, u32[]{:S(2)}) collective-permute-start(bf16[1440,128]{1,0:T(8,128)(2,1)S(1)} %get-tuple-element.50), channel_id=1, source_target_pairs={{0,192},{32,224},{64,128},{96,160},{128,64},{160,96},{192,0},{224,... | collective-permute-start | bytes 1105928 | tf_op jit(solution)/shard_map/ppermute | solution.py:161
  24.9 27.0 %collective-permute-start.10 = (bf16[576,128]{1,0:T(8,128)(2,1)S(1)}, bf16[576,128]{1,0:T(8,128)(2,1)S(1)}, u32[]{:S(2)}, u32[]{:S(2)}) collective-permute-start(bf16[576,128]{1,0:T(8,128)(2,1)S(1)} %get-tuple-element.53), channel_id=1, source_target_pairs={{0,192},{32,224},{64,128},{96,160},{128,64},{160,96},{192,0},{224,... | collective-permute-start | bytes 442376 | tf_op jit(solution)/shard_map/ppermute | solution.py:161
  26.0 25.9 %collective-permute-start.11 = (bf16[576,128]{1,0:T(8,128)(2,1)S(1)}, bf16[576,128]{1,0:T(8,128)(2,1)S(1)}, u32[]{:S(2)}, u32[]{:S(2)}) collective-permute-start(bf16[576,128]{1,0:T(8,128)(2,1)S(1)} %get-tuple-element.52), channel_id=1, source_target_pairs={{0,64},{32,96},{64,0},{96,32},{128,192},{160,224},{192,128},{224,1... | collective-permute-start | bytes 442376 | tf_op jit(solution)/shard_map/ppermute | solution.py:161
  32.8 19.1 %copy-start.2 = (f32[576,576]{1,0:T(8,128)S(1)}, f32[576,576]{1,0:T(8,128)}, u32[]{:S(2)}) copy-start(f32[576,576]{1,0:T(8,128)} %refs_6_.3) | copy-start | bytes 3981316
  32.8 19.4 %collective-permute-start.3 = (bf16[720,128]{1,0:T(8,128)(2,1)S(1)}, bf16[720,128]{1,0:T(8,128)(2,1)S(1)}, u32[]{:S(2)}, u32[]{:S(2)}) collective-permute-start(bf16[720,128]{1,0:T(8,128)(2,1)S(1)} %get-tuple-element.49), channel_id=1, source_target_pairs={{0,192},{32,224},{64,128},{96,160},{128,64},{160,96},{192,0},{224,... | collective-permute-start | bytes 552968 | tf_op jit(solution)/shard_map/ppermute | solution.py:161
  33.9 18.3 %collective-permute-start.4 = (bf16[720,128]{1,0:T(8,128)(2,1)S(1)}, bf16[720,128]{1,0:T(8,128)(2,1)S(1)}, u32[]{:S(2)}, u32[]{:S(2)}) collective-permute-start(bf16[720,128]{1,0:T(8,128)(2,1)S(1)} %get-tuple-element.48), channel_id=1, source_target_pairs={{0,64},{32,96},{64,0},{96,32},{128,192},{160,224},{192,128},{224,1... | collective-permute-start | bytes 552968 | tf_op jit(solution)/shard_map/ppermute | solution.py:161
  34.0 6.6 %collective-permute-start.12 = (bf16[288,128]{1,0:T(8,128)(2,1)S(1)}, bf16[288,128]{1,0:T(8,128)(2,1)S(1)}, u32[]{:S(2)}, u32[]{:S(2)}) collective-permute-start(bf16[288,128]{1,0:T(8,128)(2,1)S(1)} %add_convert_fusion.8), channel_id=1, source_target_pairs={{0,128},{32,160},{64,192},{96,224},{128,0},{160,32},{192,64},{224,... | collective-permute-start | bytes 221192 | tf_op jit(solution)/shard_map/ppermute | solution.py:161
  40.7 2.8 %collective-permute-start.13 = (f32[8,128]{1,0:T(8,128)S(1)}, f32[8,128]{1,0:T(8,128)S(1)}, u32[]{:S(2)}, u32[]{:S(2)}) collective-permute-start(f32[8,128]{1,0:T(8,128)S(1)} %get-tuple-element.36), channel_id=1, source_target_pairs={{0,1},{1,0},{2,3},{3,2},{4,5},{5,4},{6,7},{7,6},{8,9},{9,8},{10,11... | collective-permute-start | bytes 12296 | tf_op jit(solution)/shard_map/ppermute | solution.py:161
  43.5 3.4 %collective-permute-start.14 = (f32[8,128]{1,0:T(8,128)S(1)}, f32[8,128]{1,0:T(8,128)S(1)}, u32[]{:S(2)}, u32[]{:S(2)}) collective-permute-start(f32[8,128]{1,0:T(8,128)S(1)} %add.61), channel_id=1, source_target_pairs={{0,2},{1,3},{2,0},{3,1},{4,6},{5,7},{6,4},{7,5},{8,10},{9,11},{10,... | collective-permute-start | bytes 12296 | tf_op jit(solution)/shard_map/ppermute | solution.py:161
  46.9 5.0 %collective-permute-start.15 = (f32[8,128]{1,0:T(8,128)S(1)}, f32[8,128]{1,0:T(8,128)S(1)}, u32[]{:S(2)}, u32[]{:S(2)}) collective-permute-start(f32[8,128]{1,0:T(8,128)S(1)} %add.62), channel_id=1, source_target_pairs={{0,7},{1,6},{2,5},{3,4},{4,3},{5,2},{6,1},{7,0},{8,15},{9,14},{10,... | collective-permute-start | bytes 12296 | tf_op jit(solution)/shard_map/ppermute | solution.py:161
  52.2 15.0 %copy-start.7 = (f32[576]{0:T(1024)S(1)}, f32[576]{0:T(1024)}, u32[]{:S(2)}) copy-start(f32[576]{0:T(1024)} %param.13) | copy-start | bytes 6916
  53.4 20.8 %copy-start.3 = (f32[576,576]{1,0:T(8,128)S(1)}, f32[576,576]{1,0:T(8,128)}, u32[]{:S(2)}) copy-start(f32[576,576]{1,0:T(8,128)} %param_ref.1) | copy-start | bytes 3981316
  53.4 20.8 %copy-start.5 = (f32[72,512]{1,0:T(8,128)S(1)}, f32[72,512]{1,0:T(8,128)}, u32[]{:S(2)}) copy-start(f32[72,512]{1,0:T(8,128)} %query_param_ref.1) | copy-start | bytes 442372
  53.4 20.8 %copy-start.6 = (f32[4]{0:T(128)S(1)}, f32[4]{0:T(128)}, u32[]{:S(2)}) copy-start(f32[4]{0:T(128)} %param.16) | copy-start | bytes 52
  53.4 20.7 %all-to-all-start = ((f32[32,8,128]{2,1,0:T(8,128)}), f32[32,8,128]{2,1,0:T(8,128)S(1)}, u32[]{:S(2)}, u32[]{:S(2)}) async-start(f32[32,8,128]{2,1,0:T(8,128)} %get-tuple-element.37), calls=%async_computation | async-start | bytes 262144 | tf_op jit(solution)/shard_map/all_to_all | solution.py:430

commit v4 on v3

v4 whole, which is shorter than its diff:
```python
import jax
import jax.numpy as jnp
from jax import lax
from jax.experimental import pallas as pl
from jax.experimental.pallas import tpu as pltpu
from jax.sharding import PartitionSpec as P

D = 4608
HEAD_DIM = 128
FF = 18432

BETA_ONE = 0.9
BETA_TWO = 0.95
EPSILON = 1e-08
LEARN_RATE = 0.003
DECAY_RATE = 0.1

LANES = 128
ROW_BLOCKS = 6
GROUPS = {
    "forward0": (((0, 2),), ((0, 1), (1, 1))),
    "forward1": (((1, 2),), ((0, 3), (1, 3), (0, 2), (1, 2))),
    "keep": (((0, 1), (1, 3)), ()),
    "rest": (((0, 3), (1, 1), (0, 0), (1, 0)), ((0, 0), (1, 0))),
}
ANY = pl.BlockSpec(memory_space=pl.ANY)
HBM = pl.BlockSpec(memory_space=pltpu.HBM)
VMEM = pl.BlockSpec(memory_space=pltpu.VMEM)


PARAMS = pltpu.CompilerParams(vmem_limit_bytes=8 << 20)


def pairs(size, mask):
    return [(i, i ^ mask) for i in range(size)]


def far(x):
    return pltpu.with_memory_space_constraint(x, pltpu.HBM)


def near(x):
    return pltpu.with_memory_space_constraint(x, pltpu.VMEM)


def down_rows(width):
    return 2 * width + width // 4


def query_rows(query_chunks):
    return query_chunks.shape[1] * query_chunks.shape[2] // (2 * LANES)


def pack(parts, columns, query_chunks, after, place):
    q_rows, q_cols = query_chunks.shape[1:]
    q_wide = q_cols // LANES // 2
    width = columns.shape[0]
    quarter = width // 4
    block, query = down_rows(width), query_rows(query_chunks)
    span = columns.shape[1] // 4

    def kernel(down_ref, query_ref, _, *refs):
        outs, bufs, sems = refs[: len(parts)], refs[len(parts) : 2 * len(parts)], refs[2 * len(parts) :]
        me = lax.axis_index("dp")
        y, core = me // 2, me % 2
        shared, whole = [], []

        def put(copies, source, target, semaphore):
            if place is far:
                copies.append(pltpu.make_async_copy(source, target, semaphore))
            else:
                target[...] = source[...]

        for (group, mine), out, buf, sem in zip(parts, outs, bufs, sems):
            downs, queries = GROUPS[group]
            owner = core if mine else 1 - core
            for at, (half, d) in enumerate(downs):
                lane = pl.multiple_of(span * (y ^ d) + 4 * LANES, LANES)
                source = down_ref.at[pl.ds(half * 2 * quarter, 2 * quarter), pl.ds(lane, LANES)]
                put(shared, source, buf.at[at], sem.at[at, 0])
            for at, (half, d) in enumerate(downs):
                for j in range(2):
                    lane = pl.multiple_of(span * (y ^ d) + 5 * LANES * owner + (2 * half + j) * LANES, LANES)
                    target = out.at[pl.ds(at * block + j * (width + quarter), width), :]
                    put(whole, down_ref.at[:, pl.ds(lane, LANES)], target, sem.at[at, 1 + j])
            for at, (half, d) in enumerate(queries):
                for j in range(q_wide):
                    source = query_ref.at[2 * (y ^ d) + owner, :, pl.ds((half * q_wide + j) * LANES, LANES)]
                    target = out.at[pl.ds(len(downs) * block + at * query + j * q_rows, q_rows), :]
                    put(whole, source, target, sem.at[at, 3 + j])
        for copy in shared + whole:
            copy.start()
        for copy in shared:
            copy.wait()
        low = lax.broadcasted_iota(jnp.int32, (quarter, LANES), 1) < LANES // 2
        for (group, mine), out, buf in zip(parts, outs, bufs):
            lower = (core == 0) if mine else (core == 1)
            for at in range(len(GROUPS[group][0])):
                first = buf[at, :quarter, :].astype(jnp.float32)
                second = buf[at, quarter:, :].astype(jnp.float32)
                packed = jnp.where(
                    lower,
                    jnp.where(low, first, pltpu.roll(second, LANES // 2, 1)),
                    jnp.where(low, pltpu.roll(first, LANES // 2, 1), second),
                )
                out[pl.ds(at * block + width, quarter), :] = packed.astype(jnp.bfloat16)
        for copy in whole:
            copy.wait()

    def rows(group):
        downs, queries = GROUPS[group]
        return len(downs) * block + len(queries) * query

    return pl.pallas_call(
        kernel,
        out_shape=tuple(pltpu.VMEM((rows(group), LANES), jnp.bfloat16) for group, _ in parts),
        in_specs=[HBM, HBM, ANY] if place is far else [VMEM, VMEM, ANY],
        out_specs=(VMEM,) * len(parts),
        scratch_shapes=[pltpu.VMEM((len(GROUPS[group][0]), 2 * quarter, LANES), jnp.bfloat16) for group, _ in parts]
        + [pltpu.SemaphoreType.DMA((4, 5)) for _ in parts],
        compiler_params=PARAMS,
    )(place(columns), place(query_chunks), after)


def added(*terms):
    total = terms[0].astype(jnp.float32)
    for term in terms[1:]:
        total = total + term.astype(jnp.float32)
    return total


def sent(x, mask, axis="dp"):
    return lax.ppermute(x, axis, pairs(8, mask))


def summed(*terms):
    return added(*terms).astype(jnp.bfloat16)


def moment_new(before, grad):
    return BETA_ONE * before + (1.0 - BETA_ONE) * grad


def column_sum(x):
    return jnp.sum(x * x, axis=0, keepdims=True)


def gather_query(query, own, other, direct, query_moment):
    q_rows, q_cols = query_moment.shape
    q_wide = q_cols // LANES // 2

    def kernel(own_ref, other_ref, from_first, from_second, from_third, moment_ref, new_ref, sums_ref):
        sums_ref[...] = jnp.zeros_like(sums_ref)
        for half in range(2):
            for j in range(q_wide):
                terms = []
                for ref in (own_ref, other_ref, from_first, from_second, from_third):
                    at = ref.shape[0] - (2 - half) * query + j * q_rows
                    terms.append(ref[pl.ds(at, q_rows), :])
                grad = added(*terms) * (1.0 / 8.0)
                head = half * q_wide + j
                span = (slice(None), slice(head * LANES, (head + 1) * LANES))
                new_ref[span] = moment_new(moment_ref[span], grad)
                sums_ref[head : head + 1, :] = column_sum(grad)

    return pl.pallas_call(
        kernel,
        out_shape=(pltpu.VMEM(query_moment.shape, jnp.float32), pltpu.VMEM((8, LANES), jnp.float32)),
        in_specs=[VMEM] * 6,
        out_specs=(VMEM,) * 2,
        compiler_params=PARAMS,
        name="query",
    )(*(near(t) for t in (own, other, *direct, query_moment)))


def gather(own, other, keeps, seconds, heads, down_moment):
    _, width = down_moment.shape
    quarter = width // 4
    block = down_rows(width)
    half_tile = LANES // 2
    tensors = lax.axis_size("tensor")

    def kernel(own_ref, other_ref, keep0, keep1, second0, second1, heads_ref, moment_ref, new_ref, message_ref):
        core = lax.axis_index("dp") % 2
        me = lax.axis_index("tensor")

        def mean(half, at, count):
            kept = (2 + half) * block + at
            return added(
                own_ref[pl.ds(kept, count), :],
                other_ref[pl.ds(kept, count), :],
                (keep0, keep1)[half][pl.ds(at, count), :],
                (second0, second1)[half][pl.ds(at, count), :],
            ) * (1.0 / 8.0)

        parts = []
        for half in range(2):
            packed = mean(half, width, quarter)
            parts += [packed, pltpu.roll(packed, half_tile, 1)]
        rest = jnp.concatenate(parts, axis=0)
        row = lax.broadcasted_iota(jnp.int32, (8, LANES), 0)
        lane = lax.broadcasted_iota(jnp.int32, (8, LANES), 1)
        neurons = jnp.zeros((8, LANES), jnp.float32)
        for c in range(0, width, LANES):
            step = min(LANES, width - c)
            span = slice(c, c + step)
            total = jnp.zeros((1, step), jnp.float32)
            for tile in range(4):
                grad = mean(tile // 2, (tile % 2) * (width + quarter) + c, step).T
                at = (pl.ds(pl.multiple_of(half_tile * core + tile * LANES, half_tile), LANES), span)
                new_ref[at] = moment_new(moment_ref[at], grad)
                total += column_sum(grad)
            grad = rest[c : c + step].T[:half_tile]
            at = (pl.ds(pl.multiple_of(4 * LANES * (1 - core), half_tile), half_tile), span)
            new_ref[at] = moment_new(moment_ref[at], grad)
            total += column_sum(grad)
            if step < LANES:
                total = jnp.pad(total, ((0, 0), (0, LANES - step)))
            neurons += jnp.where(row == c // LANES, total, 0.0)
        sums = jnp.sum(heads_ref[...], axis=1, keepdims=True)
        spread = jnp.sum(jnp.where(row == lane, sums, 0.0), axis=0, keepdims=True)
        mine = neurons + jnp.where(row == 5, spread, 0.0)
        for target in range(message_ref.shape[0]):
            message_ref[target] = jnp.where(me == target % tensors, mine, neurons)

    return pl.pallas_call(
        kernel,
        out_shape=(
            pltpu.VMEM(down_moment.shape, jnp.float32),
            pltpu.VMEM((lax.axis_size("dp") * tensors, 8, LANES), jnp.float32),
        ),
        in_specs=[VMEM] * 8,
        out_specs=(VMEM,) * 2,
        compiler_params=PARAMS,
        name="gather",
    )(*(near(t) for t in (own, other, *keeps, *seconds, heads, down_moment)))


def store_kernel(new_ref, query_new_ref, moment_out, query_moment_out, sems):
    copies = (
        pltpu.make_async_copy(new_ref, moment_out, sems.at[0]),
        pltpu.make_async_copy(query_new_ref, query_moment_out, sems.at[1]),
    )
    for copy in copies:
        copy.start()
    for copy in copies:
        copy.wait()


def finish_kernel(
    keep_ref, got_ref, new_ref, param_ref, second_ref, query_new_ref, query_param_ref, query_second_ref,
    param_out, update_out, second_out, query_param_out, query_update_out, query_second_out,
    param_buf, update_buf, second_buf, query_param_buf, query_update_buf, query_second_buf, sems, query_sems, second_sems,
):
    keep_one, keep_two = keep_ref[:, 0:1], keep_ref[:, 1:2]
    total = jnp.sum(got_ref[...], axis=0)

    def second_new(before, mean):
        return BETA_TWO * before + (1.0 - BETA_TWO) * mean

    def factor(second):
        return 1.0 / (keep_one * (jnp.sqrt(second / keep_two) + EPSILON))

    def write(at, scale, new, param, update_to, param_to):
        old = param[at]
        update = new[at] * scale
        update_to[at] = update.astype(jnp.bfloat16)
        param_to[at] = old - LEARN_RATE * (update + DECAY_RATE * old)

    rows, cols = new_ref.shape
    spans = [slice(k, min(k + LANES, cols)) for k in range(0, cols, LANES)]
    factors = []
    for k, span in enumerate(spans):
        second = second_new(second_ref[:, span], total[k : k + 1, : span.stop - span.start] * (1.0 / FF))
        second_buf[span] = second[0]
        factors.append(factor(second))
    copies = [pltpu.make_async_copy(second_buf, second_out, second_sems.at[0])]
    copies[-1].start()
    block = rows // ROW_BLOCKS
    for b in range(ROW_BLOCKS):
        part = slice(b * block, (b + 1) * block)
        for span, scale in zip(spans, factors):
            write((part, span), scale, new_ref, param_ref, update_buf, param_buf)
        copies.append(pltpu.make_async_copy(param_buf.at[part], param_out.at[part], sems.at[0, b]))
        copies.append(pltpu.make_async_copy(update_buf.at[part], update_out.at[part], sems.at[1, b]))
        copies[-2].start()
        copies[-1].start()
    heads = query_new_ref.shape[1] // HEAD_DIM
    for head in range(heads):
        mean = total[5:6, head : head + 1] * (1.0 / (D * HEAD_DIM))
        second = second_new(query_second_ref[:, head : head + 1], mean)
        query_second_buf[:, head : head + 1] = second
        span = slice(head * HEAD_DIM, (head + 1) * HEAD_DIM)
        write((slice(None), span), factor(second), query_new_ref, query_param_ref, query_update_buf, query_param_buf)
    copies.append(pltpu.make_async_copy(query_param_buf, query_param_out, query_sems.at[0]))
    copies.append(pltpu.make_async_copy(query_update_buf, query_update_out, query_sems.at[1]))
    copies.append(pltpu.make_async_copy(query_second_buf, query_second_out, second_sems.at[1]))
    for copy in copies[-3:]:
        copy.start()
    for copy in copies:
        copy.wait()


def shards(
    grad_down,
    grad_query,
    down_param,
    down_moment,
    down_second,
    query_param,
    query_moment,
    query_second,
    step_count,
):
    replicas = lax.axis_size("dp")
    step_value = step_count[0].astype(jnp.float32)
    keep = jnp.stack(
        [1.0 - jnp.power(jnp.float32(BETA_ONE), step_value), 1.0 - jnp.power(jnp.float32(BETA_TWO), step_value)]
    )
    columns = grad_down[0].T
    query_chunks = grad_query[0].reshape(replicas, -1, grad_query.shape[2])
    width = columns.shape[0]
    block, query = down_rows(width), query_rows(query_chunks)

    def packed(after, place, *parts):
        return pack(parts, columns, query_chunks, after, place)

    def other_core(x):
        return sent(x, 1)

    to_first, to_second = (2, 6), (6, 2)
    sends = packed(query_chunks, far, ("forward0", False), ("forward1", False))
    others = [other_core(sends[half]) for half in range(2)]
    owns = packed(sends[0], near, ("forward0", True), ("forward1", True))
    ends = [block + 2 * query] * 2
    forwards = [summed(owns[half][: ends[half]], others[half][: ends[half]]) for half in range(2)]
    across = summed(owns[1][ends[1] :], others[1][ends[1] :])
    forwards = [sent(forwards[half], to_first[half]) for half in range(2)]
    across = sent(across, 4)
    keep_send, keep_own = packed(owns[0], near, ("keep", False), ("keep", True))
    keep_other = other_core(keep_send)
    send, own = packed(keep_own, near, ("rest", False), ("rest", True))
    other = other_core(send)
    keeps = []
    for half in range(2):
        part = slice(half * block, (half + 1) * block)
        keeps.append(summed(keep_own[part], keep_other[part]))
    keeps = [sent(keeps[half], to_first[half]) for half in range(2)]
    seconds = []
    for half in range(2):
        part = slice(half * block, (half + 1) * block)
        seconds.append(summed(own[part], other[part], forwards[half][:block]))
    seconds = [sent(seconds[half], to_second[half]) for half in range(2)]
    query_new, heads = gather_query(query, own, other, (*forwards, across), query_moment)
    for mask in (1, 2, 7):
        heads = heads + sent(heads, mask, "ctx")
    new, message = gather(own, other, keeps, seconds, heads, down_moment)
    got = lax.all_to_all(message, ("dp", "tensor"), split_axis=0, concat_axis=0, tiled=True)
    down_moment_new, query_moment_new = pl.pallas_call(
        store_kernel,
        out_shape=tuple(pltpu.HBM(x.shape, jnp.float32) for x in (new, query_new)),
        in_specs=[VMEM, VMEM],
        out_specs=(HBM, HBM),
        scratch_shapes=[pltpu.SemaphoreType.DMA((2,))],
        compiler_params=PARAMS,
        name="store",
    )(near(new), near(query_new))
    f32, bf16 = jnp.float32, jnp.bfloat16
    outs = pl.pallas_call(
        finish_kernel,
        out_shape=(
            pltpu.HBM(down_param.shape, f32),
            pltpu.HBM(down_param.shape, bf16),
            pltpu.HBM(down_second.shape, f32),
            pltpu.HBM(query_param.shape, f32),
            pltpu.HBM(query_param.shape, bf16),
            pltpu.HBM((1, query_second.shape[0]), f32),
        ),
        in_specs=[VMEM] * 8,
        out_specs=(HBM,) * 6,
        scratch_shapes=[
            pltpu.VMEM(down_param.shape, f32),
            pltpu.VMEM(down_param.shape, bf16),
            pltpu.VMEM(down_second.shape, f32),
            pltpu.VMEM(query_param.shape, f32),
            pltpu.VMEM(query_param.shape, bf16),
            pltpu.VMEM((1, query_second.shape[0]), f32),
            pltpu.SemaphoreType.DMA((2, ROW_BLOCKS)),
            pltpu.SemaphoreType.DMA((2,)),
            pltpu.SemaphoreType.DMA((2,)),
        ],
        compiler_params=PARAMS, name="finish",
    )(
        near(keep[None, :]), near(got), near(new), near(down_param), near(down_second[None, :]),
        near(query_new), near(query_param), near(query_second[None, :]),
    )
    down_param_new, down_update, down_second_new = outs[:3]
    query_param_new, query_update, query_second_new = outs[3:]
    return (
        down_param_new,
        down_moment_new,
        down_second_new,
        down_update,
        query_param_new,
        query_moment_new,
        query_second_new[0],
        query_update,
    )


def solution(mesh):
    in_specs = (
        P("dp", "tensor", "ctx"),
        P("dp", "ctx", "tensor"),
        P(("tensor", "dp"), "ctx"),
        P(("tensor", "dp"), "ctx"),
        P("ctx"),
        P(("ctx", "dp"), "tensor"),
        P(("ctx", "dp"), "tensor"),
        P("tensor"),
        P(),
    )
    out_specs = (
        P(("tensor", "dp"), "ctx"),
        P(("tensor", "dp"), "ctx"),
        P("ctx"),
        P(("tensor", "dp"), "ctx"),
        P(("ctx", "dp"), "tensor"),
        P(("ctx", "dp"), "tensor"),
        P("tensor"),
        P(("ctx", "dp"), "tensor"),
    )

    return jax.shard_map(shards, mesh=mesh, in_specs=in_specs, out_specs=out_specs, check_vma=False)
```

time: 76.1 us -> 69.6 us (0.915)
  waiting for transfers between devices: 31.8 us -> 28.2 us
  Pallas kernels: 9.73 us -> 8.59 us
  local copies, waits for them, and re-layouts: 1.04 us -> 0.04 us
    ppermute x16 -> x14, waiting for transfers between devices: 26.2 us -> 22.6 us  [sent(): return lax.ppermute(x, axis, pairs(8, mask))]
    all_to_all x1, starting transfers between devices: 13.1 us -> 9.54 us  [shards(): lax.all_to_all(message, ('dp', 'tensor'), split_axis=0, concat_axis=0, ti...]
    ppermute x16 -> x14, starting transfers between devices: 17.9 us -> 20.7 us  [sent(): return lax.ppermute(x, axis, pairs(8, mask))]
    pallas_call x7 -> x5, Pallas kernels: 6.68 us -> 5.54 us  [the longest x4 4.16 us: pack(): pl.pallas_call(kernel, out_shape=tuple((pltpu.VMEM((rows(group), LANES),...]
    unnamed x16, local copies, waits for them, and re-layouts: 1.04 us -> 0.04 us
  transfers between devices with their start and end apart: 17 -> 15, of which waited for: 11 -> 7; matrix products, arithmetic and copies ran while one was open for 1% -> 1% of each run, Pallas kernels for 4% -> 5%
where the time goes in v4:
time: 69.6 us; the launch traced here: 69.4 us
  starting transfers between devices  30.3 us (44%)
  waiting for transfers between devices  28.2 us (41%)
  Pallas kernels  8.59 us (12%)
  between operations  1.56 us (2%)
  other arithmetic  0.76 us (1%)
    ppermute x14, waiting for transfers between devices, sent(): return lax.ppermute(x, axis, pairs(8, mask))  22.6 us
    ppermute x14, starting transfers between devices, sent(): return lax.ppermute(x, axis, pairs(8, mask))  20.7 us
    all_to_all x1, starting transfers between devices, shards(): lax.all_to_all(message, ('dp', 'tensor'), split_axis=0, concat_axis=0, ti...  9.54 us
    all_to_all x1, waiting for transfers between devices, shards(): lax.all_to_all(message, ('dp', 'tensor'), split_axis=0, concat_axis=0, ti...  5.6 us
    pallas_call x4, Pallas kernels, pack(): pl.pallas_call(kernel, out_shape=tuple((pltpu.VMEM((rows(group), LANES),...  4.16 us
    pallas_call x1, Pallas kernels, shards(): pl.pallas_call(finish_kernel, out_shape=(pltpu.HBM(down_param.shape, f32)...  1.8 us
  transfers between devices with their start and end apart: 15, of which 7 were waited for; matrix products, arithmetic and copies ran while one was open for 1% of the time, Pallas kernels for 5%

profile of v4, /device:TPU:1, one launch (start us, length us, event | category | flops | bytes accessed | tf_op | source)
XLA Modules:
  0.0 69.4 jit_solution(7206372842928316100)
XLA Ops:
  0.6 0.0 copy-start
  0.6 0.0 copy-start.1
  0.7 1.8 %shard_map.152 = (bf16[1584,128]{1,0:T(8,128)(2,1)S(1)}, bf16[1872,128]{1,0:T(8,128)(2,1)S(1)}) custom-call(bf16[576,4608]{1,0:T(8,128)(2,1)} %bitcast.8, bf16[8,72,512]{2,1,0:T(8,128)(2,1)} %bitcast.12, bf16[8,72,512]{2,1,0:T(8,128)(2,1)} %bitcast.13), custom_call_target="tpu_custom_call" | custom-call | tf_op jit(solution)/shard_map/pallas_call | solution.py:114
  2.5 3.3 %collective-permute-start.4 = (bf16[1584,128]{1,0:T(8,128)(2,1)S(1)}, bf16[1584,128]{1,0:T(8,128)(2,1)S(1)}, u32[]{:S(2)}, u32[]{:S(2)}) collective-permute-start(bf16[1584,128]{1,0:T(8,128)(2,1)S(1)} %get-tuple-element.28._), channel_id=1, source_target_pairs={{0,32},{32,0},{64,96},{96,64},{128,160},{160,128},{192,224},{224,1... | collective-permute-start | bytes 1216520 | tf_op jit(solution)/shard_map/ppermute | solution.py:133
  5.7 0.1 collective-permute-start.7
  5.8 0.0 copy-done
  5.9 0.0 copy-done.1
  5.9 0.5 shard_map.153
  6.4 0.8 %shard_map.154 = (bf16[2592,128]{1,0:T(8,128)(2,1)S(1)}, bf16[2592,128]{1,0:T(8,128)(2,1)S(1)}) custom-call(bf16[576,4608]{1,0:T(8,128)(2,1)S(1)} %bitcast.10, bf16[8,72,512]{2,1,0:T(8,128)(2,1)S(1)} %bitcast.15, bf16[1584,128]{1,0:T(8,128)(2,1)S(1)} %get-tuple-element.29._), custom_call_target="tpu_custom_call" | custom-call | tf_op jit(solution)/shard_map/pallas_call | solution.py:114
  7.2 1.1 %collective-permute-start.1 = (bf16[2592,128]{1,0:T(8,128)(2,1)S(1)}, bf16[2592,128]{1,0:T(8,128)(2,1)S(1)}, u32[]{:S(2)}, u32[]{:S(2)}) collective-permute-start(bf16[2592,128]{1,0:T(8,128)(2,1)S(1)} %get-tuple-element.33), channel_id=1, source_target_pairs={{0,32},{32,0},{64,96},{96,64},{128,160},{160,128},{192,224},{224,1... | collective-permute-start | bytes 1990664 | tf_op jit(solution)/shard_map/ppermute | solution.py:133
  8.3 1.1 %shard_map.155 = (bf16[5472,128]{1,0:T(8,128)(2,1)S(1)}, bf16[5472,128]{1,0:T(8,128)(2,1)S(1)}) custom-call(bf16[576,4608]{1,0:T(8,128)(2,1)S(1)} %bitcast.11, bf16[8,72,512]{2,1,0:T(8,128)(2,1)S(1)} %bitcast.16, bf16[2592,128]{1,0:T(8,128)(2,1)S(1)} %get-tuple-element.30._), custom_call_target="tpu_custom_call" | custom-call | tf_op jit(solution)/shard_map/pallas_call | solution.py:114
  9.4 0.1 collective-permute-start
  9.5 0.0 collective-permute-done.4
  9.5 0.1 add_convert_fusion.1
  9.6 0.1 collective-permute-start.5
  9.7 0.0 collective-permute-done.7
  9.7 0.1 add_convert_fusion
  9.8 1.6 %collective-permute-start.8 = (bf16[1584,128]{1,0:T(8,128)(2,1)S(1)}, bf16[1584,128]{1,0:T(8,128)(2,1)S(1)}, u32[]{:S(2)}, u32[]{:S(2)}) collective-permute-start(bf16[1584,128]{1,0:T(8,128)(2,1)S(1)} %add_convert_fusion), channel_id=1, source_target_pairs={{0,192},{32,224},{64,128},{96,160},{128,64},{160,96},{192,0},{224,... | collective-permute-start | bytes 1216520 | tf_op jit(solution)/shard_map/ppermute | solution.py:133
  11.4 0.0 collective-permute-done.1
  11.4 0.2 add_convert_fusion.4
  11.6 0.0 copy-start.5
  11.6 1.3 %collective-permute-start.3 = (bf16[1296,128]{1,0:T(8,128)(2,1)S(1)}, bf16[1296,128]{1,0:T(8,128)(2,1)S(1)}, u32[]{:S(2)}, u32[]{:S(2)}) collective-permute-start(bf16[1296,128]{1,0:T(8,128)(2,1)S(1)} %get-tuple-element.50), channel_id=1, source_target_pairs={{0,192},{32,224},{64,128},{96,160},{128,64},{160,96},{192,0},{224,... | collective-permute-start | bytes 995336 | tf_op jit(solution)/shard_map/ppermute | solution.py:133
  12.9 0.2 collective-permute-start.2
  13.1 7.0 %collective-permute-done.5.from_first = bf16[1584,128]{1,0:T(8,128)(2,1)S(1)} collective-permute-done((bf16[1584,128]{1,0:T(8,128)(2,1)S(1)}, bf16[1584,128]{1,0:T(8,128)(2,1)S(1)}, u32[]{:S(2)}, u32[]{:S(2)}) %collective-permute-start.5) | collective-permute-done | bytes 405536 | tf_op jit(solution)/shard_map/ppermute | solution.py:133
  20.2 1.4 %collective-permute-done.8.from_second = bf16[1584,128]{1,0:T(8,128)(2,1)S(1)} collective-permute-done((bf16[1584,128]{1,0:T(8,128)(2,1)S(1)}, bf16[1584,128]{1,0:T(8,128)(2,1)S(1)}, u32[]{:S(2)}, u32[]{:S(2)}) %collective-permute-start.8) | collective-permute-done | bytes 405536 | tf_op jit(solution)/shard_map/ppermute | solution.py:133
  21.6 0.0 collective-permute-done.other_ref
  21.6 0.3 add_convert_fusion.2
  21.9 0.1 collective-permute-start.9
  22.0 1.3 %collective-permute-start.6 = (bf16[1296,128]{1,0:T(8,128)(2,1)S(1)}, bf16[1296,128]{1,0:T(8,128)(2,1)S(1)}, u32[]{:S(2)}, u32[]{:S(2)}) collective-permute-start(bf16[1296,128]{1,0:T(8,128)(2,1)S(1)} %get-tuple-element.49), channel_id=1, source_target_pairs={{0,192},{32,224},{64,128},{96,160},{128,64},{160,96},{192,0},{224,... | collective-permute-start | bytes 995336 | tf_op jit(solution)/shard_map/ppermute | solution.py:133
  23.3 0.0 copy-start.2
  23.3 2.1 %collective-permute-start.10 = (bf16[288,128]{1,0:T(8,128)(2,1)S(1)}, bf16[288,128]{1,0:T(8,128)(2,1)S(1)}, u32[]{:S(2)}, u32[]{:S(2)}) collective-permute-start(bf16[288,128]{1,0:T(8,128)(2,1)S(1)} %add_convert_fusion.6), channel_id=1, source_target_pairs={{0,128},{32,160},{64,192},{96,224},{128,0},{160,32},{192,64},{224,... | collective-permute-start | bytes 221192 | tf_op jit(solution)/shard_map/ppermute | solution.py:133
  25.3 11.1 %collective-permute-done.10.from_third = bf16[288,128]{1,0:T(8,128)(2,1)S(1)} collective-permute-done((bf16[288,128]{1,0:T(8,128)(2,1)S(1)}, bf16[288,128]{1,0:T(8,128)(2,1)S(1)}, u32[]{:S(2)}, u32[]{:S(2)}) %collective-permute-start.10) | collective-permute-done | bytes 73760 | tf_op jit(solution)/shard_map/ppermute | solution.py:133
  36.4 0.0 copy-done.5
  36.4 0.1 query.1
  36.5 1.7 %collective-permute-start.11 = (f32[8,128]{1,0:T(8,128)S(1)}, f32[8,128]{1,0:T(8,128)S(1)}, u32[]{:S(2)}, u32[]{:S(2)}) collective-permute-start(f32[8,128]{1,0:T(8,128)S(1)} %get-tuple-element.36), channel_id=1, source_target_pairs={{0,1},{1,0},{2,3},{3,2},{4,5},{5,4},{6,7},{7,6},{8,9},{9,8},{10,11... | collective-permute-start | bytes 12296 | tf_op jit(solution)/shard_map/ppermute | solution.py:133
  38.2 1.0 %collective-permute-done.11 = f32[8,128]{1,0:T(8,128)S(1)} collective-permute-done((f32[8,128]{1,0:T(8,128)S(1)}, f32[8,128]{1,0:T(8,128)S(1)}, u32[]{:S(2)}, u32[]{:S(2)}) %collective-permute-start.11) | collective-permute-done | bytes 4128 | tf_op jit(solution)/shard_map/ppermute | solution.py:133
  39.2 3.0 %collective-permute-start.12 = (f32[8,128]{1,0:T(8,128)S(1)}, f32[8,128]{1,0:T(8,128)S(1)}, u32[]{:S(2)}, u32[]{:S(2)}) collective-permute-start(f32[8,128]{1,0:T(8,128)S(1)} %add.45), channel_id=1, source_target_pairs={{0,2},{1,3},{2,0},{3,1},{4,6},{5,7},{6,4},{7,5},{8,10},{9,11},{10,... | collective-permute-start | bytes 12296 | tf_op jit(solution)/shard_map/ppermute | solution.py:133
  42.2 1.0 %collective-permute-done.12 = f32[8,128]{1,0:T(8,128)S(1)} collective-permute-done((f32[8,128]{1,0:T(8,128)S(1)}, f32[8,128]{1,0:T(8,128)S(1)}, u32[]{:S(2)}, u32[]{:S(2)}) %collective-permute-start.12) | collective-permute-done | bytes 4128 | tf_op jit(solution)/shard_map/ppermute | solution.py:133
  43.2 4.8 %collective-permute-start.13 = (f32[8,128]{1,0:T(8,128)S(1)}, f32[8,128]{1,0:T(8,128)S(1)}, u32[]{:S(2)}, u32[]{:S(2)}) collective-permute-start(f32[8,128]{1,0:T(8,128)S(1)} %add.46), channel_id=1, source_target_pairs={{0,7},{1,6},{2,5},{3,4},{4,3},{5,2},{6,1},{7,0},{8,15},{9,14},{10,... | collective-permute-start | bytes 12296 | tf_op jit(solution)/shard_map/ppermute | solution.py:133
  48.0 1.0 %collective-permute-done.13 = f32[8,128]{1,0:T(8,128)S(1)} collective-permute-done((f32[8,128]{1,0:T(8,128)S(1)}, f32[8,128]{1,0:T(8,128)S(1)}, u32[]{:S(2)}, u32[]{:S(2)}) %collective-permute-start.13) | collective-permute-done | bytes 4128 | tf_op jit(solution)/shard_map/ppermute | solution.py:133
  49.0 0.0 copy-start.7
  49.0 0.0 collective-permute-done.3.keep1
  49.0 0.0 collective-permute-done.2.keep0
  49.0 0.0 collective-permute-done.9.second1
  49.0 0.0 collective-permute-done.6.second0
  49.0 0.0 copy-done.2
  49.0 1.4 %gather.1 = (f32[576,576]{1,0:T(8,128)S(1)}, f32[32,8,128]{2,1,0:T(8,128)}) custom-call(bf16[5472,128]{1,0:T(8,128)(2,1)S(1)} %get-tuple-element.31.own_ref, bf16[5472,128]{1,0:T(8,128)(2,1)S(1)} %collective-permute-done.other_ref, bf16[1296,128]{1,0:T(8,128)(2,1)S(1)} %collective-permute-done.2.keep0, bf16[1296,128]{1,0:T(8,128)(2,1)S(1)} %collective-permute-done.3.keep1, ...), custom_call_target="tpu_custom_call" | custom-call | tf_op jit(solution)/shard_map/gather/pallas_call | solution.py:226
  50.4 0.0 copy-start.3
  50.4 0.0 copy-start.4
  50.4 0.0 copy-start.6
  50.4 9.5 %all-to-all-start = ((f32[32,8,128]{2,1,0:T(8,128)}), f32[32,8,128]{2,1,0:T(8,128)S(1)}, u32[]{:S(2)}, u32[]{:S(2)}) async-start(f32[32,8,128]{2,1,0:T(8,128)} %get-tuple-element.37), calls=%async_computation | async-start | bytes 262144 | tf_op jit(solution)/shard_map/all_to_all | solution.py:358
  60.7 0.0 copy-done.7
  60.7 0.1 maximum_bitcast_fusion.keep_ref
  60.8 1.2 %store.1 = (f32[576,576]{1,0:T(8,128)}, f32[72,512]{1,0:T(8,128)}) custom-call(f32[576,576]{1,0:T(8,128)S(1)} %get-tuple-element.38.new_ref, f32[72,512]{1,0:T(8,128)S(1)} %get-tuple-element.39.query_new_ref), custom_call_target="tpu_custom_call" | custom-call | tf_op jit(solution)/shard_map/store/pallas_call | solution.py:359
  62.0 5.6 %all-to-all-done.got_ref = f32[32,8,128]{2,1,0:T(8,128)S(1)} async-done(((f32[32,8,128]{2,1,0:T(8,128)}), f32[32,8,128]{2,1,0:T(8,128)S(1)}, u32[]{:S(2)}, u32[]{:S(2)}) %all-to-all-start) | async-done | bytes 131104 | tf_op jit(solution)/shard_map/all_to_all | solution.py:358
  67.6 0.0 copy-done.3
  67.6 0.0 copy-done.4
  67.6 0.0 copy-done.6
  67.6 1.8 %finish.1 = (f32[576,576]{1,0:T(8,128)}, bf16[576,576]{1,0:T(8,128)(2,1)}, f32[576]{0:T(1024)}, f32[72,512]{1,0:T(8,128)}, bf16[72,512]{1,0:T(8,128)(2,1)}, /*index=5*/f32[1,4]{1,0:T(1,128)}) custom-call(f32[1,2]{1,0:T(1,128)S(1)} %maximum_bitcast_fusion.keep_ref, f32[32,8,128]{2,1,0:T(8,128)S(1)} %all-to-all-done.got_ref, ...), custom_call_target="tpu_custom_call" | custom-call | tf_op jit(solution)/shard_map/finish/pallas_call | solution.py:369
  (5 shorter events, 0.0 us)
Async XLA Ops:
  0.6 5.2 %copy-start = (bf16[1,4608,576]{1,2,0:T(8,128)(2,1)S(1)}, bf16[1,4608,576]{1,2,0:T(8,128)(2,1)}, u32[]{:S(2)}) copy-start(bf16[1,4608,576]{1,2,0:T(8,128)(2,1)} %param.9) | copy-start | bytes 15925252
  0.6 5.2 %copy-start.1 = (bf16[1,576,512]{2,1,0:T(8,128)(2,1)S(1)}, bf16[1,576,512]{2,1,0:T(8,128)(2,1)}, u32[]{:S(2)}) copy-start(bf16[1,576,512]{2,1,0:T(8,128)(2,1)} %param.10) | copy-start | bytes 1769476
  2.5 7.0 %collective-permute-start.4 = (bf16[1584,128]{1,0:T(8,128)(2,1)S(1)}, bf16[1584,128]{1,0:T(8,128)(2,1)S(1)}, u32[]{:S(2)}, u32[]{:S(2)}) collective-permute-start(bf16[1584,128]{1,0:T(8,128)(2,1)S(1)} %get-tuple-element.28._), channel_id=1, source_target_pairs={{0,32},{32,0},{64,96},{96,64},{128,160},{160,128},{192,224},{224,1... | collective-permute-start | bytes 1216520 | tf_op jit(solution)/shard_map/ppermute | solution.py:133
  5.7 4.0 %collective-permute-start.7 = (bf16[1872,128]{1,0:T(8,128)(2,1)S(1)}, bf16[1872,128]{1,0:T(8,128)(2,1)S(1)}, u32[]{:S(2)}, u32[]{:S(2)}) collective-permute-start(bf16[1872,128]{1,0:T(8,128)(2,1)S(1)} %get-tuple-element.35), channel_id=1, source_target_pairs={{0,32},{32,0},{64,96},{96,64},{128,160},{160,128},{192,224},{224,1... | collective-permute-start | bytes 1437704 | tf_op jit(solution)/shard_map/ppermute | solution.py:133
  7.2 4.2 %collective-permute-start.1 = (bf16[2592,128]{1,0:T(8,128)(2,1)S(1)}, bf16[2592,128]{1,0:T(8,128)(2,1)S(1)}, u32[]{:S(2)}, u32[]{:S(2)}) collective-permute-start(bf16[2592,128]{1,0:T(8,128)(2,1)S(1)} %get-tuple-element.33), channel_id=1, source_target_pairs={{0,32},{32,0},{64,96},{96,64},{128,160},{160,128},{192,224},{224,1... | collective-permute-start | bytes 1990664 | tf_op jit(solution)/shard_map/ppermute | solution.py:133
  9.4 12.2 %collective-permute-start = (bf16[5472,128]{1,0:T(8,128)(2,1)S(1)}, bf16[5472,128]{1,0:T(8,128)(2,1)S(1)}, u32[]{:S(2)}, u32[]{:S(2)}) collective-permute-start(bf16[5472,128]{1,0:T(8,128)(2,1)S(1)} %get-tuple-element.32), channel_id=1, source_target_pairs={{0,32},{32,0},{64,96},{96,64},{128,160},{160,128},{192,224},{224,1... | collective-permute-start | bytes 4202504 | tf_op jit(solution)/shard_map/ppermute | solution.py:133
  9.6 10.5 %collective-permute-start.5 = (bf16[1584,128]{1,0:T(8,128)(2,1)S(1)}, bf16[1584,128]{1,0:T(8,128)(2,1)S(1)}, u32[]{:S(2)}, u32[]{:S(2)}) collective-permute-start(bf16[1584,128]{1,0:T(8,128)(2,1)S(1)} %add_convert_fusion.1), channel_id=1, source_target_pairs={{0,64},{32,96},{64,0},{96,32},{128,192},{160,224},{192,128},{224,1... | collective-permute-start | bytes 1216520 | tf_op jit(solution)/shard_map/ppermute | solution.py:133
  9.8 11.8 %collective-permute-start.8 = (bf16[1584,128]{1,0:T(8,128)(2,1)S(1)}, bf16[1584,128]{1,0:T(8,128)(2,1)S(1)}, u32[]{:S(2)}, u32[]{:S(2)}) collective-permute-start(bf16[1584,128]{1,0:T(8,128)(2,1)S(1)} %add_convert_fusion), channel_id=1, source_target_pairs={{0,192},{32,224},{64,128},{96,160},{128,64},{160,96},{192,0},{224,... | collective-permute-start | bytes 1216520 | tf_op jit(solution)/shard_map/ppermute | solution.py:133
  11.6 24.8 %copy-start.5 = (f32[72,512]{1,0:T(8,128)S(1)}, f32[72,512]{1,0:T(8,128)}, u32[]{:S(2)}) copy-start(f32[72,512]{1,0:T(8,128)} %moment_ref.2) | copy-start | bytes 442372
  11.6 37.4 %collective-permute-start.3 = (bf16[1296,128]{1,0:T(8,128)(2,1)S(1)}, bf16[1296,128]{1,0:T(8,128)(2,1)S(1)}, u32[]{:S(2)}, u32[]{:S(2)}) collective-permute-start(bf16[1296,128]{1,0:T(8,128)(2,1)S(1)} %get-tuple-element.50), channel_id=1, source_target_pairs={{0,192},{32,224},{64,128},{96,160},{128,64},{160,96},{192,0},{224,... | collective-permute-start | bytes 995336 | tf_op jit(solution)/shard_map/ppermute | solution.py:133
  12.9 36.1 %collective-permute-start.2 = (bf16[1296,128]{1,0:T(8,128)(2,1)S(1)}, bf16[1296,128]{1,0:T(8,128)(2,1)S(1)}, u32[]{:S(2)}, u32[]{:S(2)}) collective-permute-start(bf16[1296,128]{1,0:T(8,128)(2,1)S(1)} %get-tuple-element.51), channel_id=1, source_target_pairs={{0,64},{32,96},{64,0},{96,32},{128,192},{160,224},{192,128},{224,1... | collective-permute-start | bytes 995336 | tf_op jit(solution)/shard_map/ppermute | solution.py:133
  21.9 27.1 %collective-permute-start.9 = (bf16[1296,128]{1,0:T(8,128)(2,1)S(1)}, bf16[1296,128]{1,0:T(8,128)(2,1)S(1)}, u32[]{:S(2)}, u32[]{:S(2)}) collective-permute-start(bf16[1296,128]{1,0:T(8,128)(2,1)S(1)} %get-tuple-element.48), channel_id=1, source_target_pairs={{0,64},{32,96},{64,0},{96,32},{128,192},{160,224},{192,128},{224,1... | collective-permute-start | bytes 995336 | tf_op jit(solution)/shard_map/ppermute | solution.py:133
  22.0 27.1 %collective-permute-start.6 = (bf16[1296,128]{1,0:T(8,128)(2,1)S(1)}, bf16[1296,128]{1,0:T(8,128)(2,1)S(1)}, u32[]{:S(2)}, u32[]{:S(2)}) collective-permute-start(bf16[1296,128]{1,0:T(8,128)(2,1)S(1)} %get-tuple-element.49), channel_id=1, source_target_pairs={{0,192},{32,224},{64,128},{96,160},{128,64},{160,96},{192,0},{224,... | collective-permute-start | bytes 995336 | tf_op jit(solution)/shard_map/ppermute | solution.py:133
  23.3 25.8 %copy-start.2 = (f32[576,576]{1,0:T(8,128)S(1)}, f32[576,576]{1,0:T(8,128)}, u32[]{:S(2)}) copy-start(f32[576,576]{1,0:T(8,128)} %moment_ref.3) | copy-start | bytes 3981316
  23.3 13.1 %collective-permute-start.10 = (bf16[288,128]{1,0:T(8,128)(2,1)S(1)}, bf16[288,128]{1,0:T(8,128)(2,1)S(1)}, u32[]{:S(2)}, u32[]{:S(2)}) collective-permute-start(bf16[288,128]{1,0:T(8,128)(2,1)S(1)} %add_convert_fusion.6), channel_id=1, source_target_pairs={{0,128},{32,160},{64,192},{96,224},{128,0},{160,32},{192,64},{224,... | collective-permute-start | bytes 221192 | tf_op jit(solution)/shard_map/ppermute | solution.py:133
  36.5 2.7 %collective-permute-start.11 = (f32[8,128]{1,0:T(8,128)S(1)}, f32[8,128]{1,0:T(8,128)S(1)}, u32[]{:S(2)}, u32[]{:S(2)}) collective-permute-start(f32[8,128]{1,0:T(8,128)S(1)} %get-tuple-element.36), channel_id=1, source_target_pairs={{0,1},{1,0},{2,3},{3,2},{4,5},{5,4},{6,7},{7,6},{8,9},{9,8},{10,11... | collective-permute-start | bytes 12296 | tf_op jit(solution)/shard_map/ppermute | solution.py:133
  39.2 4.0 %collective-permute-start.12 = (f32[8,128]{1,0:T(8,128)S(1)}, f32[8,128]{1,0:T(8,128)S(1)}, u32[]{:S(2)}, u32[]{:S(2)}) collective-permute-start(f32[8,128]{1,0:T(8,128)S(1)} %add.45), channel_id=1, source_target_pairs={{0,2},{1,3},{2,0},{3,1},{4,6},{5,7},{6,4},{7,5},{8,10},{9,11},{10,... | collective-permute-start | bytes 12296 | tf_op jit(solution)/shard_map/ppermute | solution.py:133
  43.2 5.8 %collective-permute-start.13 = (f32[8,128]{1,0:T(8,128)S(1)}, f32[8,128]{1,0:T(8,128)S(1)}, u32[]{:S(2)}, u32[]{:S(2)}) collective-permute-start(f32[8,128]{1,0:T(8,128)S(1)} %add.46), channel_id=1, source_target_pairs={{0,7},{1,6},{2,5},{3,4},{4,3},{5,2},{6,1},{7,0},{8,15},{9,14},{10,... | collective-permute-start | bytes 12296 | tf_op jit(solution)/shard_map/ppermute | solution.py:133
  49.0 11.7 %copy-start.7 = (f32[576]{0:T(1024)S(1)}, f32[576]{0:T(1024)}, u32[]{:S(2)}) copy-start(f32[576]{0:T(1024)} %param.13) | copy-start | bytes 6916
  50.4 17.2 %copy-start.3 = (f32[576,576]{1,0:T(8,128)S(1)}, f32[576,576]{1,0:T(8,128)}, u32[]{:S(2)}) copy-start(f32[576,576]{1,0:T(8,128)} %param_ref.1) | copy-start | bytes 3981316
  50.4 17.2 %copy-start.4 = (f32[72,512]{1,0:T(8,128)S(1)}, f32[72,512]{1,0:T(8,128)}, u32[]{:S(2)}) copy-start(f32[72,512]{1,0:T(8,128)} %query_param_ref.1) | copy-start | bytes 442372
  50.4 17.2 %copy-start.6 = (f32[4]{0:T(128)S(1)}, f32[4]{0:T(128)}, u32[]{:S(2)}) copy-start(f32[4]{0:T(128)} %param.16) | copy-start | bytes 52
  50.4 17.2 %all-to-all-start = ((f32[32,8,128]{2,1,0:T(8,128)}), f32[32,8,128]{2,1,0:T(8,128)S(1)}, u32[]{:S(2)}, u32[]{:S(2)}) async-start(f32[32,8,128]{2,1,0:T(8,128)} %get-tuple-element.37), calls=%async_computation | async-start | bytes 262144 | tf_op jit(solution)/shard_map/all_to_all | solution.py:358

commit v5 on v4

--- a/solution.py
+++ b/solution.py
@@ -18,10 +18,11 @@
 LANES = 128
 ROW_BLOCKS = 6
 GROUPS = {
-    "forward0": (((0, 2),), ((0, 1), (1, 1))),
-    "forward1": (((1, 2),), ((0, 3), (1, 3), (0, 2), (1, 2))),
+    "query": ((), ((0, 2), (0, 1), (1, 2), (1, 3), (0, 3), (1, 1), (0, 0), (1, 0))),
+    "forward0": (((0, 2),), ()),
+    "forward1": (((1, 2),), ()),
     "keep": (((0, 1), (1, 3)), ()),
-    "rest": (((0, 3), (1, 1), (0, 0), (1, 0)), ((0, 0), (1, 0))),
+    "rest": (((0, 3), (1, 1), (0, 0), (1, 0)), ()),
 }
 ANY = pl.BlockSpec(memory_space=pl.ANY)
 HBM = pl.BlockSpec(memory_space=pltpu.HBM)
@@ -60,10 +61,11 @@
     span = columns.shape[1] // 4
 
     def kernel(down_ref, query_ref, _, *refs):
-        outs, bufs, sems = refs[: len(parts)], refs[len(parts) : 2 * len(parts)], refs[2 * len(parts) :]
+        outs, bufs, sems = (refs[i * len(parts) : (i + 1) * len(parts)] for i in range(3))
+        query_buf, query_sem = refs[3 * len(parts) :]
         me = lax.axis_index("dp")
         y, core = me // 2, me % 2
-        shared, whole = [], []
+        shared, whole, moves, chunks = [], [], [], {}
 
         def put(copies, source, target, semaphore):
             if place is far:
@@ -77,21 +79,32 @@
             for at, (half, d) in enumerate(downs):
                 lane = pl.multiple_of(span * (y ^ d) + 4 * LANES, LANES)
                 source = down_ref.at[pl.ds(half * 2 * quarter, 2 * quarter), pl.ds(lane, LANES)]
-                put(shared, source, buf.at[at], sem.at[at, 0])
+                put(shared, source, buf.at[at], sem.at[0, 0])
             for at, (half, d) in enumerate(downs):
                 for j in range(2):
                     lane = pl.multiple_of(span * (y ^ d) + 5 * LANES * owner + (2 * half + j) * LANES, LANES)
                     target = out.at[pl.ds(at * block + j * (width + quarter), width), :]
-                    put(whole, down_ref.at[:, pl.ds(lane, LANES)], target, sem.at[at, 1 + j])
+                    put(whole, down_ref.at[:, pl.ds(lane, LANES)], target, sem.at[0, 1 + j])
             for at, (half, d) in enumerate(queries):
+                chunk = query_ref.at[2 * (y ^ d) + owner]
+                if place is far:
+                    chunk = query_buf.at[0, d]
+                    chunks[d] = pltpu.make_async_copy(
+                        query_ref.at[2 * (y ^ d) + owner], chunk, query_sem.at[0, d]
+                    )
                 for j in range(q_wide):
-                    source = query_ref.at[2 * (y ^ d) + owner, :, pl.ds((half * q_wide + j) * LANES, LANES)]
+                    source = chunk.at[:, pl.ds((half * q_wide + j) * LANES, LANES)]
                     target = out.at[pl.ds(len(downs) * block + at * query + j * q_rows, q_rows), :]
-                    put(whole, source, target, sem.at[at, 3 + j])
-        for copy in shared + whole:
+                    if place is far:
+                        moves.append((source, target))
+                    else:
+                        target[...] = source[...]
+        for copy in (*chunks.values(), *shared, *whole):
             copy.start()
-        for copy in shared:
+        for copy in (*chunks.values(), *shared):
             copy.wait()
+        for source, target in moves:
+            target[...] = source[...]
         low = lax.broadcasted_iota(jnp.int32, (quarter, LANES), 1) < LANES // 2
         for (group, mine), out, buf in zip(parts, outs, bufs):
             lower = (core == 0) if mine else (core == 1)
@@ -116,8 +129,11 @@
         out_shape=tuple(pltpu.VMEM((rows(group), LANES), jnp.bfloat16) for group, _ in parts),
         in_specs=[HBM, HBM, ANY] if place is far else [VMEM, VMEM, ANY],
         out_specs=(VMEM,) * len(parts),
-        scratch_shapes=[pltpu.VMEM((len(GROUPS[group][0]), 2 * quarter, LANES), jnp.bfloat16) for group, _ in parts]
-        + [pltpu.SemaphoreType.DMA((4, 5)) for _ in parts],
+        scratch_shapes=[
+            pltpu.VMEM((max(len(GROUPS[group][0]), 1), 2 * quarter, LANES), jnp.bfloat16) for group, _ in parts
+        ]
+        + [pltpu.SemaphoreType.DMA((1, 3)) for _ in parts]
+        + [pltpu.VMEM((1, 4, q_rows, q_cols), jnp.bfloat16), pltpu.SemaphoreType.DMA((1, 4))],
         compiler_params=PARAMS,
     )(place(columns), place(query_chunks), after)
 
@@ -145,19 +161,21 @@
     return jnp.sum(x * x, axis=0, keepdims=True)
 
 
-def gather_query(query, own, other, direct, query_moment):
+def gather_query(query, own, other, asks, asked, query_moment):
     q_rows, q_cols = query_moment.shape
     q_wide = q_cols // LANES // 2
 
-    def kernel(own_ref, other_ref, from_first, from_second, from_third, moment_ref, new_ref, sums_ref):
+    def kernel(own_ref, other_ref, ask0, ask1, asked0, asked1, moment_ref, new_ref, sums_ref):
         sums_ref[...] = jnp.zeros_like(sums_ref)
         for half in range(2):
             for j in range(q_wide):
-                terms = []
-                for ref in (own_ref, other_ref, from_first, from_second, from_third):
-                    at = ref.shape[0] - (2 - half) * query + j * q_rows
-                    terms.append(ref[pl.ds(at, q_rows), :])
-                grad = added(*terms) * (1.0 / 8.0)
+                kept, at = (6 + half) * query + j * q_rows, j * q_rows
+                grad = added(
+                    own_ref[pl.ds(kept, q_rows), :],
+                    other_ref[pl.ds(kept, q_rows), :],
+                    (ask0, ask1)[half][pl.ds(query + at, q_rows), :],
+                    (asked0, asked1)[half][pl.ds(at, q_rows), :],
+                ) * (1.0 / 8.0)
                 head = half * q_wide + j
                 span = (slice(None), slice(head * LANES, (head + 1) * LANES))
                 new_ref[span] = moment_new(moment_ref[span], grad)
@@ -166,11 +184,11 @@
     return pl.pallas_call(
         kernel,
         out_shape=(pltpu.VMEM(query_moment.shape, jnp.float32), pltpu.VMEM((8, LANES), jnp.float32)),
-        in_specs=[VMEM] * 6,
+        in_specs=[VMEM] * 7,
         out_specs=(VMEM,) * 2,
         compiler_params=PARAMS,
         name="query",
-    )(*(near(t) for t in (own, other, *direct, query_moment)))
+    )(*(near(t) for t in (own, other, *asks, *asked, query_moment)))
 
 
 def gather(own, other, keeps, seconds, heads, down_moment):
@@ -329,14 +347,22 @@
         return sent(x, 1)
 
     to_first, to_second = (2, 6), (6, 2)
-    sends = packed(query_chunks, far, ("forward0", False), ("forward1", False))
+    send_query, *sends = packed(query_chunks, far, ("query", False), ("forward0", False), ("forward1", False))
+    other_query = other_core(send_query)
     others = [other_core(sends[half]) for half in range(2)]
-    owns = packed(sends[0], near, ("forward0", True), ("forward1", True))
-    ends = [block + 2 * query] * 2
-    forwards = [summed(owns[half][: ends[half]], others[half][: ends[half]]) for half in range(2)]
-    across = summed(owns[1][ends[1] :], others[1][ends[1] :])
+    own_query, *owns = packed(send_query, near, ("query", True), ("forward0", True), ("forward1", True))
+    asks = []
+    for half in range(2):
+        part = slice(2 * half * query, 2 * (half + 1) * query)
+        asks.append(summed(own_query[part], other_query[part]))
+    asks = [sent(asks[half], to_first[half]) for half in range(2)]
+    forwards = [summed(owns[half], others[half]) for half in range(2)]
     forwards = [sent(forwards[half], to_first[half]) for half in range(2)]
-    across = sent(across, 4)
+    asked = []
+    for half in range(2):
+        part = slice((4 + half) * query, (5 + half) * query)
+        asked.append(summed(own_query[part], other_query[part], asks[half][:query]))
+    asked = [sent(asked[half], to_second[half]) for half in range(2)]
     keep_send, keep_own = packed(owns[0], near, ("keep", False), ("keep", True))
     keep_other = other_core(keep_send)
     send, own = packed(keep_own, near, ("rest", False), ("rest", True))
@@ -349,9 +375,9 @@
     seconds = []
     for half in range(2):
         part = slice(half * block, (half + 1) * block)
-        seconds.append(summed(own[part], other[part], forwards[half][:block]))
+        seconds.append(summed(own[part], other[part], forwards[half]))
     seconds = [sent(seconds[half], to_second[half]) for half in range(2)]
-    query_new, heads = gather_query(query, own, other, (*forwards, across), query_moment)
+    query_new, heads = gather_query(query, own_query, other_query, asks, asked, query_moment)
     for mask in (1, 2, 7):
         heads = heads + sent(heads, mask, "ctx")
     new, message = gather(own, other, keeps, seconds, heads, down_moment)

time: 69.6 us -> 77.1 us (1.11)
  starting transfers between devices: 30.3 us -> 34.6 us
  waiting for transfers between devices: 28.2 us -> 32.3 us
  Pallas kernels: 8.59 us -> 7.67 us
    ppermute x14 -> x18, waiting for transfers between devices: 22.6 us -> 26.7 us  [sent(): return lax.ppermute(x, axis, pairs(8, mask))]
    all_to_all x1, starting transfers between devices: 9.54 us -> 13.4 us  [shards(): lax.all_to_all(message, ('dp', 'tensor'), split_axis=0, concat_axis=0, ti...]
    pallas_call x4, Pallas kernels: 4.16 us -> 3.24 us  [pack(): pl.pallas_call(kernel, out_shape=tuple((pltpu.VMEM((rows(group), LANES),...]
    ppermute x14 -> x18, starting transfers between devices: 20.7 us -> 21.2 us  [sent(): return lax.ppermute(x, axis, pairs(8, mask))]
  transfers between devices with their start and end apart: 15 -> 19, of which waited for: 7 -> 7; matrix products, arithmetic and copies ran while one was open for 1% -> 1% of each run, Pallas kernels for 5% -> 4%
where the time goes in v5:
time: 77.1 us; the launch traced here: 76.9 us
  starting transfers between devices  34.6 us (45%)
  waiting for transfers between devices  32.3 us (42%)
  Pallas kernels  7.67 us (10%)
  between operations  1.57 us (2%)
  other arithmetic  0.78 us (1%)
    ppermute x18, waiting for transfers between devices, sent(): return lax.ppermute(x, axis, pairs(8, mask))  26.7 us
    ppermute x18, starting transfers between devices, sent(): return lax.ppermute(x, axis, pairs(8, mask))  21.2 us
    all_to_all x1, starting transfers between devices, shards(): lax.all_to_all(message, ('dp', 'tensor'), split_axis=0, concat_axis=0, ti...  13.4 us
    all_to_all x1, waiting for transfers between devices, shards(): lax.all_to_all(message, ('dp', 'tensor'), split_axis=0, concat_axis=0, ti...  5.6 us
    pallas_call x4, Pallas kernels, pack(): pl.pallas_call(kernel, out_shape=tuple((pltpu.VMEM((rows(group), LANES),...  3.24 us
    pallas_call x1, Pallas kernels, shards(): pl.pallas_call(finish_kernel, out_shape=(pltpu.HBM(down_param.shape, f32)...  1.8 us
  transfers between devices with their start and end apart: 19, of which 7 were waited for; matrix products, arithmetic and copies ran while one was open for 1% of the time, Pallas kernels for 4%

profile of v5, /device:TPU:1, one launch (start us, length us, event | category | flops | bytes accessed | tf_op | source)
XLA Modules:
  0.0 76.9 jit_solution(15939685004172971287)
XLA Ops:
  0.6 0.0 copy-start
  0.6 0.0 copy-start.1
  0.7 1.7 %shard_map.152 = (bf16[1152,128]{1,0:T(8,128)(2,1)S(1)}, bf16[1296,128]{1,0:T(8,128)(2,1)S(1)}, bf16[1296,128]{1,0:T(8,128)(2,1)S(1)}) custom-call(bf16[576,4608]{1,0:T(8,128)(2,1)} %bitcast.8, bf16[8,72,512]{2,1,0:T(8,128)(2,1)} %bitcast.12, bf16[8,72,512]{2,1,0:T(8,128)(2,1)} %bitcast.13), custom_call_target="tpu_custom_call" | custom-call | tf_op jit(solution)/shard_map/pallas_call | solution.py:127
  2.3 3.3 %collective-permute-start.10 = (bf16[1152,128]{1,0:T(8,128)(2,1)S(1)}, bf16[1152,128]{1,0:T(8,128)(2,1)S(1)}, u32[]{:S(2)}, u32[]{:S(2)}) collective-permute-start(bf16[1152,128]{1,0:T(8,128)(2,1)S(1)} %get-tuple-element.30._), channel_id=1, source_target_pairs={{0,32},{32,0},{64,96},{96,64},{128,160},{160,128},{192,224},{224,1... | collective-permute-start | bytes 884744 | tf_op jit(solution)/shard_map/ppermute | solution.py:149
  5.6 0.1 collective-permute-start.4
  5.7 0.4 collective-permute-start.7
  6.1 0.0 copy-done
  6.1 0.0 copy-done.1
  6.1 0.3 shard_map.153
  6.5 0.5 shard_map.154
  7.0 0.9 %collective-permute-start.1 = (bf16[2592,128]{1,0:T(8,128)(2,1)S(1)}, bf16[2592,128]{1,0:T(8,128)(2,1)S(1)}, u32[]{:S(2)}, u32[]{:S(2)}) collective-permute-start(bf16[2592,128]{1,0:T(8,128)(2,1)S(1)} %get-tuple-element.35), channel_id=1, source_target_pairs={{0,32},{32,0},{64,96},{96,64},{128,160},{160,128},{192,224},{224,1... | collective-permute-start | bytes 1990664 | tf_op jit(solution)/shard_map/ppermute | solution.py:149
  7.8 0.8 %shard_map.155 = (bf16[5184,128]{1,0:T(8,128)(2,1)S(1)}, bf16[5184,128]{1,0:T(8,128)(2,1)S(1)}) custom-call(bf16[576,4608]{1,0:T(8,128)(2,1)S(1)} %bitcast.11, bf16[8,72,512]{2,1,0:T(8,128)(2,1)S(1)} %bitcast.16, bf16[2592,128]{1,0:T(8,128)(2,1)S(1)} %get-tuple-element.32._), custom_call_target="tpu_custom_call" | custom-call | tf_op jit(solution)/shard_map/pallas_call | solution.py:127
  8.6 0.1 collective-permute-start
  8.7 0.0 collective-permute-done.10.other_ref
  8.8 1.1 %collective-permute-start.12 = (bf16[288,128]{1,0:T(8,128)(2,1)S(1)}, bf16[288,128]{1,0:T(8,128)(2,1)S(1)}, u32[]{:S(2)}, u32[]{:S(2)}) collective-permute-start(bf16[288,128]{1,0:T(8,128)(2,1)S(1)} %get-tuple-element.58), channel_id=1, source_target_pairs={{0,192},{32,224},{64,128},{96,160},{128,64},{160,96},{192,0},{224,... | collective-permute-start | bytes 221192 | tf_op jit(solution)/shard_map/ppermute | solution.py:149
  9.9 0.0 collective-permute-done.4
  9.9 0.0 collective-permute-start.11
  9.9 0.1 add_convert_fusion.3
  10.0 0.0 collective-permute-done.7
  10.0 1.5 %collective-permute-start.5 = (bf16[1296,128]{1,0:T(8,128)(2,1)S(1)}, bf16[1296,128]{1,0:T(8,128)(2,1)S(1)}, u32[]{:S(2)}, u32[]{:S(2)}) collective-permute-start(bf16[1296,128]{1,0:T(8,128)(2,1)S(1)} %add_convert_fusion.3), channel_id=1, source_target_pairs={{0,64},{32,96},{64,0},{96,32},{128,192},{160,224},{192,128},{224,1... | collective-permute-start | bytes 995336 | tf_op jit(solution)/shard_map/ppermute | solution.py:149
  11.6 0.1 add_convert_fusion.1
  11.6 0.0 collective-permute-done.1
  11.7 1.7 %collective-permute-start.8 = (bf16[1296,128]{1,0:T(8,128)(2,1)S(1)}, bf16[1296,128]{1,0:T(8,128)(2,1)S(1)}, u32[]{:S(2)}, u32[]{:S(2)}) collective-permute-start(bf16[1296,128]{1,0:T(8,128)(2,1)S(1)} %add_convert_fusion.1), channel_id=1, source_target_pairs={{0,192},{32,224},{64,128},{96,160},{128,64},{160,96},{192,0},{224,... | collective-permute-start | bytes 995336 | tf_op jit(solution)/shard_map/ppermute | solution.py:149
  13.4 0.2 add_convert_fusion.4
  13.6 6.5 %collective-permute-done.5 = bf16[1296,128]{1,0:T(8,128)(2,1)S(1)} collective-permute-done((bf16[1296,128]{1,0:T(8,128)(2,1)S(1)}, bf16[1296,128]{1,0:T(8,128)(2,1)S(1)}, u32[]{:S(2)}, u32[]{:S(2)}) %collective-permute-start.5) | collective-permute-done | bytes 331808 | tf_op jit(solution)/shard_map/ppermute | solution.py:149
  20.1 1.6 %collective-permute-start.3 = (bf16[1296,128]{1,0:T(8,128)(2,1)S(1)}, bf16[1296,128]{1,0:T(8,128)(2,1)S(1)}, u32[]{:S(2)}, u32[]{:S(2)}) collective-permute-start(bf16[1296,128]{1,0:T(8,128)(2,1)S(1)} %get-tuple-element.54), channel_id=1, source_target_pairs={{0,192},{32,224},{64,128},{96,160},{128,64},{160,96},{192,0},{224,... | collective-permute-start | bytes 995336 | tf_op jit(solution)/shard_map/ppermute | solution.py:149
  21.7 0.0 collective-permute-done.8
  21.7 0.0 collective-permute-start.2
  21.7 0.0 collective-permute-done.other_ref
  21.7 0.0 copy-start.5
  21.8 0.0 copy-start.2
  21.8 0.3 add_convert_fusion
  22.0 1.5 %collective-permute-start.9 = (bf16[1296,128]{1,0:T(8,128)(2,1)S(1)}, bf16[1296,128]{1,0:T(8,128)(2,1)S(1)}, u32[]{:S(2)}, u32[]{:S(2)}) collective-permute-start(bf16[1296,128]{1,0:T(8,128)(2,1)S(1)} %get-tuple-element.52), channel_id=1, source_target_pairs={{0,64},{32,96},{64,0},{96,32},{128,192},{160,224},{192,128},{224,1... | collective-permute-start | bytes 995336 | tf_op jit(solution)/shard_map/ppermute | solution.py:149
  23.6 0.0 collective-permute-done.12.ask1
  23.6 1.0 %collective-permute-start.6 = (bf16[1296,128]{1,0:T(8,128)(2,1)S(1)}, bf16[1296,128]{1,0:T(8,128)(2,1)S(1)}, u32[]{:S(2)}, u32[]{:S(2)}) collective-permute-start(bf16[1296,128]{1,0:T(8,128)(2,1)S(1)} %get-tuple-element.53), channel_id=1, source_target_pairs={{0,192},{32,224},{64,128},{96,160},{128,64},{160,96},{192,0},{224,... | collective-permute-start | bytes 995336 | tf_op jit(solution)/shard_map/ppermute | solution.py:149
  24.6 0.0 collective-permute-done.11.ask0
  24.6 0.1 collective-permute-start.14
  24.7 12.4 %collective-permute-done.14.asked1 = bf16[144,128]{1,0:T(8,128)(2,1)S(1)} collective-permute-done((bf16[144,128]{1,0:T(8,128)(2,1)S(1)}, bf16[144,128]{1,0:T(8,128)(2,1)S(1)}, u32[]{:S(2)}, u32[]{:S(2)}) %collective-permute-start.14) | collective-permute-done | bytes 36896 | tf_op jit(solution)/shard_map/ppermute | solution.py:149
  37.1 0.9 %collective-permute-start.13 = (bf16[144,128]{1,0:T(8,128)(2,1)S(1)}, bf16[144,128]{1,0:T(8,128)(2,1)S(1)}, u32[]{:S(2)}, u32[]{:S(2)}) collective-permute-start(bf16[144,128]{1,0:T(8,128)(2,1)S(1)} %get-tuple-element.57), channel_id=1, source_target_pairs={{0,192},{32,224},{64,128},{96,160},{128,64},{160,96},{192,0},{224,... | collective-permute-start | bytes 110600 | tf_op jit(solution)/shard_map/ppermute | solution.py:149
  38.0 3.2 %collective-permute-done.13.asked0 = bf16[144,128]{1,0:T(8,128)(2,1)S(1)} collective-permute-done((bf16[144,128]{1,0:T(8,128)(2,1)S(1)}, bf16[144,128]{1,0:T(8,128)(2,1)S(1)}, u32[]{:S(2)}, u32[]{:S(2)}) %collective-permute-start.13) | collective-permute-done | bytes 36896 | tf_op jit(solution)/shard_map/ppermute | solution.py:149
  41.1 0.0 copy-done.5
  41.1 0.1 query.1
  41.2 0.7 collective-permute-start.15
  41.9 2.1 %collective-permute-done.15 = f32[8,128]{1,0:T(8,128)S(1)} collective-permute-done((f32[8,128]{1,0:T(8,128)S(1)}, f32[8,128]{1,0:T(8,128)S(1)}, u32[]{:S(2)}, u32[]{:S(2)}) %collective-permute-start.15) | collective-permute-done | bytes 4128 | tf_op jit(solution)/shard_map/ppermute | solution.py:149
  44.0 1.9 %collective-permute-start.16 = (f32[8,128]{1,0:T(8,128)S(1)}, f32[8,128]{1,0:T(8,128)S(1)}, u32[]{:S(2)}, u32[]{:S(2)}) collective-permute-start(f32[8,128]{1,0:T(8,128)S(1)} %add.65), channel_id=1, source_target_pairs={{0,2},{1,3},{2,0},{3,1},{4,6},{5,7},{6,4},{7,5},{8,10},{9,11},{10,... | collective-permute-start | bytes 12296 | tf_op jit(solution)/shard_map/ppermute | solution.py:149
  45.9 1.5 %collective-permute-done.16 = f32[8,128]{1,0:T(8,128)S(1)} collective-permute-done((f32[8,128]{1,0:T(8,128)S(1)}, f32[8,128]{1,0:T(8,128)S(1)}, u32[]{:S(2)}, u32[]{:S(2)}) %collective-permute-start.16) | collective-permute-done | bytes 4128 | tf_op jit(solution)/shard_map/ppermute | solution.py:149
  47.4 4.3 %collective-permute-start.17 = (f32[8,128]{1,0:T(8,128)S(1)}, f32[8,128]{1,0:T(8,128)S(1)}, u32[]{:S(2)}, u32[]{:S(2)}) collective-permute-start(f32[8,128]{1,0:T(8,128)S(1)} %add.66), channel_id=1, source_target_pairs={{0,7},{1,6},{2,5},{3,4},{4,3},{5,2},{6,1},{7,0},{8,15},{9,14},{10,... | collective-permute-start | bytes 12296 | tf_op jit(solution)/shard_map/ppermute | solution.py:149
  51.7 1.0 %collective-permute-done.17 = f32[8,128]{1,0:T(8,128)S(1)} collective-permute-done((f32[8,128]{1,0:T(8,128)S(1)}, f32[8,128]{1,0:T(8,128)S(1)}, u32[]{:S(2)}, u32[]{:S(2)}) %collective-permute-start.17) | collective-permute-done | bytes 4128 | tf_op jit(solution)/shard_map/ppermute | solution.py:149
  52.7 0.0 copy-start.7
  52.7 0.0 collective-permute-done.3.keep1
  52.7 0.0 collective-permute-done.2.keep0
  52.7 0.0 collective-permute-done.9.second1
  52.7 0.0 collective-permute-done.6.second0
  52.7 0.0 copy-done.2
  52.7 1.4 %gather.1 = (f32[576,576]{1,0:T(8,128)S(1)}, f32[32,8,128]{2,1,0:T(8,128)}) custom-call(bf16[5184,128]{1,0:T(8,128)(2,1)S(1)} %get-tuple-element.33.own_ref, bf16[5184,128]{1,0:T(8,128)(2,1)S(1)} %collective-permute-done.other_ref, bf16[1296,128]{1,0:T(8,128)(2,1)S(1)} %collective-permute-done.2.keep0, bf16[1296,128]{1,0:T(8,128)(2,1)S(1)} %collective-permute-done.3.keep1, ...), custom_call_target="tpu_custom_call" | custom-call | tf_op jit(solution)/shard_map/gather/pallas_call | solution.py:244
  54.1 13.4 %all-to-all-start = ((f32[32,8,128]{2,1,0:T(8,128)}), f32[32,8,128]{2,1,0:T(8,128)S(1)}, u32[]{:S(2)}, u32[]{:S(2)}) async-start(f32[32,8,128]{2,1,0:T(8,128)} %get-tuple-element.41), calls=%async_computation | async-start | bytes 262144 | tf_op jit(solution)/shard_map/all_to_all | solution.py:384
  68.3 0.0 copy-done.7
  68.3 0.1 maximum_bitcast_fusion.keep_ref
  68.4 1.2 %store.1 = (f32[576,576]{1,0:T(8,128)}, f32[72,512]{1,0:T(8,128)}) custom-call(f32[576,576]{1,0:T(8,128)S(1)} %get-tuple-element.42.new_ref, f32[72,512]{1,0:T(8,128)S(1)} %get-tuple-element.43.query_new_ref), custom_call_target="tpu_custom_call" | custom-call | tf_op jit(solution)/shard_map/store/pallas_call | solution.py:385
  69.5 5.6 %all-to-all-done.got_ref = f32[32,8,128]{2,1,0:T(8,128)S(1)} async-done(((f32[32,8,128]{2,1,0:T(8,128)}), f32[32,8,128]{2,1,0:T(8,128)S(1)}, u32[]{:S(2)}, u32[]{:S(2)}) %all-to-all-start) | async-done | bytes 131104 | tf_op jit(solution)/shard_map/all_to_all | solution.py:384
  75.1 0.0 copy-done.3
  75.1 0.0 copy-done.4
  75.1 0.0 copy-done.6
  75.1 1.8 %finish.1 = (f32[576,576]{1,0:T(8,128)}, bf16[576,576]{1,0:T(8,128)(2,1)}, f32[576]{0:T(1024)}, f32[72,512]{1,0:T(8,128)}, bf16[72,512]{1,0:T(8,128)(2,1)}, /*index=5*/f32[1,4]{1,0:T(1,128)}) custom-call(f32[1,2]{1,0:T(1,128)S(1)} %maximum_bitcast_fusion.keep_ref, f32[32,8,128]{2,1,0:T(8,128)S(1)} %all-to-all-done.got_ref, ...), custom_call_target="tpu_custom_call" | custom-call | tf_op jit(solution)/shard_map/finish/pallas_call | solution.py:395
  (9 shorter events, 0.1 us)
Async XLA Ops:
  0.6 5.5 %copy-start = (bf16[1,4608,576]{1,2,0:T(8,128)(2,1)S(1)}, bf16[1,4608,576]{1,2,0:T(8,128)(2,1)}, u32[]{:S(2)}) copy-start(bf16[1,4608,576]{1,2,0:T(8,128)(2,1)} %param.9) | copy-start | bytes 15925252
  0.6 5.5 %copy-start.1 = (bf16[1,576,512]{2,1,0:T(8,128)(2,1)S(1)}, bf16[1,576,512]{2,1,0:T(8,128)(2,1)}, u32[]{:S(2)}) copy-start(bf16[1,576,512]{2,1,0:T(8,128)(2,1)} %param.10) | copy-start | bytes 1769476
  2.3 6.4 %collective-permute-start.10 = (bf16[1152,128]{1,0:T(8,128)(2,1)S(1)}, bf16[1152,128]{1,0:T(8,128)(2,1)S(1)}, u32[]{:S(2)}, u32[]{:S(2)}) collective-permute-start(bf16[1152,128]{1,0:T(8,128)(2,1)S(1)} %get-tuple-element.30._), channel_id=1, source_target_pairs={{0,32},{32,0},{64,96},{96,64},{128,160},{160,128},{192,224},{224,1... | collective-permute-start | bytes 884744 | tf_op jit(solution)/shard_map/ppermute | solution.py:149
  5.6 4.3 %collective-permute-start.4 = (bf16[1296,128]{1,0:T(8,128)(2,1)S(1)}, bf16[1296,128]{1,0:T(8,128)(2,1)S(1)}, u32[]{:S(2)}, u32[]{:S(2)}) collective-permute-start(bf16[1296,128]{1,0:T(8,128)(2,1)S(1)} %get-tuple-element.36), channel_id=1, source_target_pairs={{0,32},{32,0},{64,96},{96,64},{128,160},{160,128},{192,224},{224,1... | collective-permute-start | bytes 995336 | tf_op jit(solution)/shard_map/ppermute | solution.py:149
  5.7 4.3 %collective-permute-start.7 = (bf16[1296,128]{1,0:T(8,128)(2,1)S(1)}, bf16[1296,128]{1,0:T(8,128)(2,1)S(1)}, u32[]{:S(2)}, u32[]{:S(2)}) collective-permute-start(bf16[1296,128]{1,0:T(8,128)(2,1)S(1)} %get-tuple-element.38), channel_id=1, source_target_pairs={{0,32},{32,0},{64,96},{96,64},{128,160},{160,128},{192,224},{224,1... | collective-permute-start | bytes 995336 | tf_op jit(solution)/shard_map/ppermute | solution.py:149
  7.0 4.7 %collective-permute-start.1 = (bf16[2592,128]{1,0:T(8,128)(2,1)S(1)}, bf16[2592,128]{1,0:T(8,128)(2,1)S(1)}, u32[]{:S(2)}, u32[]{:S(2)}) collective-permute-start(bf16[2592,128]{1,0:T(8,128)(2,1)S(1)} %get-tuple-element.35), channel_id=1, source_target_pairs={{0,32},{32,0},{64,96},{96,64},{128,160},{160,128},{192,224},{224,1... | collective-permute-start | bytes 1990664 | tf_op jit(solution)/shard_map/ppermute | solution.py:149
  8.6 13.1 %collective-permute-start = (bf16[5184,128]{1,0:T(8,128)(2,1)S(1)}, bf16[5184,128]{1,0:T(8,128)(2,1)S(1)}, u32[]{:S(2)}, u32[]{:S(2)}) collective-permute-start(bf16[5184,128]{1,0:T(8,128)(2,1)S(1)} %get-tuple-element.34), channel_id=1, source_target_pairs={{0,32},{32,0},{64,96},{96,64},{128,160},{160,128},{192,224},{224,1... | collective-permute-start | bytes 3981320 | tf_op jit(solution)/shard_map/ppermute | solution.py:149
  8.8 14.8 %collective-permute-start.12 = (bf16[288,128]{1,0:T(8,128)(2,1)S(1)}, bf16[288,128]{1,0:T(8,128)(2,1)S(1)}, u32[]{:S(2)}, u32[]{:S(2)}) collective-permute-start(bf16[288,128]{1,0:T(8,128)(2,1)S(1)} %get-tuple-element.58), channel_id=1, source_target_pairs={{0,192},{32,224},{64,128},{96,160},{128,64},{160,96},{192,0},{224,... | collective-permute-start | bytes 221192 | tf_op jit(solution)/shard_map/ppermute | solution.py:149
  9.9 14.7 %collective-permute-start.11 = (bf16[288,128]{1,0:T(8,128)(2,1)S(1)}, bf16[288,128]{1,0:T(8,128)(2,1)S(1)}, u32[]{:S(2)}, u32[]{:S(2)}) collective-permute-start(bf16[288,128]{1,0:T(8,128)(2,1)S(1)} %get-tuple-element.59), channel_id=1, source_target_pairs={{0,64},{32,96},{64,0},{96,32},{128,192},{160,224},{192,128},{224,1... | collective-permute-start | bytes 221192 | tf_op jit(solution)/shard_map/ppermute | solution.py:149
  10.0 10.1 %collective-permute-start.5 = (bf16[1296,128]{1,0:T(8,128)(2,1)S(1)}, bf16[1296,128]{1,0:T(8,128)(2,1)S(1)}, u32[]{:S(2)}, u32[]{:S(2)}) collective-permute-start(bf16[1296,128]{1,0:T(8,128)(2,1)S(1)} %add_convert_fusion.3), channel_id=1, source_target_pairs={{0,64},{32,96},{64,0},{96,32},{128,192},{160,224},{192,128},{224,1... | collective-permute-start | bytes 995336 | tf_op jit(solution)/shard_map/ppermute | solution.py:149
  11.7 10.1 %collective-permute-start.8 = (bf16[1296,128]{1,0:T(8,128)(2,1)S(1)}, bf16[1296,128]{1,0:T(8,128)(2,1)S(1)}, u32[]{:S(2)}, u32[]{:S(2)}) collective-permute-start(bf16[1296,128]{1,0:T(8,128)(2,1)S(1)} %add_convert_fusion.1), channel_id=1, source_target_pairs={{0,192},{32,224},{64,128},{96,160},{128,64},{160,96},{192,0},{224,... | collective-permute-start | bytes 995336 | tf_op jit(solution)/shard_map/ppermute | solution.py:149
  20.1 32.6 %collective-permute-start.3 = (bf16[1296,128]{1,0:T(8,128)(2,1)S(1)}, bf16[1296,128]{1,0:T(8,128)(2,1)S(1)}, u32[]{:S(2)}, u32[]{:S(2)}) collective-permute-start(bf16[1296,128]{1,0:T(8,128)(2,1)S(1)} %get-tuple-element.54), channel_id=1, source_target_pairs={{0,192},{32,224},{64,128},{96,160},{128,64},{160,96},{192,0},{224,... | collective-permute-start | bytes 995336 | tf_op jit(solution)/shard_map/ppermute | solution.py:149
  21.7 30.9 %collective-permute-start.2 = (bf16[1296,128]{1,0:T(8,128)(2,1)S(1)}, bf16[1296,128]{1,0:T(8,128)(2,1)S(1)}, u32[]{:S(2)}, u32[]{:S(2)}) collective-permute-start(bf16[1296,128]{1,0:T(8,128)(2,1)S(1)} %get-tuple-element.55), channel_id=1, source_target_pairs={{0,64},{32,96},{64,0},{96,32},{128,192},{160,224},{192,128},{224,1... | collective-permute-start | bytes 995336 | tf_op jit(solution)/shard_map/ppermute | solution.py:149
  21.7 19.4 %copy-start.5 = (f32[72,512]{1,0:T(8,128)S(1)}, f32[72,512]{1,0:T(8,128)}, u32[]{:S(2)}) copy-start(f32[72,512]{1,0:T(8,128)} %moment_ref.2) | copy-start | bytes 442372
  21.8 31.0 %copy-start.2 = (f32[576,576]{1,0:T(8,128)S(1)}, f32[576,576]{1,0:T(8,128)}, u32[]{:S(2)}) copy-start(f32[576,576]{1,0:T(8,128)} %moment_ref.3) | copy-start | bytes 3981316
  22.0 30.7 %collective-permute-start.9 = (bf16[1296,128]{1,0:T(8,128)(2,1)S(1)}, bf16[1296,128]{1,0:T(8,128)(2,1)S(1)}, u32[]{:S(2)}, u32[]{:S(2)}) collective-permute-start(bf16[1296,128]{1,0:T(8,128)(2,1)S(1)} %get-tuple-element.52), channel_id=1, source_target_pairs={{0,64},{32,96},{64,0},{96,32},{128,192},{160,224},{192,128},{224,1... | collective-permute-start | bytes 995336 | tf_op jit(solution)/shard_map/ppermute | solution.py:149
  23.6 29.1 %collective-permute-start.6 = (bf16[1296,128]{1,0:T(8,128)(2,1)S(1)}, bf16[1296,128]{1,0:T(8,128)(2,1)S(1)}, u32[]{:S(2)}, u32[]{:S(2)}) collective-permute-start(bf16[1296,128]{1,0:T(8,128)(2,1)S(1)} %get-tuple-element.53), channel_id=1, source_target_pairs={{0,192},{32,224},{64,128},{96,160},{128,64},{160,96},{192,0},{224,... | collective-permute-start | bytes 995336 | tf_op jit(solution)/shard_map/ppermute | solution.py:149
  24.6 12.5 %collective-permute-start.14 = (bf16[144,128]{1,0:T(8,128)(2,1)S(1)}, bf16[144,128]{1,0:T(8,128)(2,1)S(1)}, u32[]{:S(2)}, u32[]{:S(2)}) collective-permute-start(bf16[144,128]{1,0:T(8,128)(2,1)S(1)} %get-tuple-element.56), channel_id=1, source_target_pairs={{0,64},{32,96},{64,0},{96,32},{128,192},{160,224},{192,128},{224,1... | collective-permute-start | bytes 110600 | tf_op jit(solution)/shard_map/ppermute | solution.py:149
  37.1 4.0 %collective-permute-start.13 = (bf16[144,128]{1,0:T(8,128)(2,1)S(1)}, bf16[144,128]{1,0:T(8,128)(2,1)S(1)}, u32[]{:S(2)}, u32[]{:S(2)}) collective-permute-start(bf16[144,128]{1,0:T(8,128)(2,1)S(1)} %get-tuple-element.57), channel_id=1, source_target_pairs={{0,192},{32,224},{64,128},{96,160},{128,64},{160,96},{192,0},{224,... | collective-permute-start | bytes 110600 | tf_op jit(solution)/shard_map/ppermute | solution.py:149
  41.2 2.8 %collective-permute-start.15 = (f32[8,128]{1,0:T(8,128)S(1)}, f32[8,128]{1,0:T(8,128)S(1)}, u32[]{:S(2)}, u32[]{:S(2)}) collective-permute-start(f32[8,128]{1,0:T(8,128)S(1)} %get-tuple-element.40), channel_id=1, source_target_pairs={{0,1},{1,0},{2,3},{3,2},{4,5},{5,4},{6,7},{7,6},{8,9},{9,8},{10,11... | collective-permute-start | bytes 12296 | tf_op jit(solution)/shard_map/ppermute | solution.py:149
  44.0 3.4 %collective-permute-start.16 = (f32[8,128]{1,0:T(8,128)S(1)}, f32[8,128]{1,0:T(8,128)S(1)}, u32[]{:S(2)}, u32[]{:S(2)}) collective-permute-start(f32[8,128]{1,0:T(8,128)S(1)} %add.65), channel_id=1, source_target_pairs={{0,2},{1,3},{2,0},{3,1},{4,6},{5,7},{6,4},{7,5},{8,10},{9,11},{10,... | collective-permute-start | bytes 12296 | tf_op jit(solution)/shard_map/ppermute | solution.py:149
  47.4 5.3 %collective-permute-start.17 = (f32[8,128]{1,0:T(8,128)S(1)}, f32[8,128]{1,0:T(8,128)S(1)}, u32[]{:S(2)}, u32[]{:S(2)}) collective-permute-start(f32[8,128]{1,0:T(8,128)S(1)} %add.66), channel_id=1, source_target_pairs={{0,7},{1,6},{2,5},{3,4},{4,3},{5,2},{6,1},{7,0},{8,15},{9,14},{10,... | collective-permute-start | bytes 12296 | tf_op jit(solution)/shard_map/ppermute | solution.py:149
  52.7 15.6 %copy-start.7 = (f32[576]{0:T(1024)S(1)}, f32[576]{0:T(1024)}, u32[]{:S(2)}) copy-start(f32[576]{0:T(1024)} %param.13) | copy-start | bytes 6916
  54.1 21.0 %copy-start.3 = (f32[576,576]{1,0:T(8,128)S(1)}, f32[576,576]{1,0:T(8,128)}, u32[]{:S(2)}) copy-start(f32[576,576]{1,0:T(8,128)} %param_ref.1) | copy-start | bytes 3981316
  54.1 21.0 %copy-start.4 = (f32[72,512]{1,0:T(8,128)S(1)}, f32[72,512]{1,0:T(8,128)}, u32[]{:S(2)}) copy-start(f32[72,512]{1,0:T(8,128)} %query_param_ref.1) | copy-start | bytes 442372
  54.1 21.0 %copy-start.6 = (f32[4]{0:T(128)S(1)}, f32[4]{0:T(128)}, u32[]{:S(2)}) copy-start(f32[4]{0:T(128)} %param.16) | copy-start | bytes 52
  54.1 21.0 %all-to-all-start = ((f32[32,8,128]{2,1,0:T(8,128)}), f32[32,8,128]{2,1,0:T(8,128)S(1)}, u32[]{:S(2)}, u32[]{:S(2)}) async-start(f32[32,8,128]{2,1,0:T(8,128)} %get-tuple-element.41), calls=%async_computation | async-start | bytes 262144 | tf_op jit(solution)/shard_map/all_to_all | solution.py:384
